TPU v7x, 32 devices: a whole 2x2x4 slice. The times are simulated.
32 devices in a mesh: dp: 16 (over z, y, x), mp: 2 (over core).
Axes of the slice: x: 2, y: 2, z: 4, core: 2. Of those that a mesh axis runs over, the one named last changes fastest.
Arguments:
- inputs: bfloat16 [16, 2, 256, 2048], P('dp'), may hold values from -6 to 6
- grad_out: bfloat16 [16, 2, 256, 256], P('dp', None, None, 'mp'), parts along dimension 3, may hold values from -0.5 to 0.5
- momentum: float32 [16, 2048, 256], P('dp', None, 'mp'), parts along dimension 2, may hold values from -6 to 6
- select: int32 [16, 2, 16, 16], P(None, None, None, 'mp'), parts along dimension 3, may hold values from -1 to 127, as said below
Outputs:
- update: bfloat16 [2048, 256], P(None, 'mp'), parts along dimension 1
- new_momentum: float32 [16, 2048, 256], P('dp', None, 'mp'), parts along dimension 2
There are 2 independent parts, one for each index of `mp`. A program takes and returns all parts, laid end to end along the dimension named above; an argument that names none is the same for every part. Nothing has to cross between parts.
Inputs may be any that keep to these rules, and one draw needn't show every extreme that they name: `select`: in each [r, s, o] list the entries that are not -1 are distinct and come first. In every step some owner gets exactly 8 rows from every replica.
All inputs are finite; a program needn't handle non-finite values.
Results may differ from a plain program's by a relative error of at most 0.001.
Values sent between devices are 32-bit elements; how exact they have to be, the bound alone decides.
No kernel may reach another device: no remote copies, remote signals or barrier semaphores. Data moves between devices by JAX's collectives and lax.ppermute only.
A program may use at most 64 MiB of HBM per device.

v0:
```python
import jax
import jax.numpy as jnp
from jax import lax
from jax.sharding import PartitionSpec as P

GROUP = 64


def dct_matrix(order):
    freq = lax.broadcasted_iota(jnp.int32, (order, order), 0).astype(jnp.float32)
    place = lax.broadcasted_iota(jnp.int32, (order, order), 1).astype(jnp.float32)
    factor = jnp.where(freq == 0.0, jnp.sqrt(1.0 / order), jnp.sqrt(2.0 / order)).astype(
        jnp.float32
    )
    return factor * jnp.cos(jnp.pi * (2.0 * place + 1.0) * freq / (2.0 * order))


def forward_blocks(field, dct_table, col_table):
    row_count, col_count = field.shape
    order = dct_table.shape[0]
    shaped = field.reshape(row_count // order, order, col_count)
    rowwise = jnp.einsum("ui,aic->auc", dct_table, shaped, precision=lax.Precision.HIGHEST)
    return jnp.dot(
        rowwise.reshape(row_count, col_count), col_table.T, precision=lax.Precision.HIGHEST
    )


def inverse_blocks(coeffs, dct_table, col_table):
    row_count, col_count = coeffs.shape
    order = dct_table.shape[0]
    colwise = jnp.dot(coeffs, col_table, precision=lax.Precision.HIGHEST)
    shaped = colwise.reshape(row_count // order, order, col_count)
    back = jnp.einsum("ui,auc->aic", dct_table, shaped, precision=lax.Precision.HIGHEST)
    return back.reshape(row_count, col_count)


def layer_gradient(inputs, grad_out, iteration):
    return lax.dot_general(
        inputs[0, iteration],
        grad_out[0, iteration],
        (((0,), (0,)), ((), ())),
        preferred_element_type=jnp.float32,
    )


def per_device(inputs, grad_out, momentum, select):
    replica = lax.axis_index("dp")
    owners = lax.axis_size("dp")
    step_count = inputs.shape[1]
    moment_state = momentum[0]
    row_count, col_count = moment_state.shape
    per_owner = row_count // owners
    slot_count = select.shape[3]
    dct_table = dct_matrix(GROUP)
    col_table = jnp.kron(jnp.eye(col_count // GROUP, dtype=jnp.float32), dct_table)
    own_select = lax.dynamic_index_in_dim(select, replica, 0, keepdims=False)
    owner_base = lax.broadcasted_iota(jnp.int32, (owners, slot_count), 0) * per_owner
    row_ids = lax.broadcasted_iota(jnp.int32, (1, row_count), 1)
    owned_ids = lax.broadcasted_iota(jnp.int32, (1, per_owner), 1)
    update_sum = jnp.zeros((row_count, col_count), jnp.float32)
    for iteration in range(step_count):
        gradient = layer_gradient(inputs, grad_out, iteration)
        moment_state = 0.999 * moment_state + gradient
        coefficients = forward_blocks(moment_state, dct_table, col_table)
        listed = own_select[iteration]
        usable = listed >= 0
        global_rows = jnp.where(usable, listed + owner_base, -1)
        chosen = jnp.any(global_rows.reshape(-1, 1) == row_ids, axis=0)
        sent = jnp.where(chosen[:, None], coefficients, 0.0)
        picked = coefficients[jnp.where(usable, global_rows, 0)]
        picked = jnp.where(usable[:, :, None], picked, 0.0)
        arrived = lax.all_to_all(picked, "dp", split_axis=0, concat_axis=0, tiled=True)
        local_rows = lax.dynamic_index_in_dim(select[:, iteration], replica, 1, keepdims=False)
        onehot = (local_rows.reshape(-1, 1) == owned_ids).astype(jnp.float32)
        owned_sums = lax.dot_general(
            onehot,
            arrived.reshape(-1, col_count),
            (((0,), (0,)), ((), ())),
            precision=lax.Precision.HIGHEST,
        )
        summed = lax.all_gather(owned_sums, "dp", axis=0, tiled=True)
        update_sum = update_sum + inverse_blocks(summed, dct_table, col_table)
        moment_state = moment_state - inverse_blocks(sent, dct_table, col_table)
    return (update_sum.astype(jnp.bfloat16), moment_state[None])


def solution(mesh):
    return jax.shard_map(
        per_device,
        mesh=mesh,
        in_specs=(
            P("dp", None, None, None),
            P("dp", None, None, "mp"),
            P("dp", None, "mp"),
            P(None, None, None, "mp"),
        ),
        out_specs=(P(None, "mp"), P("dp", None, "mp")),
        check_vma=False,
    )
```

profile of v0, /device:TPU:0, one launch (start us, length us, event | category | flops | bytes accessed | tf_op | source)
XLA Modules:
  0.0 152.4 jit_solution(3903192236030922631)
XLA Ops:
  7.2 0.7 compare_bitcast_fusion
  9.2 2.1 %convolution_add_fusion.1 = f32[2048,128]{1,0:T(8,128)S(1)} fusion(bf16[1,2,256,2048]{3,2,1,0:T(8,128)(2,1)} %param.4, f32[1,2048,128]{2,1,0:T(8,128)} %param.6, bf16[1,2,256,128]{3,2,1,0:T(8,128)(2,1)} %param.5), kind=kOutput, calls=%fused_computation.3 | convolution fusion | flops 134742016 | bytes 3211264 | tf_op jit(solution)/shard_map/dot_general | solution.py:38
  11.3 1.2 fusion.25
  12.5 0.4 fusion.6
  12.9 1.0 broadcast_select_fusion.1
  13.9 0.6 gather_fusion
  14.6 0.7 bitcast_select_fusion.1
  15.3 8.3 %all-to-all-start = ((f32[16,8,128]{2,1,0:T(8,128)}), f32[16,8,128]{2,1,0:T(8,128)S(1)}, u32[]{:S(2)}, u32[]{:S(2)}) async-start(f32[16,8,128]{2,1,0:T(8,128)} %bitcast_select_fusion.1), calls=%async_computation | async-start | bytes 131072 | tf_op jit(solution)/shard_map/all_to_all | solution.py:72
  23.8 1.0 fusion.61
  24.8 1.3 fusion.21
  26.4 0.4 dynamic-slice_reduce_fusion.1
  26.9 4.3 %all-to-all-done = f32[16,8,128]{2,1,0:T(8,128)S(1)} async-done(((f32[16,8,128]{2,1,0:T(8,128)}), f32[16,8,128]{2,1,0:T(8,128)S(1)}, u32[]{:S(2)}, u32[]{:S(2)}) %all-to-all-start) | async-done | bytes 65568 | tf_op jit(solution)/shard_map/all_to_all | solution.py:72
  31.2 0.9 fusion.11
  32.3 1.4 copy-done
  33.7 0.5 convolution_add_fusion
  34.2 1.2 fusion.16
  35.5 1.0 broadcast_select_fusion
  36.5 0.6 gather_fusion.1
  37.1 0.7 bitcast_select_fusion
  37.8 3.5 %all-to-all-start.1 = ((f32[16,8,128]{2,1,0:T(8,128)}), f32[16,8,128]{2,1,0:T(8,128)S(1)}, u32[]{:S(2)}, u32[]{:S(2)}) async-start(f32[16,8,128]{2,1,0:T(8,128)} %bitcast_select_fusion), calls=%async_computation.1 | async-start | bytes 131072 | tf_op jit(solution)/shard_map/all_to_all | solution.py:72
  41.6 0.4 dynamic-slice_reduce_fusion
  42.1 6.8 %all-to-all-done.1 = f32[16,8,128]{2,1,0:T(8,128)S(1)} async-done(((f32[16,8,128]{2,1,0:T(8,128)}), f32[16,8,128]{2,1,0:T(8,128)S(1)}, u32[]{:S(2)}, u32[]{:S(2)}) %all-to-all-start.1) | async-done | bytes 65568 | tf_op jit(solution)/shard_map/all_to_all | solution.py:72
  48.8 0.9 fusion.8
  49.8 1.0 fusion.63
  50.8 1.3 fusion.18
  52.1 1.1 bitcast_subtract_fusion
  53.1 31.4 %all-gather.3.cloned.1.call-done = f32[2048,128]{1,0:T(8,128)} async-done(((f32[128,128]{1,0:T(8,128)}), f32[2048,128]{1,0:T(8,128)}) %all-gather.3.cloned.1.call-update) | async-done | bytes 1048592 | tf_op jit(solution)/shard_map/all_gather | solution.py:81
  84.5 2.2 %fusion.60 = f32[32,64,128]{2,1,0:T(8,128)S(1)} fusion(f32[32,64,128]{2,1,0:T(8,128)} %bitcast.116, f32[128,128,1]{1,0,2:T(8,128)S(1)} %reshape.313), kind=kOutput, calls=%fused_computation.100 | convolution fusion | flops 402653184 | bytes 2162688 | tf_op jit(solution)/shard_map/dot_general | solution.py:31
  86.7 1.3 fusion.23
  88.0 53.2 %all-gather.5.cloned.1.call-done = f32[2048,128]{1,0:T(8,128)} async-done(((f32[128,128]{1,0:T(8,128)}), f32[2048,128]{1,0:T(8,128)}) %all-gather.5.cloned.1.call-update) | async-done | bytes 1048592 | tf_op jit(solution)/shard_map/all_gather | solution.py:81
  141.2 2.2 %fusion.62 = f32[32,64,128]{2,1,0:T(8,128)S(1)} fusion(f32[32,64,128]{2,1,0:T(8,128)} %bitcast.117, f32[128,128,1]{1,0,2:T(8,128)S(1)} %reshape.313), kind=kOutput, calls=%fused_computation.102 | convolution fusion | flops 402653184 | bytes 2162688 | tf_op jit(solution)/shard_map/dot_general | solution.py:31
  143.4 2.1 %fusion = bf16[32,128,64]{1,2,0:T(8,128)(2,1)} fusion(f32[32,128,64]{1,2,0:T(8,128)S(1)} %fusion.23, f32[32,64,128]{2,1,0:T(8,128)S(1)} %fusion.62, f32[64]{0:T(128)S(1)} %convert_multiply_fusion, f32[64]{0:T(128)S(1)} %get-tuple-element.21, f32[64]{0:T(128)S(1)} %get-tuple-element.20), kind=kOutput, calls=%fused_computation.5 | convolution fusion | flops 201863168 | bytes 2622208 | tf_op jit(solution)/shard_map/ui,auc->aic/dot_general | solution.py:33
  (38 shorter events, 2.3 us)
Async XLA Ops:
  15.3 15.9 %all-to-all-start = ((f32[16,8,128]{2,1,0:T(8,128)}), f32[16,8,128]{2,1,0:T(8,128)S(1)}, u32[]{:S(2)}, u32[]{:S(2)}) async-start(f32[16,8,128]{2,1,0:T(8,128)} %bitcast_select_fusion.1), calls=%async_computation | async-start | bytes 131072 | tf_op jit(solution)/shard_map/all_to_all | solution.py:72
  23.6 60.9 %all-gather.3.cloned.1.call-start = ((), (), s32[]{:S(2)}) async-start(), calls=%async_computation.2 | async-start | bytes 1114112 | tf_op jit(solution)/shard_map/all_gather | solution.py:81
  23.8 2.3 %copy-start.1 = (s32[16,2,16,8]{2,3,1,0:T(8,128)S(1)}, s32[16,2,16,8]{2,3,1,0:T(8,128)}, u32[]{:S(2)}) copy-start(s32[16,2,16,8]{2,3,1,0:T(8,128)} %param.7) | copy-start | bytes 49156
  26.1 6.2 %copy-start.2 = (bf16[1,2,256,128]{3,2,1,0:T(8,128)(2,1)S(1)}, bf16[1,2,256,128]{3,2,1,0:T(8,128)(2,1)}, u32[]{:S(2)}) copy-start(bf16[1,2,256,128]{3,2,1,0:T(8,128)(2,1)} %param.5) | copy-start | bytes 393220
  32.1 1.6 %copy-start = (bf16[1,2,256,2048]{3,2,1,0:T(8,128)(2,1)S(1)}, bf16[1,2,256,2048]{3,2,1,0:T(8,128)(2,1)}, u32[]{:S(2)}) copy-start(bf16[1,2,256,2048]{3,2,1,0:T(8,128)(2,1)} %param.4) | copy-start | bytes 6291460
  37.8 11.0 %all-to-all-start.1 = ((f32[16,8,128]{2,1,0:T(8,128)}), f32[16,8,128]{2,1,0:T(8,128)S(1)}, u32[]{:S(2)}, u32[]{:S(2)}) async-start(f32[16,8,128]{2,1,0:T(8,128)} %bitcast_select_fusion), calls=%async_computation.1 | async-start | bytes 131072 | tf_op jit(solution)/shard_map/all_to_all | solution.py:72
  41.3 99.9 %all-gather.5.cloned.1.call-start = ((), (), s32[]{:S(2)}) async-start(), calls=%async_computation.3 | async-start | bytes 1114112 | tf_op jit(solution)/shard_map/all_gather | solution.py:81
Sparse Core Ops, SparseCore 0:
  32.3 52.2 all-gather.2
  87.3 53.9 all-gather.4
where the time goes:
time: 153 us; the launch traced here: 152 us
  waiting for transfers between devices  95.7 us (63%)
  matrix products  21.1 us (14%)
  between operations  14.3 us (9%)
  starting transfers between devices  12.1 us (8%)
  local copies, waits for them, and re-layouts  5.08 us (3%)
  other arithmetic  4.1 us (3%)
    all_gather x2, waiting for transfers between devices, per_device(): summed = lax.all_gather(owned_sums, 'dp', axis=0, tiled=True)  84.6 us
    all_to_all x2, starting transfers between devices, per_device(): lax.all_to_all(picked, 'dp', split_axis=0, concat_axis=0, tiled=True)  11.8 us
    all_to_all x2, waiting for transfers between devices, per_device(): lax.all_to_all(picked, 'dp', split_axis=0, concat_axis=0, tiled=True)  11 us
    dot_general x4, matrix products, inverse_blocks(): colwise = jnp.dot(coeffs, col_table, precision=lax.Precision.HIGHEST)  6.32 us
    dot_general x4, matrix products, inverse_blocks(): jnp.einsum('ui,auc->aic', dct_table, shaped, precision=lax.Precision.HIGH...  5.96 us
  transfers between devices with their start and end apart: 4, of which 4 were waited for; matrix products, arithmetic and copies ran while one was open for 10% of the time, Pallas kernels for 0%

commit v1 on v0

v1 whole, which is shorter than its diff:
```python
import functools

import jax
import jax.numpy as jnp
import numpy as np
from jax import lax
from jax.experimental import pallas as pl
from jax.experimental.pallas import tpu as pltpu
from jax.sharding import PartitionSpec as P

GROUP = 64
TILE = 2 * GROUP
CHUNKS = 4
F32 = jnp.float32
BF16 = jnp.bfloat16
VMEM = pl.BlockSpec(memory_space=pltpu.VMEM)
SMEM = pl.BlockSpec(memory_space=pltpu.SMEM)
ANY = pl.BlockSpec(memory_space=pl.ANY)


def block_dct(size):
    freq = np.arange(GROUP)[:, None]
    place = np.arange(GROUP)[None, :]
    factor = np.where(freq == 0, np.sqrt(1.0 / GROUP), np.sqrt(2.0 / GROUP))
    table = factor * np.cos(np.pi * (2.0 * place + 1.0) * freq / (2.0 * GROUP))
    return np.kron(np.eye(size // GROUP), table)


def halves(matrix):
    high = matrix.astype(jnp.bfloat16)
    low = (matrix - high.astype(np.float64)).astype(jnp.bfloat16)
    return high, low


def left_table(matrix):
    high, low = halves(matrix)
    return np.block([[high, high], [low, low]])


def right_table(matrix):
    high, low = halves(matrix)
    return np.block([[high, low], [high, low]])


def split(value, axis):
    high = value.astype(BF16)
    low = (value - high.astype(F32)).astype(BF16)
    return jnp.concatenate([high, low], axis=axis)


def mm(a, b):
    return jnp.dot(a, b, preferred_element_type=F32)


def mm_t(a, b):
    return lax.dot_general(a, b, (((0,), (0,)), ((), ())), preferred_element_type=F32)


def right(value, table):
    both = mm(split(value, 1), table)
    half = both.shape[1] // 2
    return both[:, :half] + both[:, half:]


def left(table, value):
    both = mm(table, split(value, 0))
    half = both.shape[0] // 2
    return both[:half] + both[half:]


def forward_kernel(index, x_hbm, g, m_hbm, row_t, col_t, picks, rest, x, m, c1, f2, sems):
    rows, cols = m.shape
    slots = index.shape[0] // 2
    width = rows // CHUNKS
    copies = []
    for c in range(CHUNKS):
        span = pl.ds(c * width, width)
        a = pltpu.make_async_copy(x_hbm.at[:, :, span], x.at[:, :, span], sems.at[c, 0])
        b = pltpu.make_async_copy(m_hbm.at[span], m.at[span], sems.at[c, 1])
        a.start()
        b.start()
        copies.append((a, b))
    c1[pl.ds(rows, 8), :] = jnp.zeros((8, cols), F32)
    rest[pl.ds(rows, 8), :] = jnp.zeros((8, cols), F32)
    table = col_t[...]
    row_table = row_t[...]
    second = mm(g[1], table[:cols])
    second = split(second[:, :cols] + second[:, cols:], 1)
    first = g[0]
    for c in range(CHUNKS):
        copies[c][0].wait()
        copies[c][1].wait()
        for r in range(c * width, (c + 1) * width, TILE):
            m1 = 0.999 * m[r : r + TILE] + mm_t(x[0, :, r : r + TILE], first)
            y1 = right(m1, table)
            y2 = mm_t(x[1, :, r : r + TILE], second)
            y2 = y2[:, :cols] + y2[:, cols:]
            z = left(row_table, jnp.concatenate([y1, y2], axis=1))
            c1[r : r + TILE] = z[:, :cols]
            f2[r : r + TILE] = z[:, cols:]
    per = picks.shape[1] // 2
    for k in range(slots):
        picks[k // per, pl.ds(k % per, 1), :] = c1[pl.ds(index[k], 1), :]
    zero = jnp.zeros((1, cols), F32)
    for k in range(slots):
        c1[pl.ds(index[k], 1), :] = zero
    rest[:rows] = 0.999 * c1[:rows] + f2[...]
    for k in range(slots):
        picks[k // per, pl.ds(per + k % per, 1), :] = rest[pl.ds(index[slots + k], 1), :]
    for k in range(slots):
        rest[pl.ds(index[slots + k], 1), :] = zero


def forward(index, x, g, m, slots):
    rows, cols = m.shape
    steps, tokens, _ = x.shape
    owners = index.shape[0] // (steps * slots)
    row_t = jnp.asarray(left_table(block_dct(TILE)))
    col_t = jnp.asarray(right_table(block_dct(cols).T))
    return pl.pallas_call(
        forward_kernel,
        out_shape=(
            jax.ShapeDtypeStruct((owners, steps * slots, cols), F32),
            jax.ShapeDtypeStruct((rows + 8, cols), F32),
        ),
        in_specs=[SMEM, ANY, VMEM, ANY, VMEM, VMEM],
        out_specs=(VMEM, VMEM),
        scratch_shapes=[
            pltpu.VMEM(x.shape, x.dtype),
            pltpu.VMEM((rows, cols), F32),
            pltpu.VMEM((rows + 8, cols), F32),
            pltpu.VMEM((rows, cols), F32),
            pltpu.SemaphoreType.DMA((CHUNKS, 2)),
        ],
        name="forward",
    )(index, x, g, m, row_t, col_t)


def inverse_tile(value, row_table, col_table):
    return left(row_table, right(value, col_table))


def inverse_kernel(coeffs, row_t, col_t, out):
    row_table, table = row_t[...], col_t[...]
    for r in range(0, out.shape[0], TILE):
        out[r : r + TILE] = inverse_tile(coeffs[r : r + TILE], row_table, table)


def inverse_tables(cols):
    return (
        jnp.asarray(left_table(block_dct(TILE).T)),
        jnp.asarray(right_table(block_dct(cols))),
    )


def inverse(coeffs, rows):
    cols = coeffs.shape[1]
    return pl.pallas_call(
        inverse_kernel,
        out_shape=jax.ShapeDtypeStruct((rows, cols), F32),
        in_specs=[VMEM] * 3,
        out_specs=VMEM,
        name="inverse",
    )(coeffs, *inverse_tables(cols))


def owned_kernel(whole, listed, arrived, row_t, col_t, out):
    rows, cols = out.shape
    slots = listed.shape[1]
    ids = lax.broadcasted_iota(jnp.int32, (rows, slots), 0)
    onehot = jnp.where(ids == listed[...], 1.0, 0.0).astype(BF16)
    both = mm(onehot, split(arrived[...].reshape(slots, cols), 1))
    summed = both[:, :cols] + both[:, cols:]
    if whole:
        for r in range(0, rows, TILE):
            out[r : r + TILE] = inverse_tile(summed[r : r + TILE], row_t[...], col_t[...])
    else:
        out[...] = summed


def owned_rows(listed, arrived, per_owner):
    cols = arrived.shape[-1]
    return pl.pallas_call(
        functools.partial(owned_kernel, per_owner % TILE == 0),
        out_shape=jax.ShapeDtypeStruct((per_owner, cols), F32),
        in_specs=[VMEM] * 4,
        out_specs=VMEM,
        name="owned",
    )(listed, arrived, *inverse_tables(cols))


def finish_kernel(whole, inner, me, row_t, col_t, *refs):
    blocks, out = refs[:-1], refs[-1]
    outer = blocks[0].shape[0]
    high, low = me[0] // inner, me[0] % inner
    for j, block in enumerate(blocks):
        for k in range(outer):
            place = (high ^ k) * inner + (low ^ j)
            out[place] = block[k].astype(out.dtype)


def finish(blocks, me, inner):
    outer, per_owner, cols = blocks[0].shape
    whole = per_owner % TILE == 0
    dtype = BF16 if whole else F32
    out = pl.pallas_call(
        functools.partial(finish_kernel, whole, inner),
        out_shape=jax.ShapeDtypeStruct((outer * inner, per_owner, cols), dtype),
        in_specs=[SMEM] + [VMEM] * (2 + len(blocks)),
        out_specs=VMEM,
        name="finish",
    )(me, *inverse_tables(cols), *blocks)
    out = out.reshape(outer * inner * per_owner, cols)
    if not whole:
        out = inverse(out, out.shape[0]).astype(BF16)
    return out


def per_device(inputs, grad_out, momentum, select):
    replica = lax.axis_index("dp")
    owners = lax.axis_size("dp")
    steps = inputs.shape[1]
    rows, cols = momentum.shape[1:]
    per_owner = rows // owners
    slots = select.shape[3]
    inner = 1
    while inner * inner < owners:
        inner *= 2
    outer = owners // inner

    own = lax.dynamic_index_in_dim(select, replica, 0, keepdims=False)
    base = lax.broadcasted_iota(jnp.int32, own.shape, 1) * per_owner
    index = jnp.where(own >= 0, own + base, rows).reshape(-1)
    picks, rest = forward(index, inputs[0], grad_out[0], momentum[0], slots)
    arrived = lax.all_to_all(picks, "dp", split_axis=0, concat_axis=0, tiled=True)

    new_momentum = inverse(rest, rows)
    listed = lax.dynamic_index_in_dim(select, replica, 2, keepdims=False).reshape(1, -1)
    mine = owned_rows(listed, arrived, per_owner)

    def from_peer(value, shift):
        return lax.ppermute(value, "dp", [(d, d ^ shift) for d in range(owners)])

    column = jnp.stack([mine] + [from_peer(mine, k * inner) for k in range(1, outer)])
    blocks = [column] + [from_peer(column, j) for j in range(1, inner)]
    update = finish(blocks, replica.reshape(1).astype(jnp.int32), inner)
    return (update, new_momentum[None])


def solution(mesh):
    return jax.shard_map(
        per_device,
        mesh=mesh,
        in_specs=(
            P("dp", None, None, None),
            P("dp", None, None, "mp"),
            P("dp", None, "mp"),
            P(None, None, None, "mp"),
        ),
        out_specs=(P(None, "mp"), P("dp", None, "mp")),
        check_vma=False,
    )
```

time: 153 us -> 55.9 us (0.37)
  waiting for transfers between devices: 95.7 us -> 15.6 us
  matrix products: 21.1 us -> 0 us
  Pallas kernels: 0 us -> 17.3 us
  between operations: 14.3 us -> 0.71 us
  starting transfers between devices: 12.1 us -> 16.3 us
  other arithmetic: 4.1 us -> 1.44 us
    all_gather x2 -> x0, waiting for transfers between devices: 84.6 us -> none  [per_device(): summed = lax.all_gather(owned_sums, 'dp', axis=0, tiled=True)]
    dot_general x16 -> x0, matrix products: 21.1 us -> none  [the longest x4 6.32 us: inverse_blocks(): colwise = jnp.dot(coeffs, col_table, precision=lax.Precision.HIGHEST)]
    pallas_call x0 -> x4, Pallas kernels: none -> 17.3 us  [the longest x1 8.72 us: forward(): pl.pallas_call(forward_kernel, out_shape=(jax.ShapeDtypeStruct((owners, s...]
    ppermute x0 -> x6, waiting for transfers between devices: none -> 9.26 us  [from_peer(): return lax.ppermute(value, 'dp', [(d, d ^ shift) for d in range(owners)])]
    ppermute x0 -> x6, starting transfers between devices: none -> 7.94 us  [from_peer(): return lax.ppermute(value, 'dp', [(d, d ^ shift) for d in range(owners)])]
    all_to_all x2 -> x1, waiting for transfers between devices: 11 us -> 6.36 us  [per_device(): lax.all_to_all(picks, 'dp', split_axis=0, concat_axis=0, tiled=True)]
    all_to_all x2 -> x1, starting transfers between devices: 11.8 us -> 8.36 us  [per_device(): lax.all_to_all(picks, 'dp', split_axis=0, concat_axis=0, tiled=True)]
  transfers between devices with their start and end apart: 4 -> 7, of which waited for: 4 -> 5; matrix products, arithmetic and copies ran while one was open for 10% -> 3% of each run, Pallas kernels for 0% -> 8%
where the time goes in v1:
time: 55.9 us; the launch traced here: 55.5 us
  Pallas kernels  17.3 us (31%)
  starting transfers between devices  16.3 us (29%)
  waiting for transfers between devices  15.6 us (28%)
  local copies, waits for them, and re-layouts  4.08 us (7%)
  other arithmetic  1.44 us (3%)
  between operations  0.71 us (1%)
    ppermute x6, waiting for transfers between devices, from_peer(): return lax.ppermute(value, 'dp', [(d, d ^ shift) for d in range(owners)])  9.26 us
    pallas_call x1, Pallas kernels, forward(): pl.pallas_call(forward_kernel, out_shape=(jax.ShapeDtypeStruct((owners, s...  8.72 us
    all_to_all x1, starting transfers between devices, per_device(): lax.all_to_all(picks, 'dp', split_axis=0, concat_axis=0, tiled=True)  8.36 us
    ppermute x6, starting transfers between devices, from_peer(): return lax.ppermute(value, 'dp', [(d, d ^ shift) for d in range(owners)])  7.94 us
    all_to_all x1, waiting for transfers between devices, per_device(): lax.all_to_all(picks, 'dp', split_axis=0, concat_axis=0, tiled=True)  6.36 us
    pallas_call x1, Pallas kernels, inverse(): pl.pallas_call(inverse_kernel, out_shape=jax.ShapeDtypeStruct((rows, cols...  4.29 us
    unnamed x12, local copies, waits for them, and re-layouts  2.32 us
    pallas_call x1, Pallas kernels, finish(): pl.pallas_call(functools.partial(finish_kernel, whole, inner), out_shape=...  2.18 us
  transfers between devices with their start and end apart: 7, of which 5 were waited for; matrix products, arithmetic and copies ran while one was open for 3% of the time, Pallas kernels for 8%

profile of v1, /device:TPU:0, one launch (start us, length us, event | category | flops | bytes accessed | tf_op | source)
XLA Modules:
  0.0 55.5 jit_solution(4717109802159152964)
XLA Ops:
  0.6 0.0 copy-start
  0.7 0.9 %copy-done = s32[16,2,16,8]{2,3,1,0:T(8,128)S(1)} copy-done((s32[16,2,16,8]{2,3,1,0:T(8,128)S(1)}, s32[16,2,16,8]{2,3,1,0:T(8,128)}, u32[]{:S(2)}) %copy-start) | copy-done | bytes 16408
  1.5 0.1 copy.14
  1.6 0.1 squeeze.15
  1.7 0.1 iota.9
  1.8 0.1 iota.10
  1.9 0.6 %compare_select_fusion.index = s32[256]{0:T(256)} fusion(s32[256]{0:T(256)S(1)} %squeeze.15, s32[256]{0:T(256)S(1)} %iota.10), kind=kLoop, calls=%fused_computation.2 | loop fusion | flops 768 | bytes 3072 | tf_op jit(solution)/shard_map/jit(_where)/select_n | solution.py:233
  2.4 8.7 %forward.1 = (f32[16,16,128]{2,1,0:T(8,128)}, f32[2056,128]{1,0:T(8,128)}) custom-call(s32[256]{0:T(256)} %compare_select_fusion.index, bf16[2,256,2048]{2,1,0:T(8,128)(2,1)} %bitcast.12, bf16[2,256,128]{2,1,0:T(8,128)(2,1)} %bitcast.17, f32[2048,128]{1,0:T(8,128)} %bitcast.14, bf16[256,256]{1,0:T(8,128)(2,1)} %constant.29.clone.row_t, ...), custom_call_target="tpu_custom_call" | custom-call | tf_op jit(solution)/shard_map/forward/pallas_call | solution.py:120
  11.2 8.4 %all-to-all-start = ((f32[16,16,128]{2,1,0:T(8,128)}), f32[16,16,128]{2,1,0:T(8,128)S(1)}, u32[]{:S(2)}, u32[]{:S(2)}) async-start(f32[16,16,128]{2,1,0:T(8,128)} %get-tuple-element.4), calls=%async_computation | async-start | bytes 262144 | tf_op jit(solution)/shard_map/all_to_all | solution.py:235
  19.5 0.7 %dynamic-slice_reduce_fusion = s32[16,2,8]{2,1,0:T(2,128)S(1)} fusion(s32[16,2,16,8]{2,3,1,0:T(8,128)S(1)} %copy-done, s32[]{:T(128)S(6)} %select_n.11), kind=kLoop, calls=%fused_computation.1 | loop fusion | bytes 2052 | tf_op jit(solution)/shard_map/jit(dynamic_index_in_dim)/dynamic_slice | solution.py:238
  20.3 0.7 %reshape.18.listed = s32[1,256]{1,0:T(1,128)} reshape(s32[16,2,8]{2,1,0:T(2,128)S(1)} %dynamic-slice_reduce_fusion) | data formatting | bytes 2048 | tf_op jit(solution)/shard_map/reshape | solution.py:238
  21.0 6.4 %all-to-all-done.arrived = f32[16,16,128]{2,1,0:T(8,128)S(1)} async-done(((f32[16,16,128]{2,1,0:T(8,128)}), f32[16,16,128]{2,1,0:T(8,128)S(1)}, u32[]{:S(2)}, u32[]{:S(2)}) %all-to-all-start) | async-done | bytes 131104 | tf_op jit(solution)/shard_map/all_to_all | solution.py:235
  27.3 0.7 %copy-done.2 = f32[16,16,128]{2,1,0:T(8,128)} copy-done((f32[16,16,128]{2,1,0:T(8,128)}, f32[16,16,128]{2,1,0:T(8,128)S(1)}, u32[]{:S(2)}) %copy-start.2) | copy-done | bytes 131096
  28.0 2.2 %owned.1 = f32[128,128]{1,0:T(8,128)} custom-call(s32[1,256]{1,0:T(1,128)} %reshape.18.listed, f32[16,16,128]{2,1,0:T(8,128)} %copy-done.2, bf16[256,256]{1,0:T(8,128)(2,1)} %constant.31.clone.row_t, bf16[256,256]{1,0:T(8,128)(2,1)} %constant.32.clone.col_t), custom_call_target="tpu_custom_call" | custom-call | tf_op jit(solution)/shard_map/owned/pallas_call | solution.py:183
  30.2 1.3 %collective-permute-start.2 = (f32[128,128]{1,0:T(8,128)}, f32[128,128]{1,0:T(8,128)S(1)}, u32[]{:S(2)}, u32[]{:S(2)}) collective-permute-start(f32[128,128]{1,0:T(8,128)} %owned.1), channel_id=1, source_target_pairs={{0,24},{2,26},{4,28},{6,30},{8,16},{10,18},{12,20},{14,22},{16,8},... | collective-permute-start | bytes 196616 | tf_op jit(solution)/shard_map/ppermute | solution.py:242
  31.4 0.9 %collective-permute-start.1 = (f32[128,128]{1,0:T(8,128)}, f32[128,128]{1,0:T(8,128)S(1)}, u32[]{:S(2)}, u32[]{:S(2)}) collective-permute-start(f32[128,128]{1,0:T(8,128)} %owned.1), channel_id=1, source_target_pairs={{0,16},{2,18},{4,20},{6,22},{8,24},{10,26},{12,28},{14,30},{16,0},... | collective-permute-start | bytes 196616 | tf_op jit(solution)/shard_map/ppermute | solution.py:242
  32.4 2.2 %collective-permute-start = (f32[128,128]{1,0:T(8,128)}, f32[128,128]{1,0:T(8,128)S(1)}, u32[]{:S(2)}, u32[]{:S(2)}) collective-permute-start(f32[128,128]{1,0:T(8,128)} %owned.1), channel_id=1, source_target_pairs={{0,8},{2,10},{4,12},{6,14},{8,0},{10,2},{12,4},{14,6},{16,24},{18,... | collective-permute-start | bytes 196616 | tf_op jit(solution)/shard_map/ppermute | solution.py:242
  34.5 2.0 %collective-permute-done.2 = f32[128,128]{1,0:T(8,128)S(1)} collective-permute-done((f32[128,128]{1,0:T(8,128)}, f32[128,128]{1,0:T(8,128)S(1)}, u32[]{:S(2)}, u32[]{:S(2)}) %collective-permute-start.2) | collective-permute-done | bytes 65568 | tf_op jit(solution)/shard_map/ppermute | solution.py:242
  36.5 1.5 %collective-permute-done.1 = f32[128,128]{1,0:T(8,128)S(1)} collective-permute-done((f32[128,128]{1,0:T(8,128)}, f32[128,128]{1,0:T(8,128)S(1)}, u32[]{:S(2)}, u32[]{:S(2)}) %collective-permute-start.1) | collective-permute-done | bytes 65568 | tf_op jit(solution)/shard_map/ppermute | solution.py:242
  38.1 0.0 collective-permute-done
  38.1 0.9 %pad_maximum_fusion.refs_0_ = f32[4,128,128]{2,1,0:T(8,128)S(1)} fusion(f32[1,128,128]{2,1,0:T(8,128)S(1)} %bitcast.18, f32[1,128,128]{2,1,0:T(8,128)S(1)} %bitcast.19, f32[1,128,128]{2,1,0:T(8,128)S(1)} %bitcast.20, f32[1,128,128]{2,1,0:T(8,128)} %bitcast.16), kind=kLoop, calls=%fused_computation | loop fusion | flops 196608 | bytes 524288 | tf_op jit(solution)/shard_map/stack | solution.py:244
  39.0 0.9 %collective-permute-start.5 = (f32[4,128,128]{2,1,0:T(8,128)S(1)}, f32[4,128,128]{2,1,0:T(8,128)S(1)}, u32[]{:S(2)}, u32[]{:S(2)}) collective-permute-start(f32[4,128,128]{2,1,0:T(8,128)S(1)} %pad_maximum_fusion.refs_0_), channel_id=1, source_target_pairs={{0,6},{2,4},{4,2},{6,0},{8,14},{10,12},{12,10},{14,8},{16,22},{18,... | collective-permute-start | bytes 786440 | tf_op jit(solution)/shard_map/ppermute | solution.py:242
  39.9 1.3 %collective-permute-start.4 = (f32[4,128,128]{2,1,0:T(8,128)S(1)}, f32[4,128,128]{2,1,0:T(8,128)S(1)}, u32[]{:S(2)}, u32[]{:S(2)}) collective-permute-start(f32[4,128,128]{2,1,0:T(8,128)S(1)} %pad_maximum_fusion.refs_0_), channel_id=1, source_target_pairs={{0,4},{2,6},{4,0},{6,2},{8,12},{10,14},{12,8},{14,10},{16,20},{18,... | collective-permute-start | bytes 786440 | tf_op jit(solution)/shard_map/ppermute | solution.py:242
  41.2 1.3 %collective-permute-start.3 = (f32[4,128,128]{2,1,0:T(8,128)S(1)}, f32[4,128,128]{2,1,0:T(8,128)S(1)}, u32[]{:S(2)}, u32[]{:S(2)}) collective-permute-start(f32[4,128,128]{2,1,0:T(8,128)S(1)} %pad_maximum_fusion.refs_0_), channel_id=1, source_target_pairs={{0,2},{2,0},{4,6},{6,4},{8,10},{10,8},{12,14},{14,12},{16,18},{18,... | collective-permute-start | bytes 786440 | tf_op jit(solution)/shard_map/ppermute | solution.py:242
  42.5 4.3 %inverse.1 = f32[2048,128]{1,0:T(8,128)} custom-call(f32[2056,128]{1,0:T(8,128)} %get-tuple-element.5.coeffs, bf16[256,256]{1,0:T(8,128)(2,1)} %constant.31.clone.row_t, bf16[256,256]{1,0:T(8,128)(2,1)} %constant.32.clone.col_t), custom_call_target="tpu_custom_call" | custom-call | tf_op jit(solution)/shard_map/inverse/pallas_call | solution.py:158
  46.8 2.3 %collective-permute-done.5.refs_3_ = f32[4,128,128]{2,1,0:T(8,128)S(1)} collective-permute-done((f32[4,128,128]{2,1,0:T(8,128)S(1)}, f32[4,128,128]{2,1,0:T(8,128)S(1)}, u32[]{:S(2)}, u32[]{:S(2)}) %collective-permute-start.5) | collective-permute-done | bytes 262176 | tf_op jit(solution)/shard_map/ppermute | solution.py:242
  49.1 3.4 %collective-permute-done.4.refs_2_ = f32[4,128,128]{2,1,0:T(8,128)S(1)} collective-permute-done((f32[4,128,128]{2,1,0:T(8,128)S(1)}, f32[4,128,128]{2,1,0:T(8,128)S(1)}, u32[]{:S(2)}, u32[]{:S(2)}) %collective-permute-start.4) | collective-permute-done | bytes 262176 | tf_op jit(solution)/shard_map/ppermute | solution.py:242
  52.5 0.0 collective-permute-done.3.refs_1_
  52.5 0.0 copy-done.3
  52.6 0.7 %copy-done.4 = f32[4,128,128]{2,1,0:T(8,128)} copy-done((f32[4,128,128]{2,1,0:T(8,128)}, f32[4,128,128]{2,1,0:T(8,128)S(1)}, u32[]{:S(2)}) %copy-start.4) | copy-done | bytes 262168
  53.2 0.1 copy-done.5
  53.3 2.2 %finish.1 = bf16[16,128,128]{2,1,0:T(8,128)(2,1)} custom-call(s32[1]{0:T(128)} %bitcast.me, bf16[256,256]{1,0:T(8,128)(2,1)} %constant.31.clone.row_t, bf16[256,256]{1,0:T(8,128)(2,1)} %constant.32.clone.col_t, f32[4,128,128]{2,1,0:T(8,128)} %copy-done.1, f32[4,128,128]{2,1,0:T(8,128)} %copy-done.5, f32[4,128,128]{2,1,0:T(8,128)} %copy-done.4, ...), custom_call_target="tpu_custom_call" | custom-call | tf_op jit(solution)/shard_map/finish/pallas_call | solution.py:206
  (8 shorter events, 0.0 us)
Async XLA Ops:
  0.6 0.9 %copy-start = (s32[16,2,16,8]{2,3,1,0:T(8,128)S(1)}, s32[16,2,16,8]{2,3,1,0:T(8,128)}, u32[]{:S(2)}) copy-start(s32[16,2,16,8]{2,3,1,0:T(8,128)} %param.15) | copy-start | bytes 49156
  11.2 16.2 %all-to-all-start = ((f32[16,16,128]{2,1,0:T(8,128)}), f32[16,16,128]{2,1,0:T(8,128)S(1)}, u32[]{:S(2)}, u32[]{:S(2)}) async-start(f32[16,16,128]{2,1,0:T(8,128)} %get-tuple-element.4), calls=%async_computation | async-start | bytes 262144 | tf_op jit(solution)/shard_map/all_to_all | solution.py:235
  27.3 0.7 %copy-start.2 = (f32[16,16,128]{2,1,0:T(8,128)}, f32[16,16,128]{2,1,0:T(8,128)S(1)}, u32[]{:S(2)}) copy-start(f32[16,16,128]{2,1,0:T(8,128)S(1)} %all-to-all-done.arrived) | copy-start | bytes 393220
  30.2 6.4 %collective-permute-start.2 = (f32[128,128]{1,0:T(8,128)}, f32[128,128]{1,0:T(8,128)S(1)}, u32[]{:S(2)}, u32[]{:S(2)}) collective-permute-start(f32[128,128]{1,0:T(8,128)} %owned.1), channel_id=1, source_target_pairs={{0,24},{2,26},{4,28},{6,30},{8,16},{10,18},{12,20},{14,22},{16,8},... | collective-permute-start | bytes 196616 | tf_op jit(solution)/shard_map/ppermute | solution.py:242
  31.4 6.7 %collective-permute-start.1 = (f32[128,128]{1,0:T(8,128)}, f32[128,128]{1,0:T(8,128)S(1)}, u32[]{:S(2)}, u32[]{:S(2)}) collective-permute-start(f32[128,128]{1,0:T(8,128)} %owned.1), channel_id=1, source_target_pairs={{0,16},{2,18},{4,20},{6,22},{8,24},{10,26},{12,28},{14,30},{16,0},... | collective-permute-start | bytes 196616 | tf_op jit(solution)/shard_map/ppermute | solution.py:242
  32.4 5.7 %collective-permute-start = (f32[128,128]{1,0:T(8,128)}, f32[128,128]{1,0:T(8,128)S(1)}, u32[]{:S(2)}, u32[]{:S(2)}) collective-permute-start(f32[128,128]{1,0:T(8,128)} %owned.1), channel_id=1, source_target_pairs={{0,8},{2,10},{4,12},{6,14},{8,0},{10,2},{12,4},{14,6},{16,24},{18,... | collective-permute-start | bytes 196616 | tf_op jit(solution)/shard_map/ppermute | solution.py:242
  38.9 13.6 %copy-start.1 = (f32[4,128,128]{2,1,0:T(8,128)}, f32[4,128,128]{2,1,0:T(8,128)S(1)}, u32[]{:S(2)}) copy-start(f32[4,128,128]{2,1,0:T(8,128)S(1)} %pad_maximum_fusion.refs_0_) | copy-start | bytes 786436
  39.0 10.1 %collective-permute-start.5 = (f32[4,128,128]{2,1,0:T(8,128)S(1)}, f32[4,128,128]{2,1,0:T(8,128)S(1)}, u32[]{:S(2)}, u32[]{:S(2)}) collective-permute-start(f32[4,128,128]{2,1,0:T(8,128)S(1)} %pad_maximum_fusion.refs_0_), channel_id=1, source_target_pairs={{0,6},{2,4},{4,2},{6,0},{8,14},{10,12},{12,10},{14,8},{16,22},{18,... | collective-permute-start | bytes 786440 | tf_op jit(solution)/shard_map/ppermute | solution.py:242
  39.9 12.7 %collective-permute-start.4 = (f32[4,128,128]{2,1,0:T(8,128)S(1)}, f32[4,128,128]{2,1,0:T(8,128)S(1)}, u32[]{:S(2)}, u32[]{:S(2)}) collective-permute-start(f32[4,128,128]{2,1,0:T(8,128)S(1)} %pad_maximum_fusion.refs_0_), channel_id=1, source_target_pairs={{0,4},{2,6},{4,0},{6,2},{8,12},{10,14},{12,8},{14,10},{16,20},{18,... | collective-permute-start | bytes 786440 | tf_op jit(solution)/shard_map/ppermute | solution.py:242
  41.2 11.4 %collective-permute-start.3 = (f32[4,128,128]{2,1,0:T(8,128)S(1)}, f32[4,128,128]{2,1,0:T(8,128)S(1)}, u32[]{:S(2)}, u32[]{:S(2)}) collective-permute-start(f32[4,128,128]{2,1,0:T(8,128)S(1)} %pad_maximum_fusion.refs_0_), channel_id=1, source_target_pairs={{0,2},{2,0},{4,6},{6,4},{8,10},{10,8},{12,14},{14,12},{16,18},{18,... | collective-permute-start | bytes 786440 | tf_op jit(solution)/shard_map/ppermute | solution.py:242
  49.1 3.4 %copy-start.3 = (f32[4,128,128]{2,1,0:T(8,128)}, f32[4,128,128]{2,1,0:T(8,128)S(1)}, u32[]{:S(2)}) copy-start(f32[4,128,128]{2,1,0:T(8,128)S(1)} %collective-permute-done.5.refs_3_) | copy-start | bytes 786436
  52.5 0.7 %copy-start.4 = (f32[4,128,128]{2,1,0:T(8,128)}, f32[4,128,128]{2,1,0:T(8,128)S(1)}, u32[]{:S(2)}) copy-start(f32[4,128,128]{2,1,0:T(8,128)S(1)} %collective-permute-done.4.refs_2_) | copy-start | bytes 786436
  52.5 0.8 %copy-start.5 = (f32[4,128,128]{2,1,0:T(8,128)}, f32[4,128,128]{2,1,0:T(8,128)S(1)}, u32[]{:S(2)}) copy-start(f32[4,128,128]{2,1,0:T(8,128)S(1)} %collective-permute-done.3.refs_1_) | copy-start | bytes 786436

commit v2 on v1

v2 whole, which is shorter than its diff:
```python
import functools

import jax
import jax.numpy as jnp
import numpy as np
from jax import lax
from jax.experimental import pallas as pl
from jax.experimental.pallas import tpu as pltpu
from jax.sharding import PartitionSpec as P

GROUP = 64
CHUNKS = 4
F32 = jnp.float32
BF16 = jnp.bfloat16
IN_VMEM = pl.BlockSpec(memory_space=pltpu.VMEM)
IN_HBM = pl.BlockSpec(memory_space=pltpu.HBM)
PARAMS = pltpu.CompilerParams(vmem_limit_bytes=16 << 20)


def tables(size):
    freq = np.arange(GROUP)[:, None]
    place = np.arange(GROUP)[None, :]
    factor = np.where(freq == 0, np.sqrt(1.0 / GROUP), np.sqrt(2.0 / GROUP))
    table = factor * np.cos(np.pi * (2.0 * place + 1.0) * freq / (2.0 * GROUP))
    table = np.kron(np.eye(size // GROUP), table)
    high = table.astype(jnp.bfloat16)
    low = (table - high.astype(np.float64)).astype(jnp.bfloat16)
    return jnp.asarray(np.stack([high, low, high.T, low.T]))


def vmem(value):
    return pltpu.with_memory_space_constraint(value, pltpu.VMEM)


def left_table(high, low):
    return jnp.concatenate(
        [jnp.concatenate([high, high], 1), jnp.concatenate([low, low], 1)], 0
    )


def right_table(high, low):
    row = jnp.concatenate([high, low], 1)
    return jnp.concatenate([row, row], 0)


def split(value, axis):
    high = value.astype(BF16)
    low = (value - high.astype(F32)).astype(BF16)
    return jnp.concatenate([high, low], axis=axis)


def mm(a, b):
    return jnp.dot(a, b, preferred_element_type=F32)


def mm_t(a, b):
    return lax.dot_general(a, b, (((0,), (0,)), ((), ())), preferred_element_type=F32)


def add_columns(both):
    half = both.shape[1] // 2
    return both[:, :half] + both[:, half:]


def right(value, table):
    return add_columns(mm(split(value, 1), table))


def left(table, value):
    both = mm(table, split(value, 0))
    half = both.shape[0] // 2
    return both[:half] + both[half:]


def forward_kernel(
    inner, select, x_hbm, g, m_hbm, dct, *refs
):
    picks, rest = refs[:inner], refs[inner]
    x, m, c1, f2, listed, index_v, index, sems, sel_sem = refs[inner + 1 :]
    me = lax.axis_index("dp")
    rows, cols = m.shape
    steps, slots, owners = index.shape
    per_class = owners // inner
    mine = me % inner
    fetch = pltpu.make_async_copy(select.at[me], listed, sel_sem)
    fetch.start()
    width = rows // CHUNKS
    copies = []
    for c in range(CHUNKS):
        span = pl.ds(c * width, width)
        a = pltpu.make_async_copy(x_hbm.at[:, :, span], x.at[:, :, span], sems.at[c, 0])
        b = pltpu.make_async_copy(m_hbm.at[span], m.at[span], sems.at[c, 1])
        a.start()
        b.start()
        copies.append((a, b))
    c1[pl.ds(rows, 8), :] = jnp.zeros((8, cols), F32)
    rest[pl.ds(rows, 8), :] = jnp.zeros((8, cols), F32)
    table = right_table(dct[2], dct[3])
    row_table = left_table(dct[0], dct[1])
    second = split(add_columns(mm(g[1], table[:cols])), 1)
    first = g[0]
    fetch.wait()
    owner = lax.broadcasted_iota(jnp.int32, listed.shape, 2)
    index_v[...] = jnp.where(listed[...] >= 0, listed[...] + owner * (rows // owners), rows)
    store = pltpu.make_async_copy(index_v, index, sel_sem)
    store.start()
    for c in range(CHUNKS):
        copies[c][0].wait()
        copies[c][1].wait()
        for r in range(c * width, (c + 1) * width, cols):
            m1 = 0.999 * m[r : r + cols] + mm_t(x[0, :, r : r + cols], first)
            y1 = right(m1, table)
            y2 = add_columns(mm_t(x[1, :, r : r + cols], second))
            z = left(row_table, jnp.concatenate([y1, y2], axis=1))
            c1[r : r + cols] = z[:, :cols]
            f2[r : r + cols] = z[:, cols:]
    store.wait()
    zero = jnp.zeros((1, cols), F32)

    def gather(step, source):
        for j in range(inner):
            base = (mine ^ j) * per_class
            for k in range(per_class):
                for c in range(slots):
                    place = (k * steps + step) * slots + c
                    picks[j][pl.ds(place, 1), :] = source[pl.ds(index[step, c, base + k], 1), :]

    def clear(step, target):
        for k in range(owners):
            for c in range(slots):
                target[pl.ds(index[step, c, k], 1), :] = zero

    gather(0, c1)
    clear(0, c1)
    rest[:rows] = 0.999 * c1[:rows] + f2[...]
    gather(1, rest)
    clear(1, rest)


def forward(select, x, g, m, dct, inner):
    rows, cols = m.shape
    steps = x.shape[0]
    owners, _, slots, _ = select.shape
    block = pltpu.VMEM((owners // inner * steps * slots, cols), F32)
    return pl.pallas_call(
        functools.partial(forward_kernel, inner),
        out_shape=[block] * inner + [pltpu.VMEM((rows + 8, cols), F32)],
        in_specs=[IN_HBM, IN_HBM, IN_VMEM, IN_HBM, IN_VMEM],
        out_specs=[IN_VMEM] * (inner + 1),
        scratch_shapes=[
            pltpu.VMEM(x.shape, x.dtype),
            pltpu.VMEM((rows, cols), F32),
            pltpu.VMEM((rows + 8, cols), F32),
            pltpu.VMEM((rows, cols), F32),
            pltpu.VMEM(select.shape[1:], jnp.int32),
            pltpu.VMEM(select.shape[1:], jnp.int32),
            pltpu.SMEM(select.shape[1:], jnp.int32),
            pltpu.SemaphoreType.DMA((CHUNKS, 2)),
            pltpu.SemaphoreType.DMA,
        ],
        compiler_params=PARAMS,
        name="forward",
    )(select, x, g, m, dct)


def inverse_tile(value, row_table, col_table):
    return left(row_table, right(value, col_table))


def inverse_kernel(coeffs, dct, out):
    row_table, table = left_table(dct[2], dct[3]), right_table(dct[0], dct[1])
    rows, cols = out.shape
    for r in range(0, rows, cols):
        out[r : r + cols] = inverse_tile(coeffs[r : r + cols], row_table, table)


def inverse(coeffs, dct, rows):
    cols = coeffs.shape[1]
    return pl.pallas_call(
        inverse_kernel,
        out_shape=jax.ShapeDtypeStruct((rows, cols), F32),
        in_specs=[IN_VMEM] * 2,
        out_specs=IN_VMEM,
        compiler_params=PARAMS,
        name="inverse",
    )(vmem(coeffs), dct)


def class_kernel(inner, listed, dct, *refs):
    blocks, out, ordered, total = refs[:-3], refs[-3], refs[-2], refs[-1]
    me = lax.axis_index("dp")
    rows, cols = out.shape
    per_class, slots = listed.shape
    per_owner = rows // per_class
    replicas = len(blocks) * inner
    each = slots // replicas
    for k, block in enumerate(blocks):
        for j in range(inner):
            replica = (me // inner ^ k) * inner + (me % inner ^ j)
            span = pl.ds(pl.multiple_of(replica * each, each), each)
            for o in range(per_class):
                ordered[o, span, :] = split(block[pl.ds((j * per_class + o) * each, each), :], 1)
    ids = lax.broadcasted_iota(jnp.int32, (per_owner, slots), 0)
    for o in range(per_class):
        onehot = jnp.where(ids == listed[pl.ds(o, 1), :], 1.0, 0.0).astype(BF16)
        total[pl.ds(o * per_owner, per_owner), :] = add_columns(mm(onehot, ordered[o]))
    row_table, table = left_table(dct[2], dct[3]), right_table(dct[0], dct[1])
    for r in range(0, rows, cols):
        out[r : r + cols] = inverse_tile(total[r : r + cols], row_table, table)


def class_rows(listed, blocks, dct, inner, rows):
    cols = blocks[0].shape[1]
    per_class, slots = listed.shape
    return pl.pallas_call(
        functools.partial(class_kernel, inner),
        out_shape=pltpu.VMEM((rows, cols), F32),
        in_specs=[IN_VMEM] * (2 + len(blocks)),
        out_specs=IN_VMEM,
        scratch_shapes=[
            pltpu.VMEM((per_class, slots, 2 * cols), BF16),
            pltpu.VMEM((rows, cols), F32),
        ],
        compiler_params=PARAMS,
        name="class_rows",
    )(listed, dct, *[vmem(b) for b in blocks])


def finish_kernel(*refs):
    count = len(refs) // 2
    blocks, out, held, sems = refs[:-3], refs[-3], refs[-2], refs[-1]
    me = lax.axis_index("dp")
    copies = []
    for j, block in enumerate(blocks):
        held[j] = block[...].astype(held.dtype)
        copy = pltpu.make_async_copy(held.at[j], out.at[me % len(blocks) ^ j], sems.at[j])
        copy.start()
        copies.append(copy)
    for copy in copies:
        copy.wait()


def finish(blocks):
    shape = (len(blocks),) + blocks[0].shape
    return pl.pallas_call(
        finish_kernel,
        out_shape=jax.ShapeDtypeStruct(shape, BF16),
        in_specs=[IN_VMEM] * len(blocks),
        out_specs=IN_HBM,
        scratch_shapes=[pltpu.VMEM(shape, BF16), pltpu.SemaphoreType.DMA((len(blocks),))],
        compiler_params=PARAMS,
        name="finish",
    )(*[vmem(b) for b in blocks])


def per_device(inputs, grad_out, momentum, select):
    replica = lax.axis_index("dp")
    owners = lax.axis_size("dp")
    rows, cols = momentum.shape[1:]
    inner = 1
    while inner * inner < owners:
        inner *= 2
    outer = owners // inner
    dct = tables(cols)

    def from_peer(value, shift):
        return lax.ppermute(value, "dp", [(d, d ^ shift) for d in range(owners)])

    *picks, rest = forward(
        jnp.swapaxes(select, 2, 3), inputs[0], grad_out[0], momentum[0], dct, inner
    )
    plane = jnp.concatenate(
        [picks[0]] + [from_peer(picks[j], j) for j in range(1, inner)]
    )
    blocks = [plane] + [from_peer(plane, k * inner) for k in range(1, outer)]
    new_momentum = inverse(rest, dct, rows)
    listed = jnp.transpose(select, (2, 0, 1, 3)).reshape(owners, -1)
    listed = lax.dynamic_slice_in_dim(listed, replica % inner * outer, outer, 0)
    own = class_rows(listed, blocks, dct, inner, rows // inner)
    update = finish([own] + [from_peer(own, j) for j in range(1, inner)])
    return (update.reshape(rows, cols), new_momentum[None])


def solution(mesh):
    return jax.shard_map(
        per_device,
        mesh=mesh,
        in_specs=(
            P("dp", None, None, None),
            P("dp", None, None, "mp"),
            P("dp", None, "mp"),
            P(None, None, None, "mp"),
        ),
        out_specs=(P(None, "mp"), P("dp", None, "mp")),
        check_vma=False,
    )
```

time: 55.9 us -> 50.3 us (0.90)
  Pallas kernels: 17.3 us -> 11.2 us
  waiting for transfers between devices: 15.6 us -> 20 us
  starting transfers between devices: 16.3 us -> 12.5 us
  local copies, waits for them, and re-layouts: 4.08 us -> 5.71 us
  other arithmetic: 1.44 us -> 0 us
    ppermute x6 -> x9, waiting for transfers between devices: 9.26 us -> 20 us  [from_peer(): return lax.ppermute(value, 'dp', [(d, d ^ shift) for d in range(owners)])]
    all_to_all x1 -> x0, starting transfers between devices: 8.36 us -> none  [per_device(): lax.all_to_all(picks, 'dp', split_axis=0, concat_axis=0, tiled=True)]
    all_to_all x1 -> x0, waiting for transfers between devices: 6.36 us -> none  [per_device(): lax.all_to_all(picks, 'dp', split_axis=0, concat_axis=0, tiled=True)]
    pallas_call x3, Pallas kernels: 13.1 us -> 8.19 us  [the longest x1 6.52 us: forward(): pl.pallas_call(functools.partial(forward_kernel, inner), out_shape=[block...]
    ppermute x6 -> x9, starting transfers between devices: 7.94 us -> 12.5 us  [from_peer(): return lax.ppermute(value, 'dp', [(d, d ^ shift) for d in range(owners)])]
    unnamed x12 -> x18, local copies, waits for them, and re-layouts: 2.32 us -> 5.62 us
    pallas_call x1, Pallas kernels: 4.29 us -> 2.98 us  [inverse(): pl.pallas_call(inverse_kernel, out_shape=jax.ShapeDtypeStruct((rows, cols...]
    another operation x1 -> x0, other arithmetic: 0.87 us -> none  [per_device(): jnp.stack([mine] + [from_peer(mine, k * inner) for k in range(1, outer)])]
  transfers between devices with their start and end apart: 7 -> 9, of which waited for: 5 -> 7; matrix products, arithmetic and copies ran while one was open for 3% -> 0% of each run, Pallas kernels for 8% -> 6%
where the time goes in v2:
time: 50.3 us; the launch traced here: 50 us
  waiting for transfers between devices  20 us (40%)
  starting transfers between devices  12.5 us (25%)
  Pallas kernels  11.2 us (22%)
  local copies, waits for them, and re-layouts  5.71 us (11%)
  between operations  0.68 us (1%)
    ppermute x9, waiting for transfers between devices, from_peer(): return lax.ppermute(value, 'dp', [(d, d ^ shift) for d in range(owners)])  20 us
    ppermute x9, starting transfers between devices, from_peer(): return lax.ppermute(value, 'dp', [(d, d ^ shift) for d in range(owners)])  12.5 us
    pallas_call x1, Pallas kernels, forward(): pl.pallas_call(functools.partial(forward_kernel, inner), out_shape=[block...  6.52 us
    unnamed x18, local copies, waits for them, and re-layouts  5.62 us
    pallas_call x1, Pallas kernels, inverse(): pl.pallas_call(inverse_kernel, out_shape=jax.ShapeDtypeStruct((rows, cols...  2.98 us
  transfers between devices with their start and end apart: 9, of which 7 were waited for; matrix products, arithmetic and copies ran while one was open for 0% of the time, Pallas kernels for 6%

profile of v2, /device:TPU:0, one launch (start us, length us, event | category | flops | bytes accessed | tf_op | source)
XLA Modules:
  0.0 50.0 jit_solution(9452550187729897285)
XLA Ops:
  0.6 0.0 copy-start
  0.6 1.6 %copy-done = bf16[1,2,256,2048]{3,2,1,0:T(8,128)(2,1)S(1)} copy-done((bf16[1,2,256,2048]{3,2,1,0:T(8,128)(2,1)S(1)}, bf16[1,2,256,2048]{3,2,1,0:T(8,128)(2,1)}, u32[]{:S(2)}) %copy-start) | copy-done | bytes 2097176
  2.2 0.9 %copy-done.1 = bf16[4,128,128]{2,1,0:T(8,128)(2,1)S(1)} copy-done((bf16[4,128,128]{2,1,0:T(8,128)(2,1)S(1)}, bf16[4,128,128]{2,1,0:T(8,128)(2,1)}, u32[]{:S(2)}) %copy-start.1) | copy-done | bytes 131096
  3.1 1.2 %copy-done.3 = f32[1,2048,128]{2,1,0:T(8,128)S(1)} copy-done((f32[1,2048,128]{2,1,0:T(8,128)S(1)}, f32[1,2048,128]{2,1,0:T(8,128)}, u32[]{:S(2)}) %copy-start.3) | copy-done | bytes 1048600
  4.4 0.9 %copy-done.4 = s32[16,2,16,8]{2,3,1,0:T(8,128)S(1)} copy-done((s32[16,2,16,8]{2,3,1,0:T(8,128)S(1)}, s32[16,2,16,8]{2,3,1,0:T(8,128)}, u32[]{:S(2)}) %copy-start.4) | copy-done | bytes 16408
  5.3 0.9 %copy-done.6 = bf16[1,2,256,128]{3,2,1,0:T(8,128)(2,1)S(1)} copy-done((bf16[1,2,256,128]{3,2,1,0:T(8,128)(2,1)S(1)}, bf16[1,2,256,128]{3,2,1,0:T(8,128)(2,1)}, u32[]{:S(2)}) %copy-start.6) | copy-done | bytes 131096
  6.2 6.5 %forward.1 = (f32[64,128]{1,0:T(8,128)S(1)}, f32[64,128]{1,0:T(8,128)S(1)}, f32[64,128]{1,0:T(8,128)S(1)}, f32[64,128]{1,0:T(8,128)S(1)}, f32[2056,128]{1,0:T(8,128)S(1)}) custom-call(s32[16,2,8,16]{3,2,1,0:T(8,128)S(1)} %bitcast.11, bf16[2,256,2048]{2,1,0:T(8,128)(2,1)S(1)} %bitcast.9, bf16[2,256,128]{2,1,0:T(8,128)(2,1)S(1)} %bitcast.13, ...), custom_call_target="tpu_custom_call" | custom-call | tf_op jit(solution)/shard_map/forward/pallas_call | solution.py:145
  12.7 3.0 %collective-permute-start = (f32[64,128]{1,0:T(8,128)S(1)}, f32[64,128]{1,0:T(8,128)S(1)}, u32[]{:S(2)}, u32[]{:S(2)}) collective-permute-start(f32[64,128]{1,0:T(8,128)S(1)} %get-tuple-element.8), channel_id=1, source_target_pairs={{0,2},{2,0},{4,6},{6,4},{8,10},{10,8},{12,14},{14,12},{16,18},{18,... | collective-permute-start | bytes 98312 | tf_op jit(solution)/shard_map/ppermute | solution.py:267
  15.7 1.5 %collective-permute-start.1 = (f32[64,128]{1,0:T(8,128)S(1)}, f32[64,128]{1,0:T(8,128)S(1)}, u32[]{:S(2)}, u32[]{:S(2)}) collective-permute-start(f32[64,128]{1,0:T(8,128)S(1)} %get-tuple-element.9), channel_id=1, source_target_pairs={{0,4},{2,6},{4,0},{6,2},{8,12},{10,14},{12,8},{14,10},{16,20},{18,... | collective-permute-start | bytes 98312 | tf_op jit(solution)/shard_map/ppermute | solution.py:267
  17.2 0.0 collective-permute-start.2
  17.3 0.3 collective-permute-done
  17.6 2.0 %collective-permute-done.1 = f32[64,128]{1,0:T(8,128)S(1)} collective-permute-done((f32[64,128]{1,0:T(8,128)S(1)}, f32[64,128]{1,0:T(8,128)S(1)}, u32[]{:S(2)}, u32[]{:S(2)}) %collective-permute-start.1) | collective-permute-done | bytes 32800 | tf_op jit(solution)/shard_map/ppermute | solution.py:267
  19.6 2.4 %collective-permute-done.2 = f32[64,128]{1,0:T(8,128)S(1)} collective-permute-done((f32[64,128]{1,0:T(8,128)S(1)}, f32[64,128]{1,0:T(8,128)S(1)}, u32[]{:S(2)}, u32[]{:S(2)}) %collective-permute-start.2) | collective-permute-done | bytes 32800 | tf_op jit(solution)/shard_map/ppermute | solution.py:267
  22.1 3.6 %collective-permute-start.5 = (f32[256,128]{1,0:T(8,128)S(1)}, f32[256,128]{1,0:T(8,128)S(1)}, u32[]{:S(2)}, u32[]{:S(2)}) collective-permute-start(f32[256,128]{1,0:T(8,128)S(1)} %constant_dynamic-update-slice_fusion.refs_0_), channel_id=1, source_target_pairs={{0,24},{2,26},{4,28},{6,30},{8,16},{10,18},{12,20},{14,22},{16,8},... | collective-permute-start | bytes 393224 | tf_op jit(solution)/shard_map/ppermute | solution.py:267
  25.7 0.0 collective-permute-start.4
  25.7 0.8 %collective-permute-start.3 = (f32[256,128]{1,0:T(8,128)S(1)}, f32[256,128]{1,0:T(8,128)S(1)}, u32[]{:S(2)}, u32[]{:S(2)}) collective-permute-start(f32[256,128]{1,0:T(8,128)S(1)} %constant_dynamic-update-slice_fusion.refs_0_), channel_id=1, source_target_pairs={{0,8},{2,10},{4,12},{6,14},{8,0},{10,2},{12,4},{14,6},{16,24},{18,... | collective-permute-start | bytes 393224 | tf_op jit(solution)/shard_map/ppermute | solution.py:267
  26.5 0.0 copy-done.5
  26.5 0.1 constant_dynamic-slice_fusion
  26.6 0.1 copy.9.listed
  26.6 3.0 %collective-permute-done.5.refs_3_ = f32[256,128]{1,0:T(8,128)S(1)} collective-permute-done((f32[256,128]{1,0:T(8,128)S(1)}, f32[256,128]{1,0:T(8,128)S(1)}, u32[]{:S(2)}, u32[]{:S(2)}) %collective-permute-start.5) | collective-permute-done | bytes 131104 | tf_op jit(solution)/shard_map/ppermute | solution.py:267
  29.6 5.4 %collective-permute-done.4.refs_2_ = f32[256,128]{1,0:T(8,128)S(1)} collective-permute-done((f32[256,128]{1,0:T(8,128)S(1)}, f32[256,128]{1,0:T(8,128)S(1)}, u32[]{:S(2)}, u32[]{:S(2)}) %collective-permute-start.4) | collective-permute-done | bytes 131104 | tf_op jit(solution)/shard_map/ppermute | solution.py:267
  35.0 0.0 collective-permute-done.3.refs_1_
  35.0 0.0 copy-done.2
  35.0 0.8 %class_rows.1.refs_0_ = f32[512,128]{1,0:T(8,128)S(1)} custom-call(s32[4,256]{1,0:T(4,128)S(1)} %copy.9.listed, bf16[4,128,128]{2,1,0:T(8,128)(2,1)S(1)} %copy-done.2, f32[256,128]{1,0:T(8,128)S(1)} %constant_dynamic-update-slice_fusion.refs_0_, f32[256,128]{1,0:T(8,128)S(1)} %collective-permute-done.3.refs_1_, ...), custom_call_target="tpu_custom_call" | custom-call | tf_op jit(solution)/shard_map/class_rows/pallas_call | solution.py:215
  35.9 0.6 %collective-permute-start.8 = (f32[512,128]{1,0:T(8,128)S(1)}, f32[512,128]{1,0:T(8,128)S(1)}, u32[]{:S(2)}, u32[]{:S(2)}) collective-permute-start(f32[512,128]{1,0:T(8,128)S(1)} %class_rows.1.refs_0_), channel_id=1, source_target_pairs={{0,6},{2,4},{4,2},{6,0},{8,14},{10,12},{12,10},{14,8},{16,22},{18,... | collective-permute-start | bytes 786440 | tf_op jit(solution)/shard_map/ppermute | solution.py:267
  36.5 1.5 %collective-permute-start.7 = (f32[512,128]{1,0:T(8,128)S(1)}, f32[512,128]{1,0:T(8,128)S(1)}, u32[]{:S(2)}, u32[]{:S(2)}) collective-permute-start(f32[512,128]{1,0:T(8,128)S(1)} %class_rows.1.refs_0_), channel_id=1, source_target_pairs={{0,4},{2,6},{4,0},{6,2},{8,12},{10,14},{12,8},{14,10},{16,20},{18,... | collective-permute-start | bytes 786440 | tf_op jit(solution)/shard_map/ppermute | solution.py:267
  38.0 1.4 %collective-permute-start.6 = (f32[512,128]{1,0:T(8,128)S(1)}, f32[512,128]{1,0:T(8,128)S(1)}, u32[]{:S(2)}, u32[]{:S(2)}) collective-permute-start(f32[512,128]{1,0:T(8,128)S(1)} %class_rows.1.refs_0_), channel_id=1, source_target_pairs={{0,2},{2,0},{4,6},{6,4},{8,10},{10,8},{12,14},{14,12},{16,18},{18,... | collective-permute-start | bytes 786440 | tf_op jit(solution)/shard_map/ppermute | solution.py:267
  39.4 3.0 %inverse.1 = f32[2048,128]{1,0:T(8,128)} custom-call(f32[2056,128]{1,0:T(8,128)S(1)} %get-tuple-element.11.coeffs, bf16[4,128,128]{2,1,0:T(8,128)(2,1)S(1)} %copy-done.2), custom_call_target="tpu_custom_call" | custom-call | tf_op jit(solution)/shard_map/inverse/pallas_call | solution.py:179
  42.4 3.6 %collective-permute-done.8.refs_3_ = f32[512,128]{1,0:T(8,128)S(1)} collective-permute-done((f32[512,128]{1,0:T(8,128)S(1)}, f32[512,128]{1,0:T(8,128)S(1)}, u32[]{:S(2)}, u32[]{:S(2)}) %collective-permute-start.8) | collective-permute-done | bytes 262176 | tf_op jit(solution)/shard_map/ppermute | solution.py:267
  46.0 3.2 %collective-permute-done.7.refs_2_ = f32[512,128]{1,0:T(8,128)S(1)} collective-permute-done((f32[512,128]{1,0:T(8,128)S(1)}, f32[512,128]{1,0:T(8,128)S(1)}, u32[]{:S(2)}, u32[]{:S(2)}) %collective-permute-start.7) | collective-permute-done | bytes 262176 | tf_op jit(solution)/shard_map/ppermute | solution.py:267
  49.2 0.0 collective-permute-done.6.refs_1_
  49.2 0.8 %finish.1 = bf16[4,512,128]{2,1,0:T(8,128)(2,1)} custom-call(f32[512,128]{1,0:T(8,128)S(1)} %class_rows.1.refs_0_, f32[512,128]{1,0:T(8,128)S(1)} %collective-permute-done.6.refs_1_, f32[512,128]{1,0:T(8,128)S(1)} %collective-permute-done.7.refs_2_, f32[512,128]{1,0:T(8,128)S(1)} %collective-permute-done.8.refs_3_), custom_call_target="tpu_custom_call" | custom-call | tf_op jit(solution)/shard_map/finish/pallas_call | solution.py:245
  (10 shorter events, 0.0 us)
Async XLA Ops:
  0.6 1.6 %copy-start = (bf16[1,2,256,2048]{3,2,1,0:T(8,128)(2,1)S(1)}, bf16[1,2,256,2048]{3,2,1,0:T(8,128)(2,1)}, u32[]{:S(2)}) copy-start(bf16[1,2,256,2048]{3,2,1,0:T(8,128)(2,1)} %param.5) | copy-start | bytes 6291460
  2.2 0.9 %copy-start.1 = (bf16[4,128,128]{2,1,0:T(8,128)(2,1)S(1)}, bf16[4,128,128]{2,1,0:T(8,128)(2,1)}, u32[]{:S(2)}) copy-start(bf16[4,128,128]{2,1,0:T(8,128)(2,1)} %constant.24.clone.dct) | copy-start | bytes 393220
  3.1 1.2 %copy-start.3 = (f32[1,2048,128]{2,1,0:T(8,128)S(1)}, f32[1,2048,128]{2,1,0:T(8,128)}, u32[]{:S(2)}) copy-start(f32[1,2048,128]{2,1,0:T(8,128)} %param.7) | copy-start | bytes 3145732
  4.4 0.9 %copy-start.4 = (s32[16,2,16,8]{2,3,1,0:T(8,128)S(1)}, s32[16,2,16,8]{2,3,1,0:T(8,128)}, u32[]{:S(2)}) copy-start(s32[16,2,16,8]{2,3,1,0:T(8,128)} %param.8) | copy-start | bytes 49156
  5.3 0.9 %copy-start.6 = (bf16[1,2,256,128]{3,2,1,0:T(8,128)(2,1)S(1)}, bf16[1,2,256,128]{3,2,1,0:T(8,128)(2,1)}, u32[]{:S(2)}) copy-start(bf16[1,2,256,128]{3,2,1,0:T(8,128)(2,1)} %param.6) | copy-start | bytes 393220
  6.2 20.3 %copy-start.5 = (s32[16,2,16,8]{2,3,1,0:T(8,128)S(1)}, s32[16,2,16,8]{2,3,1,0:T(8,128)}, u32[]{:S(2)}) copy-start(s32[16,2,16,8]{2,3,1,0:T(8,128)} %param.8) | copy-start | bytes 49156
  6.2 28.9 %copy-start.2 = (bf16[4,128,128]{2,1,0:T(8,128)(2,1)S(1)}, bf16[4,128,128]{2,1,0:T(8,128)(2,1)}, u32[]{:S(2)}) copy-start(bf16[4,128,128]{2,1,0:T(8,128)(2,1)} %constant.24.clone.dct) | copy-start | bytes 393220
  12.7 4.9 %collective-permute-start = (f32[64,128]{1,0:T(8,128)S(1)}, f32[64,128]{1,0:T(8,128)S(1)}, u32[]{:S(2)}, u32[]{:S(2)}) collective-permute-start(f32[64,128]{1,0:T(8,128)S(1)} %get-tuple-element.8), channel_id=1, source_target_pairs={{0,2},{2,0},{4,6},{6,4},{8,10},{10,8},{12,14},{14,12},{16,18},{18,... | collective-permute-start | bytes 98312 | tf_op jit(solution)/shard_map/ppermute | solution.py:267
  15.7 3.9 %collective-permute-start.1 = (f32[64,128]{1,0:T(8,128)S(1)}, f32[64,128]{1,0:T(8,128)S(1)}, u32[]{:S(2)}, u32[]{:S(2)}) collective-permute-start(f32[64,128]{1,0:T(8,128)S(1)} %get-tuple-element.9), channel_id=1, source_target_pairs={{0,4},{2,6},{4,0},{6,2},{8,12},{10,14},{12,8},{14,10},{16,20},{18,... | collective-permute-start | bytes 98312 | tf_op jit(solution)/shard_map/ppermute | solution.py:267
  17.2 4.8 %collective-permute-start.2 = (f32[64,128]{1,0:T(8,128)S(1)}, f32[64,128]{1,0:T(8,128)S(1)}, u32[]{:S(2)}, u32[]{:S(2)}) collective-permute-start(f32[64,128]{1,0:T(8,128)S(1)} %get-tuple-element.10), channel_id=1, source_target_pairs={{0,6},{2,4},{4,2},{6,0},{8,14},{10,12},{12,10},{14,8},{16,22},{18,... | collective-permute-start | bytes 98312 | tf_op jit(solution)/shard_map/ppermute | solution.py:267
  22.1 7.6 %collective-permute-start.5 = (f32[256,128]{1,0:T(8,128)S(1)}, f32[256,128]{1,0:T(8,128)S(1)}, u32[]{:S(2)}, u32[]{:S(2)}) collective-permute-start(f32[256,128]{1,0:T(8,128)S(1)} %constant_dynamic-update-slice_fusion.refs_0_), channel_id=1, source_target_pairs={{0,24},{2,26},{4,28},{6,30},{8,16},{10,18},{12,20},{14,22},{16,8},... | collective-permute-start | bytes 393224 | tf_op jit(solution)/shard_map/ppermute | solution.py:267
  25.7 9.4 %collective-permute-start.4 = (f32[256,128]{1,0:T(8,128)S(1)}, f32[256,128]{1,0:T(8,128)S(1)}, u32[]{:S(2)}, u32[]{:S(2)}) collective-permute-start(f32[256,128]{1,0:T(8,128)S(1)} %constant_dynamic-update-slice_fusion.refs_0_), channel_id=1, source_target_pairs={{0,16},{2,18},{4,20},{6,22},{8,24},{10,26},{12,28},{14,30},{16,0},... | collective-permute-start | bytes 393224 | tf_op jit(solution)/shard_map/ppermute | solution.py:267
  25.7 9.4 %collective-permute-start.3 = (f32[256,128]{1,0:T(8,128)S(1)}, f32[256,128]{1,0:T(8,128)S(1)}, u32[]{:S(2)}, u32[]{:S(2)}) collective-permute-start(f32[256,128]{1,0:T(8,128)S(1)} %constant_dynamic-update-slice_fusion.refs_0_), channel_id=1, source_target_pairs={{0,8},{2,10},{4,12},{6,14},{8,0},{10,2},{12,4},{14,6},{16,24},{18,... | collective-permute-start | bytes 393224 | tf_op jit(solution)/shard_map/ppermute | solution.py:267
  35.9 10.1 %collective-permute-start.8 = (f32[512,128]{1,0:T(8,128)S(1)}, f32[512,128]{1,0:T(8,128)S(1)}, u32[]{:S(2)}, u32[]{:S(2)}) collective-permute-start(f32[512,128]{1,0:T(8,128)S(1)} %class_rows.1.refs_0_), channel_id=1, source_target_pairs={{0,6},{2,4},{4,2},{6,0},{8,14},{10,12},{12,10},{14,8},{16,22},{18,... | collective-permute-start | bytes 786440 | tf_op jit(solution)/shard_map/ppermute | solution.py:267
  36.5 12.7 %collective-permute-start.7 = (f32[512,128]{1,0:T(8,128)S(1)}, f32[512,128]{1,0:T(8,128)S(1)}, u32[]{:S(2)}, u32[]{:S(2)}) collective-permute-start(f32[512,128]{1,0:T(8,128)S(1)} %class_rows.1.refs_0_), channel_id=1, source_target_pairs={{0,4},{2,6},{4,0},{6,2},{8,12},{10,14},{12,8},{14,10},{16,20},{18,... | collective-permute-start | bytes 786440 | tf_op jit(solution)/shard_map/ppermute | solution.py:267
  38.0 11.2 %collective-permute-start.6 = (f32[512,128]{1,0:T(8,128)S(1)}, f32[512,128]{1,0:T(8,128)S(1)}, u32[]{:S(2)}, u32[]{:S(2)}) collective-permute-start(f32[512,128]{1,0:T(8,128)S(1)} %class_rows.1.refs_0_), channel_id=1, source_target_pairs={{0,2},{2,0},{4,6},{6,4},{8,10},{10,8},{12,14},{14,12},{16,18},{18,... | collective-permute-start | bytes 786440 | tf_op jit(solution)/shard_map/ppermute | solution.py:267

commit v3 on v2

--- a/solution.py
+++ b/solution.py
@@ -9,7 +9,7 @@
 from jax.sharding import PartitionSpec as P
 
 GROUP = 64
-CHUNKS = 4
+CHUNKS = 2
 F32 = jnp.float32
 BF16 = jnp.bfloat16
 IN_VMEM = pl.BlockSpec(memory_space=pltpu.VMEM)
@@ -32,6 +32,10 @@
     return pltpu.with_memory_space_constraint(value, pltpu.VMEM)
 
 
+def hbm(value):
+    return pltpu.with_memory_space_constraint(value, pltpu.HBM)
+
+
 def left_table(high, low):
     return jnp.concatenate(
         [jnp.concatenate([high, high], 1), jnp.concatenate([low, low], 1)], 0
@@ -53,8 +57,8 @@
     return jnp.dot(a, b, preferred_element_type=F32)
 
 
-def mm_t(a, b):
-    return lax.dot_general(a, b, (((0,), (0,)), ((), ())), preferred_element_type=F32)
+def mm_nt(a, b):
+    return lax.dot_general(a, b, (((1,), (1,)), ((), ())), preferred_element_type=F32)
 
 
 def add_columns(both):
@@ -62,73 +66,105 @@
     return both[:, :half] + both[:, half:]
 
 
+def add_rows(both):
+    half = both.shape[0] // 2
+    return both[:half] + both[half:]
+
+
 def right(value, table):
     return add_columns(mm(split(value, 1), table))
 
 
 def left(table, value):
-    both = mm(table, split(value, 0))
-    half = both.shape[0] // 2
-    return both[:half] + both[half:]
-
-
-def forward_kernel(
-    inner, select, x_hbm, g, m_hbm, dct, *refs
-):
+    return add_rows(mm(table, split(value, 0)))
+
+
+def forward_kernel(inner, select, x_hbm, g_hbm, m_hbm, dct_hbm, *refs):
     picks, rest = refs[:inner], refs[inner]
-    x, m, c1, f2, listed, index_v, index, sems, sel_sem = refs[inner + 1 :]
+    x, m, c1, f2, y, g, dct, listed, index_v, index, sems, small = refs[inner + 1 :]
     me = lax.axis_index("dp")
     rows, cols = m.shape
     steps, slots, owners = index.shape
     per_class = owners // inner
     mine = me % inner
-    fetch = pltpu.make_async_copy(select.at[me], listed, sel_sem)
-    fetch.start()
     width = rows // CHUNKS
-    copies = []
+
+    def begin(source, target, sem):
+        copy = pltpu.make_async_copy(source, target, sem)
+        copy.start()
+        return copy
+
+    fetch_dct = begin(dct_hbm, dct, small.at[0])
+    fetch_g = begin(g_hbm, g, small.at[1])
+    fetch_select = begin(select.at[me], listed, small.at[2])
     for c in range(CHUNKS):
         span = pl.ds(c * width, width)
-        a = pltpu.make_async_copy(x_hbm.at[:, :, span], x.at[:, :, span], sems.at[c, 0])
-        b = pltpu.make_async_copy(m_hbm.at[span], m.at[span], sems.at[c, 1])
-        a.start()
-        b.start()
-        copies.append((a, b))
+        begin(m_hbm.at[span], m.at[span], sems.at[c, 0])
+        begin(x_hbm.at[:, :, span], x.at[:, :, span], sems.at[c, 1])
     c1[pl.ds(rows, 8), :] = jnp.zeros((8, cols), F32)
     rest[pl.ds(rows, 8), :] = jnp.zeros((8, cols), F32)
-    table = right_table(dct[2], dct[3])
-    row_table = left_table(dct[0], dct[1])
-    second = split(add_columns(mm(g[1], table[:cols])), 1)
-    first = g[0]
-    fetch.wait()
+    fetch_dct.wait()
+    table = left_table(dct[0], dct[1])
+    fetch_g.wait()
+    gradients = [split(add_rows(mm_nt(table[:, :cols], g[s])), 0) for s in range(steps)]
+    fetch_select.wait()
     owner = lax.broadcasted_iota(jnp.int32, listed.shape, 2)
     index_v[...] = jnp.where(listed[...] >= 0, listed[...] + owner * (rows // owners), rows)
-    store = pltpu.make_async_copy(index_v, index, sel_sem)
-    store.start()
+    store = begin(index_v, index, small.at[2])
+    def arrive(c):
+        span = pl.ds(c * width, width)
+        pltpu.make_async_copy(m_hbm.at[span], m.at[span], sems.at[c, 0]).wait()
+        pltpu.make_async_copy(x_hbm.at[:, :, span], x.at[:, :, span], sems.at[c, 1]).wait()
+
+    def columns(c):
+        span = pl.ds(c * width, width)
+        y1 = 0.999 * add_rows(mm_nt(table, split(m[span, :], 1)))
+        y1 = y1 + add_rows(mm(gradients[0], x[0, :, span]))
+        y2 = add_rows(mm(gradients[1], x[1, :, span]))
+        y[c % 2] = jnp.concatenate([y1, y2], axis=0)
+
+    def transform(c):
+        for t in range(0, width, cols):
+            z = add_rows(mm_nt(table, split(y[c % 2, :, t : t + cols], 1)))
+            span = pl.ds(c * width + t, cols)
+            c1[span, :] = z[:, :cols]
+            f2[span, :] = z[:, cols:]
+
     for c in range(CHUNKS):
-        copies[c][0].wait()
-        copies[c][1].wait()
-        for r in range(c * width, (c + 1) * width, cols):
-            m1 = 0.999 * m[r : r + cols] + mm_t(x[0, :, r : r + cols], first)
-            y1 = right(m1, table)
-            y2 = add_columns(mm_t(x[1, :, r : r + cols], second))
-            z = left(row_table, jnp.concatenate([y1, y2], axis=1))
-            c1[r : r + cols] = z[:, :cols]
-            f2[r : r + cols] = z[:, cols:]
+        arrive(c)
+        if c > 0:
+            transform(c - 1)
+        columns(c)
+    transform(CHUNKS - 1)
     store.wait()
     zero = jnp.zeros((1, cols), F32)
 
     def gather(step, source):
         for j in range(inner):
-            base = (mine ^ j) * per_class
-            for k in range(per_class):
+
+            def one(k, _, j=j):
+                base = (mine ^ j) * per_class
                 for c in range(slots):
                     place = (k * steps + step) * slots + c
                     picks[j][pl.ds(place, 1), :] = source[pl.ds(index[step, c, base + k], 1), :]
+                return 0
+
+            for k in range(per_class):
+                one(k, 0)
 
     def clear(step, target):
-        for k in range(owners):
+        def one(k, _):
             for c in range(slots):
                 target[pl.ds(index[step, c, k], 1), :] = zero
+            return 0
+
+        for k in range(owners):
+            one(k, 0)
+
+    def second_step(c, _):
+        span = pl.ds(pl.multiple_of(c * cols, cols), cols)
+        rest[span, :] = 0.999 * c1[span, :] + f2[span, :]
+        return 0
 
     gather(0, c1)
     clear(0, c1)
@@ -145,33 +181,47 @@
     return pl.pallas_call(
         functools.partial(forward_kernel, inner),
         out_shape=[block] * inner + [pltpu.VMEM((rows + 8, cols), F32)],
-        in_specs=[IN_HBM, IN_HBM, IN_VMEM, IN_HBM, IN_VMEM],
+        in_specs=[IN_HBM] * 5,
         out_specs=[IN_VMEM] * (inner + 1),
         scratch_shapes=[
             pltpu.VMEM(x.shape, x.dtype),
             pltpu.VMEM((rows, cols), F32),
             pltpu.VMEM((rows + 8, cols), F32),
             pltpu.VMEM((rows, cols), F32),
+            pltpu.VMEM((2, steps * cols, rows // CHUNKS), F32),
+            pltpu.VMEM(g.shape, g.dtype),
+            pltpu.VMEM(dct.shape, dct.dtype),
             pltpu.VMEM(select.shape[1:], jnp.int32),
             pltpu.VMEM(select.shape[1:], jnp.int32),
             pltpu.SMEM(select.shape[1:], jnp.int32),
             pltpu.SemaphoreType.DMA((CHUNKS, 2)),
-            pltpu.SemaphoreType.DMA,
+            pltpu.SemaphoreType.DMA((3,)),
         ],
         compiler_params=PARAMS,
         name="forward",
-    )(select, x, g, m, dct)
+    )(hbm(select), hbm(x), hbm(g), hbm(m), hbm(dct))
 
 
 def inverse_tile(value, row_table, col_table):
     return left(row_table, right(value, col_table))
+
+
+def invert(source, target, row_table, table):
+    rows, cols = target.shape
+
+    def pair(c, _):
+        for t in range(2):
+            span = pl.ds(pl.multiple_of((2 * c + t) * cols, cols), cols)
+            target[span, :] = inverse_tile(source[span, :], row_table, table)
+        return 0
+
+    lax.fori_loop(0, rows // (2 * cols), pair, 0)
 
 
 def inverse_kernel(coeffs, dct, out):
     row_table, table = left_table(dct[2], dct[3]), right_table(dct[0], dct[1])
     rows, cols = out.shape
-    for r in range(0, rows, cols):
-        out[r : r + cols] = inverse_tile(coeffs[r : r + cols], row_table, table)
+    invert(coeffs, out, row_table, table)
 
 
 def inverse(coeffs, dct, rows):
@@ -187,7 +237,7 @@
 
 
 def class_kernel(inner, listed, dct, *refs):
-    blocks, out, ordered, total = refs[:-3], refs[-3], refs[-2], refs[-1]
+    blocks, out, ordered, total = refs[-4::-1], refs[-3], refs[-2], refs[-1]
     me = lax.axis_index("dp")
     rows, cols = out.shape
     per_class, slots = listed.shape
@@ -205,8 +255,7 @@
         onehot = jnp.where(ids == listed[pl.ds(o, 1), :], 1.0, 0.0).astype(BF16)
         total[pl.ds(o * per_owner, per_owner), :] = add_columns(mm(onehot, ordered[o]))
     row_table, table = left_table(dct[2], dct[3]), right_table(dct[0], dct[1])
-    for r in range(0, rows, cols):
-        out[r : r + cols] = inverse_tile(total[r : r + cols], row_table, table)
+    invert(total, out, row_table, table)
 
 
 def class_rows(listed, blocks, dct, inner, rows):
@@ -223,12 +272,11 @@
         ],
         compiler_params=PARAMS,
         name="class_rows",
-    )(listed, dct, *[vmem(b) for b in blocks])
+    )(listed, dct, *[vmem(b) for b in reversed(blocks)])
 
 
 def finish_kernel(*refs):
-    count = len(refs) // 2
-    blocks, out, held, sems = refs[:-3], refs[-3], refs[-2], refs[-1]
+    blocks, out, held, sems = refs[-4::-1], refs[-3], refs[-2], refs[-1]
     me = lax.axis_index("dp")
     copies = []
     for j, block in enumerate(blocks):
@@ -250,7 +298,7 @@
         scratch_shapes=[pltpu.VMEM(shape, BF16), pltpu.SemaphoreType.DMA((len(blocks),))],
         compiler_params=PARAMS,
         name="finish",
-    )(*[vmem(b) for b in blocks])
+    )(*[vmem(b) for b in reversed(blocks)])
 
 
 def per_device(inputs, grad_out, momentum, select):
@@ -266,18 +314,21 @@
     def from_peer(value, shift):
         return lax.ppermute(value, "dp", [(d, d ^ shift) for d in range(owners)])
 
+    def from_peers(values, stride):
+        return [values[0]] + [
+            from_peer(values[j], j * stride) for j in range(1, len(values))
+        ]
+
     *picks, rest = forward(
         jnp.swapaxes(select, 2, 3), inputs[0], grad_out[0], momentum[0], dct, inner
     )
-    plane = jnp.concatenate(
-        [picks[0]] + [from_peer(picks[j], j) for j in range(1, inner)]
-    )
-    blocks = [plane] + [from_peer(plane, k * inner) for k in range(1, outer)]
+    plane = jnp.concatenate(from_peers(picks, 1))
+    blocks = from_peers([plane] * outer, inner)
     new_momentum = inverse(rest, dct, rows)
     listed = jnp.transpose(select, (2, 0, 1, 3)).reshape(owners, -1)
     listed = lax.dynamic_slice_in_dim(listed, replica % inner * outer, outer, 0)
     own = class_rows(listed, blocks, dct, inner, rows // inner)
-    update = finish([own] + [from_peer(own, j) for j in range(1, inner)])
+    update = finish(from_peers([own] * inner, 1))
     return (update.reshape(rows, cols), new_momentum[None])
 
 

time: 50.3 us -> 40.5 us (0.81)
  the two profiles are of different devices: /device:TPU:0 before, /device:TPU:8 now
where the time goes in v3:
time: 40.5 us; the launch traced here: 40.3 us
  waiting for transfers between devices  18.2 us (45%)
  Pallas kernels  10.6 us (26%)
  starting transfers between devices  10.6 us (26%)
  between operations  0.68 us (2%)
    ppermute x9, waiting for transfers between devices, from_peer(): return lax.ppermute(value, 'dp', [(d, d ^ shift) for d in range(owners)])  18.2 us
    ppermute x9, starting transfers between devices, from_peer(): return lax.ppermute(value, 'dp', [(d, d ^ shift) for d in range(owners)])  10.6 us
    pallas_call x1, Pallas kernels, inverse(): pl.pallas_call(inverse_kernel, out_shape=jax.ShapeDtypeStruct((rows, cols...  4.34 us
    pallas_call x1, Pallas kernels, forward(): pl.pallas_call(functools.partial(forward_kernel, inner), out_shape=[block...  4.29 us
    pallas_call x1, Pallas kernels, class_rows(): pl.pallas_call(functools.partial(class_kernel, inner), out_shape=pltpu.VM...  1.15 us
    pallas_call x1, Pallas kernels, finish(): pl.pallas_call(finish_kernel, out_shape=jax.ShapeDtypeStruct(shape, BF16)...  0.83 us
  transfers between devices with their start and end apart: 9, of which 8 were waited for; matrix products, arithmetic and copies ran while one was open for 0% of the time, Pallas kernels for 11%

profile of v3, /device:TPU:8, one launch (start us, length us, event | category | flops | bytes accessed | tf_op | source)
XLA Modules:
  0.0 40.3 jit_solution(5310261262327706305)
XLA Ops:
  0.6 0.0 copy-start.1
  0.6 0.0 copy-start
  0.7 4.3 %forward.1 = (f32[64,128]{1,0:T(8,128)S(1)}, f32[64,128]{1,0:T(8,128)S(1)}, f32[64,128]{1,0:T(8,128)S(1)}, f32[64,128]{1,0:T(8,128)S(1)}, f32[2056,128]{1,0:T(8,128)S(1)}) custom-call(s32[16,2,8,16]{3,2,1,0:T(8,128)} %bitcast.12, bf16[2,256,2048]{2,1,0:T(8,128)(2,1)} %bitcast.9, bf16[2,256,128]{2,1,0:T(8,128)(2,1)} %bitcast.15, f32[2048,128]{1,0:T(8,128)} %bitcast.10, ...), custom_call_target="tpu_custom_call" | custom-call | tf_op jit(solution)/shard_map/forward/pallas_call | solution.py:181
  5.0 1.6 %collective-permute-start = (f32[64,128]{1,0:T(8,128)S(1)}, f32[64,128]{1,0:T(8,128)S(1)}, u32[]{:S(2)}, u32[]{:S(2)}) collective-permute-start(f32[64,128]{1,0:T(8,128)S(1)} %get-tuple-element.8), channel_id=1, source_target_pairs={{0,2},{2,0},{4,6},{6,4},{8,10},{10,8},{12,14},{14,12},{16,18},{18,... | collective-permute-start | bytes 98312 | tf_op jit(solution)/shard_map/ppermute | solution.py:315
  6.5 1.5 %collective-permute-start.1 = (f32[64,128]{1,0:T(8,128)S(1)}, f32[64,128]{1,0:T(8,128)S(1)}, u32[]{:S(2)}, u32[]{:S(2)}) collective-permute-start(f32[64,128]{1,0:T(8,128)S(1)} %get-tuple-element.9), channel_id=1, source_target_pairs={{0,4},{2,6},{4,0},{6,2},{8,12},{10,14},{12,8},{14,10},{16,20},{18,... | collective-permute-start | bytes 98312 | tf_op jit(solution)/shard_map/ppermute | solution.py:315
  8.0 0.5 %collective-permute-start.2 = (f32[64,128]{1,0:T(8,128)S(1)}, f32[64,128]{1,0:T(8,128)S(1)}, u32[]{:S(2)}, u32[]{:S(2)}) collective-permute-start(f32[64,128]{1,0:T(8,128)S(1)} %get-tuple-element.10), channel_id=1, source_target_pairs={{0,6},{2,4},{4,2},{6,0},{8,14},{10,12},{12,10},{14,8},{16,22},{18,... | collective-permute-start | bytes 98312 | tf_op jit(solution)/shard_map/ppermute | solution.py:315
  8.5 0.4 %collective-permute-done = f32[64,128]{1,0:T(8,128)S(1)} collective-permute-done((f32[64,128]{1,0:T(8,128)S(1)}, f32[64,128]{1,0:T(8,128)S(1)}, u32[]{:S(2)}, u32[]{:S(2)}) %collective-permute-start) | collective-permute-done | bytes 32800 | tf_op jit(solution)/shard_map/ppermute | solution.py:315
  8.9 1.5 %collective-permute-done.1 = f32[64,128]{1,0:T(8,128)S(1)} collective-permute-done((f32[64,128]{1,0:T(8,128)S(1)}, f32[64,128]{1,0:T(8,128)S(1)}, u32[]{:S(2)}, u32[]{:S(2)}) %collective-permute-start.1) | collective-permute-done | bytes 32800 | tf_op jit(solution)/shard_map/ppermute | solution.py:315
  10.4 2.4 %collective-permute-done.2 = f32[64,128]{1,0:T(8,128)S(1)} collective-permute-done((f32[64,128]{1,0:T(8,128)S(1)}, f32[64,128]{1,0:T(8,128)S(1)}, u32[]{:S(2)}, u32[]{:S(2)}) %collective-permute-start.2) | collective-permute-done | bytes 32800 | tf_op jit(solution)/shard_map/ppermute | solution.py:315
  12.8 0.4 %collective-permute-start.5 = (f32[256,128]{1,0:T(8,128)S(1)}, f32[256,128]{1,0:T(8,128)S(1)}, u32[]{:S(2)}, u32[]{:S(2)}) collective-permute-start(f32[256,128]{1,0:T(8,128)S(1)} %constant_dynamic-update-slice_fusion.refs_3_), channel_id=1, source_target_pairs={{0,8},{2,10},{4,12},{6,14},{8,0},{10,2},{12,4},{14,6},{16,24},{18,... | collective-permute-start | bytes 393224 | tf_op jit(solution)/shard_map/ppermute | solution.py:315
  13.3 2.6 %collective-permute-start.4 = (f32[256,128]{1,0:T(8,128)S(1)}, f32[256,128]{1,0:T(8,128)S(1)}, u32[]{:S(2)}, u32[]{:S(2)}) collective-permute-start(f32[256,128]{1,0:T(8,128)S(1)} %constant_dynamic-update-slice_fusion.refs_3_), channel_id=1, source_target_pairs={{0,16},{2,18},{4,20},{6,22},{8,24},{10,26},{12,28},{14,30},{16,0},... | collective-permute-start | bytes 393224 | tf_op jit(solution)/shard_map/ppermute | solution.py:315
  15.9 0.4 %collective-permute-start.3 = (f32[256,128]{1,0:T(8,128)S(1)}, f32[256,128]{1,0:T(8,128)S(1)}, u32[]{:S(2)}, u32[]{:S(2)}) collective-permute-start(f32[256,128]{1,0:T(8,128)S(1)} %constant_dynamic-update-slice_fusion.refs_3_), channel_id=1, source_target_pairs={{0,24},{2,26},{4,28},{6,30},{8,16},{10,18},{12,20},{14,22},{16,8},... | collective-permute-start | bytes 393224 | tf_op jit(solution)/shard_map/ppermute | solution.py:315
  16.3 0.0 copy-done.1
  16.3 0.1 constant_dynamic-slice_fusion
  16.4 0.1 copy.9.listed
  16.5 2.7 %collective-permute-done.5.refs_2_ = f32[256,128]{1,0:T(8,128)S(1)} collective-permute-done((f32[256,128]{1,0:T(8,128)S(1)}, f32[256,128]{1,0:T(8,128)S(1)}, u32[]{:S(2)}, u32[]{:S(2)}) %collective-permute-start.5) | collective-permute-done | bytes 131104 | tf_op jit(solution)/shard_map/ppermute | solution.py:315
  19.2 4.5 %collective-permute-done.4.refs_1_ = f32[256,128]{1,0:T(8,128)S(1)} collective-permute-done((f32[256,128]{1,0:T(8,128)S(1)}, f32[256,128]{1,0:T(8,128)S(1)}, u32[]{:S(2)}, u32[]{:S(2)}) %collective-permute-start.4) | collective-permute-done | bytes 131104 | tf_op jit(solution)/shard_map/ppermute | solution.py:315
  23.7 2.3 %collective-permute-done.3.refs_0_ = f32[256,128]{1,0:T(8,128)S(1)} collective-permute-done((f32[256,128]{1,0:T(8,128)S(1)}, f32[256,128]{1,0:T(8,128)S(1)}, u32[]{:S(2)}, u32[]{:S(2)}) %collective-permute-start.3) | collective-permute-done | bytes 131104 | tf_op jit(solution)/shard_map/ppermute | solution.py:315
  26.0 0.0 copy-done
  26.0 1.1 %class_rows.1.refs_3_ = f32[512,128]{1,0:T(8,128)S(1)} custom-call(s32[4,256]{1,0:T(4,128)S(1)} %copy.9.listed, bf16[4,128,128]{2,1,0:T(8,128)(2,1)S(1)} %copy-done, f32[256,128]{1,0:T(8,128)S(1)} %collective-permute-done.3.refs_0_, f32[256,128]{1,0:T(8,128)S(1)} %collective-permute-done.4.refs_1_, f32[256,128]{1,0:T(8,128)S(1)} %collective-permute-done.5.refs_2_, ...), custom_call_target="tpu_custom_call" | custom-call | tf_op jit(solution)/shard_map/class_rows/pallas_call | solution.py:264
  27.1 0.6 %collective-permute-start.8 = (f32[512,128]{1,0:T(8,128)S(1)}, f32[512,128]{1,0:T(8,128)S(1)}, u32[]{:S(2)}, u32[]{:S(2)}) collective-permute-start(f32[512,128]{1,0:T(8,128)S(1)} %class_rows.1.refs_3_), channel_id=1, source_target_pairs={{0,2},{2,0},{4,6},{6,4},{8,10},{10,8},{12,14},{14,12},{16,18},{18,... | collective-permute-start | bytes 786440 | tf_op jit(solution)/shard_map/ppermute | solution.py:315
  27.8 0.5 %collective-permute-start.7 = (f32[512,128]{1,0:T(8,128)S(1)}, f32[512,128]{1,0:T(8,128)S(1)}, u32[]{:S(2)}, u32[]{:S(2)}) collective-permute-start(f32[512,128]{1,0:T(8,128)S(1)} %class_rows.1.refs_3_), channel_id=1, source_target_pairs={{0,4},{2,6},{4,0},{6,2},{8,12},{10,14},{12,8},{14,10},{16,20},{18,... | collective-permute-start | bytes 786440 | tf_op jit(solution)/shard_map/ppermute | solution.py:315
  28.3 2.4 %collective-permute-start.6 = (f32[512,128]{1,0:T(8,128)S(1)}, f32[512,128]{1,0:T(8,128)S(1)}, u32[]{:S(2)}, u32[]{:S(2)}) collective-permute-start(f32[512,128]{1,0:T(8,128)S(1)} %class_rows.1.refs_3_), channel_id=1, source_target_pairs={{0,6},{2,4},{4,2},{6,0},{8,14},{10,12},{12,10},{14,8},{16,22},{18,... | collective-permute-start | bytes 786440 | tf_op jit(solution)/shard_map/ppermute | solution.py:315
  30.7 4.3 %inverse.1 = f32[2048,128]{1,0:T(8,128)} custom-call(f32[2056,128]{1,0:T(8,128)S(1)} %get-tuple-element.11.coeffs, bf16[4,128,128]{2,1,0:T(8,128)(2,1)S(1)} %copy-done), custom_call_target="tpu_custom_call" | custom-call | tf_op jit(solution)/shard_map/inverse/pallas_call | solution.py:229
  35.0 1.3 %collective-permute-done.8.refs_2_ = f32[512,128]{1,0:T(8,128)S(1)} collective-permute-done((f32[512,128]{1,0:T(8,128)S(1)}, f32[512,128]{1,0:T(8,128)S(1)}, u32[]{:S(2)}, u32[]{:S(2)}) %collective-permute-start.8) | collective-permute-done | bytes 262176 | tf_op jit(solution)/shard_map/ppermute | solution.py:315
  36.3 3.1 %collective-permute-done.7.refs_1_ = f32[512,128]{1,0:T(8,128)S(1)} collective-permute-done((f32[512,128]{1,0:T(8,128)S(1)}, f32[512,128]{1,0:T(8,128)S(1)}, u32[]{:S(2)}, u32[]{:S(2)}) %collective-permute-start.7) | collective-permute-done | bytes 262176 | tf_op jit(solution)/shard_map/ppermute | solution.py:315
  39.5 0.0 collective-permute-done.6.refs_0_
  39.5 0.8 %finish.1 = bf16[4,512,128]{2,1,0:T(8,128)(2,1)} custom-call(f32[512,128]{1,0:T(8,128)S(1)} %collective-permute-done.6.refs_0_, f32[512,128]{1,0:T(8,128)S(1)} %collective-permute-done.7.refs_1_, f32[512,128]{1,0:T(8,128)S(1)} %collective-permute-done.8.refs_2_, f32[512,128]{1,0:T(8,128)S(1)} %class_rows.1.refs_3_), custom_call_target="tpu_custom_call" | custom-call | tf_op jit(solution)/shard_map/finish/pallas_call | solution.py:293
  (4 shorter events, 0.0 us)
Async XLA Ops:
  0.6 15.7 %copy-start.1 = (s32[16,2,16,8]{2,3,1,0:T(8,128)S(1)}, s32[16,2,16,8]{2,3,1,0:T(8,128)}, u32[]{:S(2)}) copy-start(s32[16,2,16,8]{2,3,1,0:T(8,128)} %param.8) | copy-start | bytes 49156
  0.6 25.3 %copy-start = (bf16[4,128,128]{2,1,0:T(8,128)(2,1)S(1)}, bf16[4,128,128]{2,1,0:T(8,128)(2,1)}, u32[]{:S(2)}) copy-start(bf16[4,128,128]{2,1,0:T(8,128)(2,1)} %constant.24.clone.dct_hbm.dct) | copy-start | bytes 393220
  5.0 4.0 %collective-permute-start = (f32[64,128]{1,0:T(8,128)S(1)}, f32[64,128]{1,0:T(8,128)S(1)}, u32[]{:S(2)}, u32[]{:S(2)}) collective-permute-start(f32[64,128]{1,0:T(8,128)S(1)} %get-tuple-element.8), channel_id=1, source_target_pairs={{0,2},{2,0},{4,6},{6,4},{8,10},{10,8},{12,14},{14,12},{16,18},{18,... | collective-permute-start | bytes 98312 | tf_op jit(solution)/shard_map/ppermute | solution.py:315
  6.5 3.9 %collective-permute-start.1 = (f32[64,128]{1,0:T(8,128)S(1)}, f32[64,128]{1,0:T(8,128)S(1)}, u32[]{:S(2)}, u32[]{:S(2)}) collective-permute-start(f32[64,128]{1,0:T(8,128)S(1)} %get-tuple-element.9), channel_id=1, source_target_pairs={{0,4},{2,6},{4,0},{6,2},{8,12},{10,14},{12,8},{14,10},{16,20},{18,... | collective-permute-start | bytes 98312 | tf_op jit(solution)/shard_map/ppermute | solution.py:315
  8.0 4.8 %collective-permute-start.2 = (f32[64,128]{1,0:T(8,128)S(1)}, f32[64,128]{1,0:T(8,128)S(1)}, u32[]{:S(2)}, u32[]{:S(2)}) collective-permute-start(f32[64,128]{1,0:T(8,128)S(1)} %get-tuple-element.10), channel_id=1, source_target_pairs={{0,6},{2,4},{4,2},{6,0},{8,14},{10,12},{12,10},{14,8},{16,22},{18,... | collective-permute-start | bytes 98312 | tf_op jit(solution)/shard_map/ppermute | solution.py:315
  12.8 6.4 %collective-permute-start.5 = (f32[256,128]{1,0:T(8,128)S(1)}, f32[256,128]{1,0:T(8,128)S(1)}, u32[]{:S(2)}, u32[]{:S(2)}) collective-permute-start(f32[256,128]{1,0:T(8,128)S(1)} %constant_dynamic-update-slice_fusion.refs_3_), channel_id=1, source_target_pairs={{0,8},{2,10},{4,12},{6,14},{8,0},{10,2},{12,4},{14,6},{16,24},{18,... | collective-permute-start | bytes 393224 | tf_op jit(solution)/shard_map/ppermute | solution.py:315
  13.3 10.4 %collective-permute-start.4 = (f32[256,128]{1,0:T(8,128)S(1)}, f32[256,128]{1,0:T(8,128)S(1)}, u32[]{:S(2)}, u32[]{:S(2)}) collective-permute-start(f32[256,128]{1,0:T(8,128)S(1)} %constant_dynamic-update-slice_fusion.refs_3_), channel_id=1, source_target_pairs={{0,16},{2,18},{4,20},{6,22},{8,24},{10,26},{12,28},{14,30},{16,0},... | collective-permute-start | bytes 393224 | tf_op jit(solution)/shard_map/ppermute | solution.py:315
  15.9 10.1 %collective-permute-start.3 = (f32[256,128]{1,0:T(8,128)S(1)}, f32[256,128]{1,0:T(8,128)S(1)}, u32[]{:S(2)}, u32[]{:S(2)}) collective-permute-start(f32[256,128]{1,0:T(8,128)S(1)} %constant_dynamic-update-slice_fusion.refs_3_), channel_id=1, source_target_pairs={{0,24},{2,26},{4,28},{6,30},{8,16},{10,18},{12,20},{14,22},{16,8},... | collective-permute-start | bytes 393224 | tf_op jit(solution)/shard_map/ppermute | solution.py:315
  27.1 9.2 %collective-permute-start.8 = (f32[512,128]{1,0:T(8,128)S(1)}, f32[512,128]{1,0:T(8,128)S(1)}, u32[]{:S(2)}, u32[]{:S(2)}) collective-permute-start(f32[512,128]{1,0:T(8,128)S(1)} %class_rows.1.refs_3_), channel_id=1, source_target_pairs={{0,2},{2,0},{4,6},{6,4},{8,10},{10,8},{12,14},{14,12},{16,18},{18,... | collective-permute-start | bytes 786440 | tf_op jit(solution)/shard_map/ppermute | solution.py:315
  27.8 11.7 %collective-permute-start.7 = (f32[512,128]{1,0:T(8,128)S(1)}, f32[512,128]{1,0:T(8,128)S(1)}, u32[]{:S(2)}, u32[]{:S(2)}) collective-permute-start(f32[512,128]{1,0:T(8,128)S(1)} %class_rows.1.refs_3_), channel_id=1, source_target_pairs={{0,4},{2,6},{4,0},{6,2},{8,12},{10,14},{12,8},{14,10},{16,20},{18,... | collective-permute-start | bytes 786440 | tf_op jit(solution)/shard_map/ppermute | solution.py:315
  28.3 11.2 %collective-permute-start.6 = (f32[512,128]{1,0:T(8,128)S(1)}, f32[512,128]{1,0:T(8,128)S(1)}, u32[]{:S(2)}, u32[]{:S(2)}) collective-permute-start(f32[512,128]{1,0:T(8,128)S(1)} %class_rows.1.refs_3_), channel_id=1, source_target_pairs={{0,6},{2,4},{4,2},{6,0},{8,14},{10,12},{12,10},{14,8},{16,22},{18,... | collective-permute-start | bytes 786440 | tf_op jit(solution)/shard_map/ppermute | solution.py:315

commit v4 on v3

--- a/solution.py
+++ b/solution.py
@@ -8,8 +8,10 @@
 from jax.experimental.pallas import tpu as pltpu
 from jax.sharding import PartitionSpec as P
 
+
 GROUP = 64
 CHUNKS = 2
+HALVES = 2
 F32 = jnp.float32
 BF16 = jnp.bfloat16
 IN_VMEM = pl.BlockSpec(memory_space=pltpu.VMEM)
@@ -111,6 +113,7 @@
     owner = lax.broadcasted_iota(jnp.int32, listed.shape, 2)
     index_v[...] = jnp.where(listed[...] >= 0, listed[...] + owner * (rows // owners), rows)
     store = begin(index_v, index, small.at[2])
+
     def arrive(c):
         span = pl.ds(c * width, width)
         pltpu.make_async_copy(m_hbm.at[span], m.at[span], sems.at[c, 0]).wait()
@@ -142,7 +145,7 @@
     def gather(step, source):
         for j in range(inner):
 
-            def one(k, _, j=j):
+            def one(k, j=j):
                 base = (mine ^ j) * per_class
                 for c in range(slots):
                     place = (k * steps + step) * slots + c
@@ -150,21 +153,16 @@
                 return 0
 
             for k in range(per_class):
-                one(k, 0)
+                one(k)
 
     def clear(step, target):
-        def one(k, _):
+        def one(k):
             for c in range(slots):
                 target[pl.ds(index[step, c, k], 1), :] = zero
             return 0
 
         for k in range(owners):
-            one(k, 0)
-
-    def second_step(c, _):
-        span = pl.ds(pl.multiple_of(c * cols, cols), cols)
-        rest[span, :] = 0.999 * c1[span, :] + f2[span, :]
-        return 0
+            one(k)
 
     gather(0, c1)
     clear(0, c1)
@@ -209,18 +207,18 @@
 def invert(source, target, row_table, table):
     rows, cols = target.shape
 
-    def pair(c, _):
+    def pair(c):
         for t in range(2):
-            span = pl.ds(pl.multiple_of((2 * c + t) * cols, cols), cols)
+            span = pl.ds((2 * c + t) * cols, cols)
             target[span, :] = inverse_tile(source[span, :], row_table, table)
         return 0
 
-    lax.fori_loop(0, rows // (2 * cols), pair, 0)
+    for c in range(rows // (2 * cols)):
+        pair(c)
 
 
 def inverse_kernel(coeffs, dct, out):
     row_table, table = left_table(dct[2], dct[3]), right_table(dct[0], dct[1])
-    rows, cols = out.shape
     invert(coeffs, out, row_table, table)
 
 
@@ -255,7 +253,8 @@
         onehot = jnp.where(ids == listed[pl.ds(o, 1), :], 1.0, 0.0).astype(BF16)
         total[pl.ds(o * per_owner, per_owner), :] = add_columns(mm(onehot, ordered[o]))
     row_table, table = left_table(dct[2], dct[3]), right_table(dct[0], dct[1])
-    invert(total, out, row_table, table)
+    for r in range(0, rows, cols):
+        out[r : r + cols] = inverse_tile(total[r : r + cols], row_table, table)
 
 
 def class_rows(listed, blocks, dct, inner, rows):
@@ -275,39 +274,51 @@
     )(listed, dct, *[vmem(b) for b in reversed(blocks)])
 
 
-def finish_kernel(*refs):
+def finish_kernel(halves, *refs):
     blocks, out, held, sems = refs[-4::-1], refs[-3], refs[-2], refs[-1]
     me = lax.axis_index("dp")
+    inner = len(blocks) // halves
     copies = []
-    for j, block in enumerate(blocks):
-        held[j] = block[...].astype(held.dtype)
-        copy = pltpu.make_async_copy(held.at[j], out.at[me % len(blocks) ^ j], sems.at[j])
-        copy.start()
-        copies.append(copy)
+    for h in range(halves):
+        for j in range(inner):
+            i = h * inner + j
+            held[i] = blocks[i][...].astype(held.dtype)
+            copy = pltpu.make_async_copy(held.at[i], out.at[me % inner ^ j, h], sems.at[i])
+            copy.start()
+            copies.append(copy)
     for copy in copies:
         copy.wait()
 
 
-def finish(blocks):
-    shape = (len(blocks),) + blocks[0].shape
+def finish(outs):
+    blocks = [b for half in outs for b in half]
+    shape = blocks[0].shape
     return pl.pallas_call(
-        finish_kernel,
-        out_shape=jax.ShapeDtypeStruct(shape, BF16),
+        functools.partial(finish_kernel, len(outs)),
+        out_shape=jax.ShapeDtypeStruct((len(outs[0]), len(outs)) + shape, BF16),
         in_specs=[IN_VMEM] * len(blocks),
         out_specs=IN_HBM,
-        scratch_shapes=[pltpu.VMEM(shape, BF16), pltpu.SemaphoreType.DMA((len(blocks),))],
+        scratch_shapes=[
+            pltpu.VMEM((len(blocks),) + shape, BF16),
+            pltpu.SemaphoreType.DMA((len(blocks),)),
+        ],
         compiler_params=PARAMS,
         name="finish",
     )(*[vmem(b) for b in reversed(blocks)])
+
+
+def inner_size(owners):
+    inner = 1
+    while inner * inner < owners:
+        inner *= 2
+    return inner
 
 
 def per_device(inputs, grad_out, momentum, select):
     replica = lax.axis_index("dp")
     owners = lax.axis_size("dp")
     rows, cols = momentum.shape[1:]
-    inner = 1
-    while inner * inner < owners:
-        inner *= 2
+    inner = inner_size(owners)
     outer = owners // inner
     dct = tables(cols)
 
@@ -315,20 +326,30 @@
         return lax.ppermute(value, "dp", [(d, d ^ shift) for d in range(owners)])
 
     def from_peers(values, stride):
-        return [values[0]] + [
-            from_peer(values[j], j * stride) for j in range(1, len(values))
-        ]
+        got = [values[0]]
+        for j in range(1, len(values)):
+            got.append(from_peer(values[j], j * stride))
+        return got
 
     *picks, rest = forward(
         jnp.swapaxes(select, 2, 3), inputs[0], grad_out[0], momentum[0], dct, inner
     )
-    plane = jnp.concatenate(from_peers(picks, 1))
-    blocks = from_peers([plane] * outer, inner)
-    new_momentum = inverse(rest, dct, rows)
     listed = jnp.transpose(select, (2, 0, 1, 3)).reshape(owners, -1)
     listed = lax.dynamic_slice_in_dim(listed, replica % inner * outer, outer, 0)
-    own = class_rows(listed, blocks, dct, inner, rows // inner)
-    update = finish(from_peers([own] * inner, 1))
+    peers = from_peers(picks, 1)
+    each = owners // inner // HALVES
+    lines, outs = [], []
+    for h in range(HALVES):
+        span = slice(h * picks[0].shape[0] // HALVES, (h + 1) * picks[0].shape[0] // HALVES)
+        plane = jnp.concatenate([p[span] for p in peers])
+        lines.append(from_peers([plane] * outer, inner))
+    for h in range(HALVES):
+        own = class_rows(
+            listed[h * each : (h + 1) * each], lines[h], dct, inner, rows // inner // HALVES
+        )
+        outs.append(from_peers([own] * inner, 1))
+    new_momentum = inverse(rest, dct, rows)
+    update = finish(outs)
     return (update.reshape(rows, cols), new_momentum[None])
 
 

time: 40.5 us -> 42.8 us (1.057)
  the two profiles are of different devices: /device:TPU:8 before, /device:TPU:0 now
where the time goes in v4:
time: 42.8 us; the launch traced here: 42.6 us
  starting transfers between devices  20.5 us (48%)
  waiting for transfers between devices  11.8 us (28%)
  Pallas kernels  9.3 us (22%)
  between operations  0.72 us (2%)
    ppermute x15, starting transfers between devices, from_peer(): return lax.ppermute(value, 'dp', [(d, d ^ shift) for d in range(owners)])  20.5 us
    ppermute x15, waiting for transfers between devices, from_peer(): return lax.ppermute(value, 'dp', [(d, d ^ shift) for d in range(owners)])  11.8 us
    pallas_call x1, Pallas kernels, forward(): pl.pallas_call(functools.partial(forward_kernel, inner), out_shape=[block...  4.3 us
    pallas_call x1, Pallas kernels, inverse(): pl.pallas_call(inverse_kernel, out_shape=jax.ShapeDtypeStruct((rows, cols...  2.98 us
    pallas_call x2, Pallas kernels, class_rows(): pl.pallas_call(functools.partial(class_kernel, inner), out_shape=pltpu.VM...  1.16 us
    pallas_call x1, Pallas kernels, finish(): pl.pallas_call(functools.partial(finish_kernel, len(outs)), out_shape=jax...  0.86 us
  transfers between devices with their start and end apart: 15, of which 6 were waited for; matrix products, arithmetic and copies ran while one was open for 1% of the time, Pallas kernels for 8%

profile of v4, /device:TPU:0, one launch (start us, length us, event | category | flops | bytes accessed | tf_op | source)
XLA Modules:
  0.0 42.6 jit_solution(9548920395712587673)
XLA Ops:
  0.6 0.0 copy-start
  0.7 4.3 %forward.1 = (f32[64,128]{1,0:T(8,128)S(1)}, f32[64,128]{1,0:T(8,128)S(1)}, f32[64,128]{1,0:T(8,128)S(1)}, f32[64,128]{1,0:T(8,128)S(1)}, f32[2056,128]{1,0:T(8,128)S(1)}) custom-call(s32[16,2,8,16]{3,2,1,0:T(8,128)} %bitcast.10, bf16[2,256,2048]{2,1,0:T(8,128)(2,1)} %bitcast.9, bf16[2,256,128]{2,1,0:T(8,128)(2,1)} %bitcast.15, f32[2048,128]{1,0:T(8,128)} %bitcast.12, ...), custom_call_target="tpu_custom_call" | custom-call | tf_op jit(solution)/shard_map/forward/pallas_call | solution.py:179
  5.0 3.0 %collective-permute-start = (f32[64,128]{1,0:T(8,128)S(1)}, f32[64,128]{1,0:T(8,128)S(1)}, u32[]{:S(2)}, u32[]{:S(2)}) collective-permute-start(f32[64,128]{1,0:T(8,128)S(1)} %get-tuple-element.8), channel_id=1, source_target_pairs={{0,2},{2,0},{4,6},{6,4},{8,10},{10,8},{12,14},{14,12},{16,18},{18,... | collective-permute-start | bytes 98312 | tf_op jit(solution)/shard_map/ppermute | solution.py:326
  8.0 1.5 %collective-permute-start.1 = (f32[64,128]{1,0:T(8,128)S(1)}, f32[64,128]{1,0:T(8,128)S(1)}, u32[]{:S(2)}, u32[]{:S(2)}) collective-permute-start(f32[64,128]{1,0:T(8,128)S(1)} %get-tuple-element.9), channel_id=1, source_target_pairs={{0,4},{2,6},{4,0},{6,2},{8,12},{10,14},{12,8},{14,10},{16,20},{18,... | collective-permute-start | bytes 98312 | tf_op jit(solution)/shard_map/ppermute | solution.py:326
  9.5 0.0 collective-permute-start.2
  9.5 0.3 collective-permute-done
  9.9 2.0 %collective-permute-done.1 = f32[64,128]{1,0:T(8,128)S(1)} collective-permute-done((f32[64,128]{1,0:T(8,128)S(1)}, f32[64,128]{1,0:T(8,128)S(1)}, u32[]{:S(2)}, u32[]{:S(2)}) %collective-permute-start.1) | collective-permute-done | bytes 32800 | tf_op jit(solution)/shard_map/ppermute | solution.py:326
  11.9 2.4 %collective-permute-done.2 = f32[64,128]{1,0:T(8,128)S(1)} collective-permute-done((f32[64,128]{1,0:T(8,128)S(1)}, f32[64,128]{1,0:T(8,128)S(1)}, u32[]{:S(2)}, u32[]{:S(2)}) %collective-permute-start.2) | collective-permute-done | bytes 32800 | tf_op jit(solution)/shard_map/ppermute | solution.py:326
  14.3 1.6 %collective-permute-start.11 = (f32[128,128]{1,0:T(8,128)S(1)}, f32[128,128]{1,0:T(8,128)S(1)}, u32[]{:S(2)}, u32[]{:S(2)}) collective-permute-start(f32[128,128]{1,0:T(8,128)S(1)} %pad_maximum_fusion.1.refs_3_), channel_id=1, source_target_pairs={{0,8},{2,10},{4,12},{6,14},{8,0},{10,2},{12,4},{14,6},{16,24},{18,... | collective-permute-start | bytes 196616 | tf_op jit(solution)/shard_map/ppermute | solution.py:326
  16.0 2.6 %collective-permute-start.10 = (f32[128,128]{1,0:T(8,128)S(1)}, f32[128,128]{1,0:T(8,128)S(1)}, u32[]{:S(2)}, u32[]{:S(2)}) collective-permute-start(f32[128,128]{1,0:T(8,128)S(1)} %pad_maximum_fusion.1.refs_3_), channel_id=1, source_target_pairs={{0,16},{2,18},{4,20},{6,22},{8,24},{10,26},{12,28},{14,30},{16,0},... | collective-permute-start | bytes 196616 | tf_op jit(solution)/shard_map/ppermute | solution.py:326
  18.6 0.2 collective-permute-start.9
  18.8 0.1 constant_dynamic-slice_fusion.1
  18.9 0.1 copy.11.listed
  19.0 0.0 collective-permute-done.11.refs_2_
  19.0 3.5 %collective-permute-done.10.refs_1_ = f32[128,128]{1,0:T(8,128)S(1)} collective-permute-done((f32[128,128]{1,0:T(8,128)S(1)}, f32[128,128]{1,0:T(8,128)S(1)}, u32[]{:S(2)}, u32[]{:S(2)}) %collective-permute-start.10) | collective-permute-done | bytes 65568 | tf_op jit(solution)/shard_map/ppermute | solution.py:326
  22.5 2.2 %collective-permute-done.9.refs_0_ = f32[128,128]{1,0:T(8,128)S(1)} collective-permute-done((f32[128,128]{1,0:T(8,128)S(1)}, f32[128,128]{1,0:T(8,128)S(1)}, u32[]{:S(2)}, u32[]{:S(2)}) %collective-permute-start.9) | collective-permute-done | bytes 65568 | tf_op jit(solution)/shard_map/ppermute | solution.py:326
  24.7 0.6 %class_rows.3.refs_7_ = f32[256,128]{1,0:T(8,128)S(1)} custom-call(s32[2,256]{1,0:T(2,128)S(1)} %copy.11.listed, bf16[4,128,128]{2,1,0:T(8,128)(2,1)S(1)} %copy-done, f32[128,128]{1,0:T(8,128)S(1)} %collective-permute-done.9.refs_0_, f32[128,128]{1,0:T(8,128)S(1)} %collective-permute-done.10.refs_1_, f32[128,128]{1,0:T(8,128)S(1)} %collective-permute-done.11.refs_2_, ...), custom_call_target="tpu_custom_call" | custom-call | tf_op jit(solution)/shard_map/class_rows/pallas_call | solution.py:263
  25.3 0.5 %collective-permute-start.14 = (f32[256,128]{1,0:T(8,128)S(1)}, f32[256,128]{1,0:T(8,128)S(1)}, u32[]{:S(2)}, u32[]{:S(2)}) collective-permute-start(f32[256,128]{1,0:T(8,128)S(1)} %class_rows.3.refs_7_), channel_id=1, source_target_pairs={{0,2},{2,0},{4,6},{6,4},{8,10},{10,8},{12,14},{14,12},{16,18},{18,... | collective-permute-start | bytes 393224 | tf_op jit(solution)/shard_map/ppermute | solution.py:326
  25.8 0.0 collective-permute-start.5
  25.8 1.4 %collective-permute-start.4 = (f32[128,128]{1,0:T(8,128)S(1)}, f32[128,128]{1,0:T(8,128)S(1)}, u32[]{:S(2)}, u32[]{:S(2)}) collective-permute-start(f32[128,128]{1,0:T(8,128)S(1)} %pad_maximum_fusion.refs_3_), channel_id=1, source_target_pairs={{0,16},{2,18},{4,20},{6,22},{8,24},{10,26},{12,28},{14,30},{16,0},... | collective-permute-start | bytes 196616 | tf_op jit(solution)/shard_map/ppermute | solution.py:326
  27.2 3.0 %collective-permute-start.3 = (f32[128,128]{1,0:T(8,128)S(1)}, f32[128,128]{1,0:T(8,128)S(1)}, u32[]{:S(2)}, u32[]{:S(2)}) collective-permute-start(f32[128,128]{1,0:T(8,128)S(1)} %pad_maximum_fusion.refs_3_), channel_id=1, source_target_pairs={{0,24},{2,26},{4,28},{6,30},{8,16},{10,18},{12,20},{14,22},{16,8},... | collective-permute-start | bytes 196616 | tf_op jit(solution)/shard_map/ppermute | solution.py:326
  30.2 0.1 copy.10.listed
  30.3 0.5 %collective-permute-start.13 = (f32[256,128]{1,0:T(8,128)S(1)}, f32[256,128]{1,0:T(8,128)S(1)}, u32[]{:S(2)}, u32[]{:S(2)}) collective-permute-start(f32[256,128]{1,0:T(8,128)S(1)} %class_rows.3.refs_7_), channel_id=1, source_target_pairs={{0,4},{2,6},{4,0},{6,2},{8,12},{10,14},{12,8},{14,10},{16,20},{18,... | collective-permute-start | bytes 393224 | tf_op jit(solution)/shard_map/ppermute | solution.py:326
  30.8 0.0 collective-permute-done.5.refs_2_
  30.8 2.5 %collective-permute-start.12 = (f32[256,128]{1,0:T(8,128)S(1)}, f32[256,128]{1,0:T(8,128)S(1)}, u32[]{:S(2)}, u32[]{:S(2)}) collective-permute-start(f32[256,128]{1,0:T(8,128)S(1)} %class_rows.3.refs_7_), channel_id=1, source_target_pairs={{0,6},{2,4},{4,2},{6,0},{8,14},{10,12},{12,10},{14,8},{16,22},{18,... | collective-permute-start | bytes 393224 | tf_op jit(solution)/shard_map/ppermute | solution.py:326
  33.3 0.6 %class_rows.2.refs_3_ = f32[256,128]{1,0:T(8,128)S(1)} custom-call(s32[2,256]{1,0:T(2,128)S(1)} %copy.10.listed, bf16[4,128,128]{2,1,0:T(8,128)(2,1)S(1)} %copy-done, f32[128,128]{1,0:T(8,128)S(1)} %collective-permute-done.3.refs_0_, f32[128,128]{1,0:T(8,128)S(1)} %collective-permute-done.4.refs_1_, f32[128,128]{1,0:T(8,128)S(1)} %collective-permute-done.5.refs_2_, ...), custom_call_target="tpu_custom_call" | custom-call | tf_op jit(solution)/shard_map/class_rows/pallas_call | solution.py:263
  33.9 1.5 %collective-permute-start.8 = (f32[256,128]{1,0:T(8,128)S(1)}, f32[256,128]{1,0:T(8,128)S(1)}, u32[]{:S(2)}, u32[]{:S(2)}) collective-permute-start(f32[256,128]{1,0:T(8,128)S(1)} %class_rows.2.refs_3_), channel_id=1, source_target_pairs={{0,2},{2,0},{4,6},{6,4},{8,10},{10,8},{12,14},{14,12},{16,18},{18,... | collective-permute-start | bytes 393224 | tf_op jit(solution)/shard_map/ppermute | solution.py:326
  35.4 0.5 %collective-permute-start.7 = (f32[256,128]{1,0:T(8,128)S(1)}, f32[256,128]{1,0:T(8,128)S(1)}, u32[]{:S(2)}, u32[]{:S(2)}) collective-permute-start(f32[256,128]{1,0:T(8,128)S(1)} %class_rows.2.refs_3_), channel_id=1, source_target_pairs={{0,4},{2,6},{4,0},{6,2},{8,12},{10,14},{12,8},{14,10},{16,20},{18,... | collective-permute-start | bytes 393224 | tf_op jit(solution)/shard_map/ppermute | solution.py:326
  35.9 1.6 %collective-permute-start.6 = (f32[256,128]{1,0:T(8,128)S(1)}, f32[256,128]{1,0:T(8,128)S(1)}, u32[]{:S(2)}, u32[]{:S(2)}) collective-permute-start(f32[256,128]{1,0:T(8,128)S(1)} %class_rows.2.refs_3_), channel_id=1, source_target_pairs={{0,6},{2,4},{4,2},{6,0},{8,14},{10,12},{12,10},{14,8},{16,22},{18,... | collective-permute-start | bytes 393224 | tf_op jit(solution)/shard_map/ppermute | solution.py:326
  37.5 3.0 %inverse.1 = f32[2048,128]{1,0:T(8,128)} custom-call(f32[2056,128]{1,0:T(8,128)S(1)} %get-tuple-element.11.coeffs, bf16[4,128,128]{2,1,0:T(8,128)(2,1)S(1)} %copy-done), custom_call_target="tpu_custom_call" | custom-call | tf_op jit(solution)/shard_map/inverse/pallas_call | solution.py:227
  40.5 1.3 %collective-permute-done.6.refs_0_ = f32[256,128]{1,0:T(8,128)S(1)} collective-permute-done((f32[256,128]{1,0:T(8,128)S(1)}, f32[256,128]{1,0:T(8,128)S(1)}, u32[]{:S(2)}, u32[]{:S(2)}) %collective-permute-start.6) | collective-permute-done | bytes 131104 | tf_op jit(solution)/shard_map/ppermute | solution.py:326
  41.8 0.9 %finish.1 = bf16[4,2,256,128]{3,2,1,0:T(8,128)(2,1)} custom-call(f32[256,128]{1,0:T(8,128)S(1)} %collective-permute-done.6.refs_0_, f32[256,128]{1,0:T(8,128)S(1)} %collective-permute-done.7.refs_1_, f32[256,128]{1,0:T(8,128)S(1)} %collective-permute-done.8.refs_2_, f32[256,128]{1,0:T(8,128)S(1)} %class_rows.2.refs_3_, ...), custom_call_target="tpu_custom_call" | custom-call | tf_op jit(solution)/shard_map/finish/pallas_call | solution.py:296
  (16 shorter events, 0.0 us)
Async XLA Ops:
  0.6 18.2 %copy-start.1 = (s32[16,2,16,8]{2,3,1,0:T(8,128)S(1)}, s32[16,2,16,8]{2,3,1,0:T(8,128)}, u32[]{:S(2)}) copy-start(s32[16,2,16,8]{2,3,1,0:T(8,128)} %param.8) | copy-start | bytes 49156
  0.6 24.1 %copy-start = (bf16[4,128,128]{2,1,0:T(8,128)(2,1)S(1)}, bf16[4,128,128]{2,1,0:T(8,128)(2,1)}, u32[]{:S(2)}) copy-start(bf16[4,128,128]{2,1,0:T(8,128)(2,1)} %constant.24.clone.dct_hbm.dct) | copy-start | bytes 393220
  5.0 4.9 %collective-permute-start = (f32[64,128]{1,0:T(8,128)S(1)}, f32[64,128]{1,0:T(8,128)S(1)}, u32[]{:S(2)}, u32[]{:S(2)}) collective-permute-start(f32[64,128]{1,0:T(8,128)S(1)} %get-tuple-element.8), channel_id=1, source_target_pairs={{0,2},{2,0},{4,6},{6,4},{8,10},{10,8},{12,14},{14,12},{16,18},{18,... | collective-permute-start | bytes 98312 | tf_op jit(solution)/shard_map/ppermute | solution.py:326
  8.0 3.9 %collective-permute-start.1 = (f32[64,128]{1,0:T(8,128)S(1)}, f32[64,128]{1,0:T(8,128)S(1)}, u32[]{:S(2)}, u32[]{:S(2)}) collective-permute-start(f32[64,128]{1,0:T(8,128)S(1)} %get-tuple-element.9), channel_id=1, source_target_pairs={{0,4},{2,6},{4,0},{6,2},{8,12},{10,14},{12,8},{14,10},{16,20},{18,... | collective-permute-start | bytes 98312 | tf_op jit(solution)/shard_map/ppermute | solution.py:326
  9.5 4.8 %collective-permute-start.2 = (f32[64,128]{1,0:T(8,128)S(1)}, f32[64,128]{1,0:T(8,128)S(1)}, u32[]{:S(2)}, u32[]{:S(2)}) collective-permute-start(f32[64,128]{1,0:T(8,128)S(1)} %get-tuple-element.10), channel_id=1, source_target_pairs={{0,6},{2,4},{4,2},{6,0},{8,14},{10,12},{12,10},{14,8},{16,22},{18,... | collective-permute-start | bytes 98312 | tf_op jit(solution)/shard_map/ppermute | solution.py:326
  14.3 4.7 %collective-permute-start.11 = (f32[128,128]{1,0:T(8,128)S(1)}, f32[128,128]{1,0:T(8,128)S(1)}, u32[]{:S(2)}, u32[]{:S(2)}) collective-permute-start(f32[128,128]{1,0:T(8,128)S(1)} %pad_maximum_fusion.1.refs_3_), channel_id=1, source_target_pairs={{0,8},{2,10},{4,12},{6,14},{8,0},{10,2},{12,4},{14,6},{16,24},{18,... | collective-permute-start | bytes 196616 | tf_op jit(solution)/shard_map/ppermute | solution.py:326
  16.0 6.6 %collective-permute-start.10 = (f32[128,128]{1,0:T(8,128)S(1)}, f32[128,128]{1,0:T(8,128)S(1)}, u32[]{:S(2)}, u32[]{:S(2)}) collective-permute-start(f32[128,128]{1,0:T(8,128)S(1)} %pad_maximum_fusion.1.refs_3_), channel_id=1, source_target_pairs={{0,16},{2,18},{4,20},{6,22},{8,24},{10,26},{12,28},{14,30},{16,0},... | collective-permute-start | bytes 196616 | tf_op jit(solution)/shard_map/ppermute | solution.py:326
  18.6 6.1 %collective-permute-start.9 = (f32[128,128]{1,0:T(8,128)S(1)}, f32[128,128]{1,0:T(8,128)S(1)}, u32[]{:S(2)}, u32[]{:S(2)}) collective-permute-start(f32[128,128]{1,0:T(8,128)S(1)} %pad_maximum_fusion.1.refs_3_), channel_id=1, source_target_pairs={{0,24},{2,26},{4,28},{6,30},{8,16},{10,18},{12,20},{14,22},{16,8},... | collective-permute-start | bytes 196616 | tf_op jit(solution)/shard_map/ppermute | solution.py:326
  25.3 10.6 %collective-permute-start.14 = (f32[256,128]{1,0:T(8,128)S(1)}, f32[256,128]{1,0:T(8,128)S(1)}, u32[]{:S(2)}, u32[]{:S(2)}) collective-permute-start(f32[256,128]{1,0:T(8,128)S(1)} %class_rows.3.refs_7_), channel_id=1, source_target_pairs={{0,2},{2,0},{4,6},{6,4},{8,10},{10,8},{12,14},{14,12},{16,18},{18,... | collective-permute-start | bytes 393224 | tf_op jit(solution)/shard_map/ppermute | solution.py:326
  25.8 5.0 %collective-permute-start.5 = (f32[128,128]{1,0:T(8,128)S(1)}, f32[128,128]{1,0:T(8,128)S(1)}, u32[]{:S(2)}, u32[]{:S(2)}) collective-permute-start(f32[128,128]{1,0:T(8,128)S(1)} %pad_maximum_fusion.refs_3_), channel_id=1, source_target_pairs={{0,8},{2,10},{4,12},{6,14},{8,0},{10,2},{12,4},{14,6},{16,24},{18,... | collective-permute-start | bytes 196616 | tf_op jit(solution)/shard_map/ppermute | solution.py:326
  25.8 7.5 %collective-permute-start.4 = (f32[128,128]{1,0:T(8,128)S(1)}, f32[128,128]{1,0:T(8,128)S(1)}, u32[]{:S(2)}, u32[]{:S(2)}) collective-permute-start(f32[128,128]{1,0:T(8,128)S(1)} %pad_maximum_fusion.refs_3_), channel_id=1, source_target_pairs={{0,16},{2,18},{4,20},{6,22},{8,24},{10,26},{12,28},{14,30},{16,0},... | collective-permute-start | bytes 196616 | tf_op jit(solution)/shard_map/ppermute | solution.py:326
  27.2 6.2 %collective-permute-start.3 = (f32[128,128]{1,0:T(8,128)S(1)}, f32[128,128]{1,0:T(8,128)S(1)}, u32[]{:S(2)}, u32[]{:S(2)}) collective-permute-start(f32[128,128]{1,0:T(8,128)S(1)} %pad_maximum_fusion.refs_3_), channel_id=1, source_target_pairs={{0,24},{2,26},{4,28},{6,30},{8,16},{10,18},{12,20},{14,22},{16,8},... | collective-permute-start | bytes 196616 | tf_op jit(solution)/shard_map/ppermute | solution.py:326
  30.3 10.2 %collective-permute-start.13 = (f32[256,128]{1,0:T(8,128)S(1)}, f32[256,128]{1,0:T(8,128)S(1)}, u32[]{:S(2)}, u32[]{:S(2)}) collective-permute-start(f32[256,128]{1,0:T(8,128)S(1)} %class_rows.3.refs_7_), channel_id=1, source_target_pairs={{0,4},{2,6},{4,0},{6,2},{8,12},{10,14},{12,8},{14,10},{16,20},{18,... | collective-permute-start | bytes 393224 | tf_op jit(solution)/shard_map/ppermute | solution.py:326
  30.8 9.7 %collective-permute-start.12 = (f32[256,128]{1,0:T(8,128)S(1)}, f32[256,128]{1,0:T(8,128)S(1)}, u32[]{:S(2)}, u32[]{:S(2)}) collective-permute-start(f32[256,128]{1,0:T(8,128)S(1)} %class_rows.3.refs_7_), channel_id=1, source_target_pairs={{0,6},{2,4},{4,2},{6,0},{8,14},{10,12},{12,10},{14,8},{16,22},{18,... | collective-permute-start | bytes 393224 | tf_op jit(solution)/shard_map/ppermute | solution.py:326
  33.9 6.6 %collective-permute-start.8 = (f32[256,128]{1,0:T(8,128)S(1)}, f32[256,128]{1,0:T(8,128)S(1)}, u32[]{:S(2)}, u32[]{:S(2)}) collective-permute-start(f32[256,128]{1,0:T(8,128)S(1)} %class_rows.2.refs_3_), channel_id=1, source_target_pairs={{0,2},{2,0},{4,6},{6,4},{8,10},{10,8},{12,14},{14,12},{16,18},{18,... | collective-permute-start | bytes 393224 | tf_op jit(solution)/shard_map/ppermute | solution.py:326
  35.4 5.1 %collective-permute-start.7 = (f32[256,128]{1,0:T(8,128)S(1)}, f32[256,128]{1,0:T(8,128)S(1)}, u32[]{:S(2)}, u32[]{:S(2)}) collective-permute-start(f32[256,128]{1,0:T(8,128)S(1)} %class_rows.2.refs_3_), channel_id=1, source_target_pairs={{0,4},{2,6},{4,0},{6,2},{8,12},{10,14},{12,8},{14,10},{16,20},{18,... | collective-permute-start | bytes 393224 | tf_op jit(solution)/shard_map/ppermute | solution.py:326
  35.9 5.9 %collective-permute-start.6 = (f32[256,128]{1,0:T(8,128)S(1)}, f32[256,128]{1,0:T(8,128)S(1)}, u32[]{:S(2)}, u32[]{:S(2)}) collective-permute-start(f32[256,128]{1,0:T(8,128)S(1)} %class_rows.2.refs_3_), channel_id=1, source_target_pairs={{0,6},{2,4},{4,2},{6,0},{8,14},{10,12},{12,10},{14,8},{16,22},{18,... | collective-permute-start | bytes 393224 | tf_op jit(solution)/shard_map/ppermute | solution.py:326

commit v5 on v4

--- a/solution.py
+++ b/solution.py
@@ -82,14 +82,16 @@
 
 
 def forward_kernel(inner, select, x_hbm, g_hbm, m_hbm, dct_hbm, *refs):
-    picks, rest = refs[:inner], refs[inner]
-    x, m, c1, f2, y, g, dct, listed, index_v, index, sems, small = refs[inner + 1 :]
+    picks, rest = refs[:inner], refs[inner : inner + CHUNKS]
+    scratch = refs[inner + CHUNKS :]
+    c1, f2, scratch = scratch[:CHUNKS], scratch[CHUNKS : 2 * CHUNKS], scratch[2 * CHUNKS :]
+    x, m, y, chosen, g, dct, listed, index_v, index, sems, small = scratch
     me = lax.axis_index("dp")
     rows, cols = m.shape
     steps, slots, owners = index.shape
     per_class = owners // inner
-    mine = me % inner
     width = rows // CHUNKS
+    owned = owners // CHUNKS
 
     def begin(source, target, sem):
         copy = pltpu.make_async_copy(source, target, sem)
@@ -103,15 +105,17 @@
         span = pl.ds(c * width, width)
         begin(m_hbm.at[span], m.at[span], sems.at[c, 0])
         begin(x_hbm.at[:, :, span], x.at[:, :, span], sems.at[c, 1])
-    c1[pl.ds(rows, 8), :] = jnp.zeros((8, cols), F32)
-    rest[pl.ds(rows, 8), :] = jnp.zeros((8, cols), F32)
+    zero = jnp.zeros((1, cols), F32)
+    for c in range(CHUNKS):
+        c1[c][pl.ds(width, 8), :] = jnp.zeros((8, cols), F32)
+        rest[c][pl.ds(width, 8), :] = jnp.zeros((8, cols), F32)
     fetch_dct.wait()
     table = left_table(dct[0], dct[1])
     fetch_g.wait()
     gradients = [split(add_rows(mm_nt(table[:, :cols], g[s])), 0) for s in range(steps)]
     fetch_select.wait()
-    owner = lax.broadcasted_iota(jnp.int32, listed.shape, 2)
-    index_v[...] = jnp.where(listed[...] >= 0, listed[...] + owner * (rows // owners), rows)
+    owner = lax.broadcasted_iota(jnp.int32, listed.shape, 2) % owned
+    index_v[...] = jnp.where(listed[...] >= 0, listed[...] + owner * (rows // owners), width)
     store = begin(index_v, index, small.at[2])
 
     def arrive(c):
@@ -129,46 +133,40 @@
     def transform(c):
         for t in range(0, width, cols):
             z = add_rows(mm_nt(table, split(y[c % 2, :, t : t + cols], 1)))
-            span = pl.ds(c * width + t, cols)
-            c1[span, :] = z[:, :cols]
-            f2[span, :] = z[:, cols:]
+            c1[c][t : t + cols] = z[:, :cols]
+            f2[c][t : t + cols] = z[:, cols:]
+
+    def choose(c, step, source):
+        for o in range(c * owned, (c + 1) * owned):
+            for k in range(slots):
+                chosen[o, pl.ds(step * slots + k, 1), :] = source[pl.ds(index[step, k, o], 1), :]
+
+    def clear(c, step, target):
+        for o in range(c * owned, (c + 1) * owned):
+            for k in range(slots):
+                target[pl.ds(index[step, k, o], 1), :] = zero
+
+    def pick(c):
+        choose(c, 0, c1[c])
+        clear(c, 0, c1[c])
+        rest[c][:width] = 0.999 * c1[c][:width] + f2[c][...]
+        choose(c, 1, rest[c])
+        clear(c, 1, rest[c])
 
     for c in range(CHUNKS):
         arrive(c)
+        if c == CHUNKS - 1:
+            store.wait()
         if c > 0:
             transform(c - 1)
         columns(c)
+        if c > 0:
+            pick(c - 1)
     transform(CHUNKS - 1)
-    store.wait()
-    zero = jnp.zeros((1, cols), F32)
-
-    def gather(step, source):
-        for j in range(inner):
-
-            def one(k, j=j):
-                base = (mine ^ j) * per_class
-                for c in range(slots):
-                    place = (k * steps + step) * slots + c
-                    picks[j][pl.ds(place, 1), :] = source[pl.ds(index[step, c, base + k], 1), :]
-                return 0
-
-            for k in range(per_class):
-                one(k)
-
-    def clear(step, target):
-        def one(k):
-            for c in range(slots):
-                target[pl.ds(index[step, c, k], 1), :] = zero
-            return 0
-
-        for k in range(owners):
-            one(k)
-
-    gather(0, c1)
-    clear(0, c1)
-    rest[:rows] = 0.999 * c1[:rows] + f2[...]
-    gather(1, rest)
-    clear(1, rest)
+    pick(CHUNKS - 1)
+    for j in range(inner):
+        own = chosen[pl.ds((me % inner ^ j) * per_class, per_class)]
+        picks[j][...] = own.reshape(picks[j].shape)
 
 
 def forward(select, x, g, m, dct, inner):
@@ -176,17 +174,19 @@
     steps = x.shape[0]
     owners, _, slots, _ = select.shape
     block = pltpu.VMEM((owners // inner * steps * slots, cols), F32)
+    chunk = pltpu.VMEM((rows // CHUNKS + 8, cols), F32)
     return pl.pallas_call(
         functools.partial(forward_kernel, inner),
-        out_shape=[block] * inner + [pltpu.VMEM((rows + 8, cols), F32)],
+        out_shape=[block] * inner + [chunk] * CHUNKS,
         in_specs=[IN_HBM] * 5,
-        out_specs=[IN_VMEM] * (inner + 1),
-        scratch_shapes=[
+        out_specs=[IN_VMEM] * (inner + CHUNKS),
+        scratch_shapes=[chunk] * CHUNKS
+        + [pltpu.VMEM((rows // CHUNKS, cols), F32)] * CHUNKS
+        + [
             pltpu.VMEM(x.shape, x.dtype),
             pltpu.VMEM((rows, cols), F32),
-            pltpu.VMEM((rows + 8, cols), F32),
-            pltpu.VMEM((rows, cols), F32),
             pltpu.VMEM((2, steps * cols, rows // CHUNKS), F32),
+            pltpu.VMEM((owners, steps * slots, cols), F32),
             pltpu.VMEM(g.shape, g.dtype),
             pltpu.VMEM(dct.shape, dct.dtype),
             pltpu.VMEM(select.shape[1:], jnp.int32),
@@ -204,34 +204,38 @@
     return left(row_table, right(value, col_table))
 
 
-def invert(source, target, row_table, table):
-    rows, cols = target.shape
-
-    def pair(c):
-        for t in range(2):
-            span = pl.ds((2 * c + t) * cols, cols)
-            target[span, :] = inverse_tile(source[span, :], row_table, table)
-        return 0
-
-    for c in range(rows // (2 * cols)):
-        pair(c)
-
-
-def inverse_kernel(coeffs, dct, out):
+def inverse_kernel(dct, *refs):
+    coeffs, (out, held, sems) = refs[:-3], refs[-3:]
     row_table, table = left_table(dct[2], dct[3]), right_table(dct[0], dct[1])
-    invert(coeffs, out, row_table, table)
+    rows, cols = out.shape
+    width = rows // len(coeffs)
+    part = rows // sems.shape[0]
+    copies = []
+    for r in range(0, rows, cols):
+        source = coeffs[r // width]
+        held[r : r + cols] = inverse_tile(
+            source[r % width : r % width + cols], row_table, table
+        )
+        if (r + cols) % part == 0:
+            span = pl.ds(r + cols - part, part)
+            copy = pltpu.make_async_copy(held.at[span], out.at[span], sems.at[r // part])
+            copy.start()
+            copies.append(copy)
+    for copy in copies:
+        copy.wait()
 
 
 def inverse(coeffs, dct, rows):
-    cols = coeffs.shape[1]
+    cols = coeffs[0].shape[1]
     return pl.pallas_call(
         inverse_kernel,
         out_shape=jax.ShapeDtypeStruct((rows, cols), F32),
-        in_specs=[IN_VMEM] * 2,
-        out_specs=IN_VMEM,
+        in_specs=[IN_VMEM] * (1 + len(coeffs)),
+        out_specs=IN_HBM,
+        scratch_shapes=[pltpu.VMEM((rows, cols), F32), pltpu.SemaphoreType.DMA((4,))],
         compiler_params=PARAMS,
         name="inverse",
-    )(vmem(coeffs), dct)
+    )(dct, *[vmem(c) for c in coeffs])
 
 
 def class_kernel(inner, listed, dct, *refs):
@@ -274,37 +278,32 @@
     )(listed, dct, *[vmem(b) for b in reversed(blocks)])
 
 
-def finish_kernel(halves, *refs):
-    blocks, out, held, sems = refs[-4::-1], refs[-3], refs[-2], refs[-1]
+def finish_kernel(half, count, *refs):
+    blocks, (out, held, sems) = refs[count - 1 :: -1], refs[-3:]
     me = lax.axis_index("dp")
-    inner = len(blocks) // halves
     copies = []
-    for h in range(halves):
-        for j in range(inner):
-            i = h * inner + j
-            held[i] = blocks[i][...].astype(held.dtype)
-            copy = pltpu.make_async_copy(held.at[i], out.at[me % inner ^ j, h], sems.at[i])
-            copy.start()
-            copies.append(copy)
+    for j, block in enumerate(blocks):
+        held[j] = block[...].astype(held.dtype)
+        copy = pltpu.make_async_copy(held.at[j], out.at[me % count ^ j, half], sems.at[j])
+        copy.start()
+        copies.append(copy)
     for copy in copies:
         copy.wait()
 
 
-def finish(outs):
-    blocks = [b for half in outs for b in half]
-    shape = blocks[0].shape
+def finish(half, blocks, earlier=None):
+    kept = [] if earlier is None else [earlier]
+    count, shape = len(blocks), blocks[0].shape
     return pl.pallas_call(
-        functools.partial(finish_kernel, len(outs)),
-        out_shape=jax.ShapeDtypeStruct((len(outs[0]), len(outs)) + shape, BF16),
-        in_specs=[IN_VMEM] * len(blocks),
+        functools.partial(finish_kernel, half, count),
+        out_shape=jax.ShapeDtypeStruct((count, HALVES) + shape, BF16),
+        in_specs=[IN_VMEM] * count + [IN_HBM] * len(kept),
         out_specs=IN_HBM,
-        scratch_shapes=[
-            pltpu.VMEM((len(blocks),) + shape, BF16),
-            pltpu.SemaphoreType.DMA((len(blocks),)),
-        ],
+        input_output_aliases={count: 0} if kept else {},
+        scratch_shapes=[pltpu.VMEM((count,) + shape, BF16), pltpu.SemaphoreType.DMA((count,))],
         compiler_params=PARAMS,
         name="finish",
-    )(*[vmem(b) for b in reversed(blocks)])
+    )(*[vmem(b) for b in reversed(blocks)], *kept)
 
 
 def inner_size(owners):
@@ -331,9 +330,10 @@
             got.append(from_peer(values[j], j * stride))
         return got
 
-    *picks, rest = forward(
+    made = forward(
         jnp.swapaxes(select, 2, 3), inputs[0], grad_out[0], momentum[0], dct, inner
     )
+    picks, rest = made[:inner], made[inner:]
     listed = jnp.transpose(select, (2, 0, 1, 3)).reshape(owners, -1)
     listed = lax.dynamic_slice_in_dim(listed, replica % inner * outer, outer, 0)
     peers = from_peers(picks, 1)
@@ -349,7 +349,9 @@
         )
         outs.append(from_peers([own] * inner, 1))
     new_momentum = inverse(rest, dct, rows)
-    update = finish(outs)
+    update = None
+    for h, blocks in enumerate(outs):
+        update = finish(h, blocks, update)
     return (update.reshape(rows, cols), new_momentum[None])
 
 

time: 42.8 us -> 42.5 us (level)
  waiting for transfers between devices: 11.8 us -> 11.2 us
    pallas_call x1 -> x2, Pallas kernels: 0.86 us -> 1.49 us  [finish(): pl.pallas_call(functools.partial(finish_kernel, half, count), out_shape=j...]
    ppermute x15, waiting for transfers between devices: 11.8 us -> 11.2 us  [from_peer(): return lax.ppermute(value, 'dp', [(d, d ^ shift) for d in range(owners)])]
  transfers between devices with their start and end apart: 15 -> 15, of which waited for: 6 -> 6; matrix products, arithmetic and copies ran while one was open for 1% -> 1% of each run, Pallas kernels for 8% -> 10%
where the time goes in v5:
time: 42.5 us; the launch traced here: 42.3 us
  starting transfers between devices  20.6 us (48%)
  waiting for transfers between devices  11.2 us (26%)
  Pallas kernels  9.51 us (22%)
  between operations  0.75 us (2%)
    ppermute x15, starting transfers between devices, from_peer(): return lax.ppermute(value, 'dp', [(d, d ^ shift) for d in range(owners)])  20.6 us
    ppermute x15, waiting for transfers between devices, from_peer(): return lax.ppermute(value, 'dp', [(d, d ^ shift) for d in range(owners)])  11.2 us
    pallas_call x1, Pallas kernels, forward(): pl.pallas_call(functools.partial(forward_kernel, inner), out_shape=[block...  4.12 us
    pallas_call x1, Pallas kernels, inverse(): pl.pallas_call(inverse_kernel, out_shape=jax.ShapeDtypeStruct((rows, cols...  2.75 us
    pallas_call x2, Pallas kernels, finish(): pl.pallas_call(functools.partial(finish_kernel, half, count), out_shape=j...  1.49 us
    pallas_call x2, Pallas kernels, class_rows(): pl.pallas_call(functools.partial(class_kernel, inner), out_shape=pltpu.VM...  1.15 us
  transfers between devices with their start and end apart: 15, of which 6 were waited for; matrix products, arithmetic and copies ran while one was open for 1% of the time, Pallas kernels for 10%

profile of v5, /device:TPU:0, one launch (start us, length us, event | category | flops | bytes accessed | tf_op | source)
XLA Modules:
  0.0 42.3 jit_solution(1009275178679080852)
XLA Ops:
  0.6 0.0 copy-start
  0.7 4.1 %forward.1 = (f32[64,128]{1,0:T(8,128)S(1)}, f32[64,128]{1,0:T(8,128)S(1)}, f32[64,128]{1,0:T(8,128)S(1)}, f32[64,128]{1,0:T(8,128)S(1)}, f32[1032,128]{1,0:T(8,128)S(1)}, /*index=5*/f32[1032,128]{1,0:T(8,128)S(1)}) custom-call(s32[16,2,8,16]{3,2,1,0:T(8,128)} %bitcast.11, bf16[2,256,2048]{2,1,0:T(8,128)(2,1)} %bitcast.9, bf16[2,256,128]{2,1,0:T(8,128)(2,1)} %bitcast.15, ...), custom_call_target="tpu_custom_call" | custom-call | tf_op jit(solution)/shard_map/forward/pallas_call | solution.py:178
  4.8 3.0 %collective-permute-start = (f32[64,128]{1,0:T(8,128)S(1)}, f32[64,128]{1,0:T(8,128)S(1)}, u32[]{:S(2)}, u32[]{:S(2)}) collective-permute-start(f32[64,128]{1,0:T(8,128)S(1)} %get-tuple-element.9), channel_id=1, source_target_pairs={{0,2},{2,0},{4,6},{6,4},{8,10},{10,8},{12,14},{14,12},{16,18},{18,... | collective-permute-start | bytes 98312 | tf_op jit(solution)/shard_map/ppermute | solution.py:325
  7.8 1.5 %collective-permute-start.1 = (f32[64,128]{1,0:T(8,128)S(1)}, f32[64,128]{1,0:T(8,128)S(1)}, u32[]{:S(2)}, u32[]{:S(2)}) collective-permute-start(f32[64,128]{1,0:T(8,128)S(1)} %get-tuple-element.10), channel_id=1, source_target_pairs={{0,4},{2,6},{4,0},{6,2},{8,12},{10,14},{12,8},{14,10},{16,20},{18,... | collective-permute-start | bytes 98312 | tf_op jit(solution)/shard_map/ppermute | solution.py:325
  9.3 0.0 collective-permute-start.2
  9.4 0.3 collective-permute-done
  9.7 2.0 %collective-permute-done.1 = f32[64,128]{1,0:T(8,128)S(1)} collective-permute-done((f32[64,128]{1,0:T(8,128)S(1)}, f32[64,128]{1,0:T(8,128)S(1)}, u32[]{:S(2)}, u32[]{:S(2)}) %collective-permute-start.1) | collective-permute-done | bytes 32800 | tf_op jit(solution)/shard_map/ppermute | solution.py:325
  11.7 2.4 %collective-permute-done.2 = f32[64,128]{1,0:T(8,128)S(1)} collective-permute-done((f32[64,128]{1,0:T(8,128)S(1)}, f32[64,128]{1,0:T(8,128)S(1)}, u32[]{:S(2)}, u32[]{:S(2)}) %collective-permute-start.2) | collective-permute-done | bytes 32800 | tf_op jit(solution)/shard_map/ppermute | solution.py:325
  14.2 1.6 %collective-permute-start.11 = (f32[128,128]{1,0:T(8,128)S(1)}, f32[128,128]{1,0:T(8,128)S(1)}, u32[]{:S(2)}, u32[]{:S(2)}) collective-permute-start(f32[128,128]{1,0:T(8,128)S(1)} %pad_maximum_fusion.1.refs_3_), channel_id=1, source_target_pairs={{0,8},{2,10},{4,12},{6,14},{8,0},{10,2},{12,4},{14,6},{16,24},{18,... | collective-permute-start | bytes 196616 | tf_op jit(solution)/shard_map/ppermute | solution.py:325
  15.8 2.6 %collective-permute-start.10 = (f32[128,128]{1,0:T(8,128)S(1)}, f32[128,128]{1,0:T(8,128)S(1)}, u32[]{:S(2)}, u32[]{:S(2)}) collective-permute-start(f32[128,128]{1,0:T(8,128)S(1)} %pad_maximum_fusion.1.refs_3_), channel_id=1, source_target_pairs={{0,16},{2,18},{4,20},{6,22},{8,24},{10,26},{12,28},{14,30},{16,0},... | collective-permute-start | bytes 196616 | tf_op jit(solution)/shard_map/ppermute | solution.py:325
  18.4 0.2 collective-permute-start.9
  18.6 0.1 constant_dynamic-slice_fusion.1
  18.8 0.1 copy.12.listed
  18.8 0.0 collective-permute-done.11.refs_2_
  18.8 3.5 %collective-permute-done.10.refs_1_ = f32[128,128]{1,0:T(8,128)S(1)} collective-permute-done((f32[128,128]{1,0:T(8,128)S(1)}, f32[128,128]{1,0:T(8,128)S(1)}, u32[]{:S(2)}, u32[]{:S(2)}) %collective-permute-start.10) | collective-permute-done | bytes 65568 | tf_op jit(solution)/shard_map/ppermute | solution.py:325
  22.4 2.2 %collective-permute-done.9.refs_0_ = f32[128,128]{1,0:T(8,128)S(1)} collective-permute-done((f32[128,128]{1,0:T(8,128)S(1)}, f32[128,128]{1,0:T(8,128)S(1)}, u32[]{:S(2)}, u32[]{:S(2)}) %collective-permute-start.9) | collective-permute-done | bytes 65568 | tf_op jit(solution)/shard_map/ppermute | solution.py:325
  24.6 0.6 %class_rows.3.refs_3_ = f32[256,128]{1,0:T(8,128)S(1)} custom-call(s32[2,256]{1,0:T(2,128)S(1)} %copy.12.listed, bf16[4,128,128]{2,1,0:T(8,128)(2,1)S(1)} %copy-done, f32[128,128]{1,0:T(8,128)S(1)} %collective-permute-done.9.refs_0_, f32[128,128]{1,0:T(8,128)S(1)} %collective-permute-done.10.refs_1_, f32[128,128]{1,0:T(8,128)S(1)} %collective-permute-done.11.refs_2_, ...), custom_call_target="tpu_custom_call" | custom-call | tf_op jit(solution)/shard_map/class_rows/pallas_call | solution.py:267
  25.1 0.5 %collective-permute-start.14 = (f32[256,128]{1,0:T(8,128)S(1)}, f32[256,128]{1,0:T(8,128)S(1)}, u32[]{:S(2)}, u32[]{:S(2)}) collective-permute-start(f32[256,128]{1,0:T(8,128)S(1)} %class_rows.3.refs_3_), channel_id=1, source_target_pairs={{0,2},{2,0},{4,6},{6,4},{8,10},{10,8},{12,14},{14,12},{16,18},{18,... | collective-permute-start | bytes 393224 | tf_op jit(solution)/shard_map/ppermute | solution.py:325
  25.6 0.0 collective-permute-start.5
  25.7 1.4 %collective-permute-start.4 = (f32[128,128]{1,0:T(8,128)S(1)}, f32[128,128]{1,0:T(8,128)S(1)}, u32[]{:S(2)}, u32[]{:S(2)}) collective-permute-start(f32[128,128]{1,0:T(8,128)S(1)} %pad_maximum_fusion.refs_3_), channel_id=1, source_target_pairs={{0,16},{2,18},{4,20},{6,22},{8,24},{10,26},{12,28},{14,30},{16,0},... | collective-permute-start | bytes 196616 | tf_op jit(solution)/shard_map/ppermute | solution.py:325
  27.0 3.0 %collective-permute-start.3 = (f32[128,128]{1,0:T(8,128)S(1)}, f32[128,128]{1,0:T(8,128)S(1)}, u32[]{:S(2)}, u32[]{:S(2)}) collective-permute-start(f32[128,128]{1,0:T(8,128)S(1)} %pad_maximum_fusion.refs_3_), channel_id=1, source_target_pairs={{0,24},{2,26},{4,28},{6,30},{8,16},{10,18},{12,20},{14,22},{16,8},... | collective-permute-start | bytes 196616 | tf_op jit(solution)/shard_map/ppermute | solution.py:325
  30.0 0.1 copy.11.listed
  30.1 0.5 %collective-permute-start.13 = (f32[256,128]{1,0:T(8,128)S(1)}, f32[256,128]{1,0:T(8,128)S(1)}, u32[]{:S(2)}, u32[]{:S(2)}) collective-permute-start(f32[256,128]{1,0:T(8,128)S(1)} %class_rows.3.refs_3_), channel_id=1, source_target_pairs={{0,4},{2,6},{4,0},{6,2},{8,12},{10,14},{12,8},{14,10},{16,20},{18,... | collective-permute-start | bytes 393224 | tf_op jit(solution)/shard_map/ppermute | solution.py:325
  30.7 2.5 %collective-permute-start.12 = (f32[256,128]{1,0:T(8,128)S(1)}, f32[256,128]{1,0:T(8,128)S(1)}, u32[]{:S(2)}, u32[]{:S(2)}) collective-permute-start(f32[256,128]{1,0:T(8,128)S(1)} %class_rows.3.refs_3_), channel_id=1, source_target_pairs={{0,6},{2,4},{4,2},{6,0},{8,14},{10,12},{12,10},{14,8},{16,22},{18,... | collective-permute-start | bytes 393224 | tf_op jit(solution)/shard_map/ppermute | solution.py:325
  33.2 0.6 %class_rows.2.refs_3_ = f32[256,128]{1,0:T(8,128)S(1)} custom-call(s32[2,256]{1,0:T(2,128)S(1)} %copy.11.listed, bf16[4,128,128]{2,1,0:T(8,128)(2,1)S(1)} %copy-done, f32[128,128]{1,0:T(8,128)S(1)} %collective-permute-done.3.refs_0_, f32[128,128]{1,0:T(8,128)S(1)} %collective-permute-done.4.refs_1_, f32[128,128]{1,0:T(8,128)S(1)} %collective-permute-done.5.refs_2_, ...), custom_call_target="tpu_custom_call" | custom-call | tf_op jit(solution)/shard_map/class_rows/pallas_call | solution.py:267
  33.8 1.4 %collective-permute-start.8 = (f32[256,128]{1,0:T(8,128)S(1)}, f32[256,128]{1,0:T(8,128)S(1)}, u32[]{:S(2)}, u32[]{:S(2)}) collective-permute-start(f32[256,128]{1,0:T(8,128)S(1)} %class_rows.2.refs_3_), channel_id=1, source_target_pairs={{0,2},{2,0},{4,6},{6,4},{8,10},{10,8},{12,14},{14,12},{16,18},{18,... | collective-permute-start | bytes 393224 | tf_op jit(solution)/shard_map/ppermute | solution.py:325
  35.2 0.5 %collective-permute-start.7 = (f32[256,128]{1,0:T(8,128)S(1)}, f32[256,128]{1,0:T(8,128)S(1)}, u32[]{:S(2)}, u32[]{:S(2)}) collective-permute-start(f32[256,128]{1,0:T(8,128)S(1)} %class_rows.2.refs_3_), channel_id=1, source_target_pairs={{0,4},{2,6},{4,0},{6,2},{8,12},{10,14},{12,8},{14,10},{16,20},{18,... | collective-permute-start | bytes 393224 | tf_op jit(solution)/shard_map/ppermute | solution.py:325
  35.7 1.6 %collective-permute-start.6 = (f32[256,128]{1,0:T(8,128)S(1)}, f32[256,128]{1,0:T(8,128)S(1)}, u32[]{:S(2)}, u32[]{:S(2)}) collective-permute-start(f32[256,128]{1,0:T(8,128)S(1)} %class_rows.2.refs_3_), channel_id=1, source_target_pairs={{0,6},{2,4},{4,2},{6,0},{8,14},{10,12},{12,10},{14,8},{16,22},{18,... | collective-permute-start | bytes 393224 | tf_op jit(solution)/shard_map/ppermute | solution.py:325
  37.3 2.8 %inverse.1 = f32[2048,128]{1,0:T(8,128)} custom-call(bf16[4,128,128]{2,1,0:T(8,128)(2,1)S(1)} %copy-done, f32[1032,128]{1,0:T(8,128)S(1)} %get-tuple-element.12.refs_0_, f32[1032,128]{1,0:T(8,128)S(1)} %get-tuple-element.13.refs_1_), custom_call_target="tpu_custom_call" | custom-call | tf_op jit(solution)/shard_map/inverse/pallas_call | solution.py:230
  40.1 0.7 %finish.2.refs_4_ = bf16[4,2,256,128]{3,2,1,0:T(8,128)(2,1)} custom-call(f32[256,128]{1,0:T(8,128)S(1)} %collective-permute-done.12.refs_0_, f32[256,128]{1,0:T(8,128)S(1)} %collective-permute-done.13.refs_1_, f32[256,128]{1,0:T(8,128)S(1)} %collective-permute-done.14.refs_2_, f32[256,128]{1,0:T(8,128)S(1)} %class_rows.3.refs_3_), custom_call_target="tpu_custom_call" | custom-call | tf_op jit(solution)/shard_map/finish/pallas_call | solution.py:297
  40.9 0.7 %collective-permute-done.6.refs_0_ = f32[256,128]{1,0:T(8,128)S(1)} collective-permute-done((f32[256,128]{1,0:T(8,128)S(1)}, f32[256,128]{1,0:T(8,128)S(1)}, u32[]{:S(2)}, u32[]{:S(2)}) %collective-permute-start.6) | collective-permute-done | bytes 131104 | tf_op jit(solution)/shard_map/ppermute | solution.py:325
  41.6 0.7 %finish.3 = bf16[4,2,256,128]{3,2,1,0:T(8,128)(2,1)} custom-call(f32[256,128]{1,0:T(8,128)S(1)} %collective-permute-done.6.refs_0_, f32[256,128]{1,0:T(8,128)S(1)} %collective-permute-done.7.refs_1_, f32[256,128]{1,0:T(8,128)S(1)} %collective-permute-done.8.refs_2_, f32[256,128]{1,0:T(8,128)S(1)} %class_rows.2.refs_3_, ...), custom_call_target="tpu_custom_call", output_to_operand_aliasing={{}: (4, {})} | custom-call | tf_op jit(solution)/shard_map/finish/pallas_call | solution.py:297
  (17 shorter events, 0.1 us)
Async XLA Ops:
  0.6 18.0 %copy-start.1 = (s32[16,2,16,8]{2,3,1,0:T(8,128)S(1)}, s32[16,2,16,8]{2,3,1,0:T(8,128)}, u32[]{:S(2)}) copy-start(s32[16,2,16,8]{2,3,1,0:T(8,128)} %param.8) | copy-start | bytes 49156
  0.6 23.9 %copy-start = (bf16[4,128,128]{2,1,0:T(8,128)(2,1)S(1)}, bf16[4,128,128]{2,1,0:T(8,128)(2,1)}, u32[]{:S(2)}) copy-start(bf16[4,128,128]{2,1,0:T(8,128)(2,1)} %constant.24.clone.dct_hbm.dct) | copy-start | bytes 393220
  4.8 4.9 %collective-permute-start = (f32[64,128]{1,0:T(8,128)S(1)}, f32[64,128]{1,0:T(8,128)S(1)}, u32[]{:S(2)}, u32[]{:S(2)}) collective-permute-start(f32[64,128]{1,0:T(8,128)S(1)} %get-tuple-element.9), channel_id=1, source_target_pairs={{0,2},{2,0},{4,6},{6,4},{8,10},{10,8},{12,14},{14,12},{16,18},{18,... | collective-permute-start | bytes 98312 | tf_op jit(solution)/shard_map/ppermute | solution.py:325
  7.8 3.9 %collective-permute-start.1 = (f32[64,128]{1,0:T(8,128)S(1)}, f32[64,128]{1,0:T(8,128)S(1)}, u32[]{:S(2)}, u32[]{:S(2)}) collective-permute-start(f32[64,128]{1,0:T(8,128)S(1)} %get-tuple-element.10), channel_id=1, source_target_pairs={{0,4},{2,6},{4,0},{6,2},{8,12},{10,14},{12,8},{14,10},{16,20},{18,... | collective-permute-start | bytes 98312 | tf_op jit(solution)/shard_map/ppermute | solution.py:325
  9.3 4.8 %collective-permute-start.2 = (f32[64,128]{1,0:T(8,128)S(1)}, f32[64,128]{1,0:T(8,128)S(1)}, u32[]{:S(2)}, u32[]{:S(2)}) collective-permute-start(f32[64,128]{1,0:T(8,128)S(1)} %get-tuple-element.11), channel_id=1, source_target_pairs={{0,6},{2,4},{4,2},{6,0},{8,14},{10,12},{12,10},{14,8},{16,22},{18,... | collective-permute-start | bytes 98312 | tf_op jit(solution)/shard_map/ppermute | solution.py:325
  14.2 4.7 %collective-permute-start.11 = (f32[128,128]{1,0:T(8,128)S(1)}, f32[128,128]{1,0:T(8,128)S(1)}, u32[]{:S(2)}, u32[]{:S(2)}) collective-permute-start(f32[128,128]{1,0:T(8,128)S(1)} %pad_maximum_fusion.1.refs_3_), channel_id=1, source_target_pairs={{0,8},{2,10},{4,12},{6,14},{8,0},{10,2},{12,4},{14,6},{16,24},{18,... | collective-permute-start | bytes 196616 | tf_op jit(solution)/shard_map/ppermute | solution.py:325
  15.8 6.6 %collective-permute-start.10 = (f32[128,128]{1,0:T(8,128)S(1)}, f32[128,128]{1,0:T(8,128)S(1)}, u32[]{:S(2)}, u32[]{:S(2)}) collective-permute-start(f32[128,128]{1,0:T(8,128)S(1)} %pad_maximum_fusion.1.refs_3_), channel_id=1, source_target_pairs={{0,16},{2,18},{4,20},{6,22},{8,24},{10,26},{12,28},{14,30},{16,0},... | collective-permute-start | bytes 196616 | tf_op jit(solution)/shard_map/ppermute | solution.py:325
  18.4 6.2 %collective-permute-start.9 = (f32[128,128]{1,0:T(8,128)S(1)}, f32[128,128]{1,0:T(8,128)S(1)}, u32[]{:S(2)}, u32[]{:S(2)}) collective-permute-start(f32[128,128]{1,0:T(8,128)S(1)} %pad_maximum_fusion.1.refs_3_), channel_id=1, source_target_pairs={{0,24},{2,26},{4,28},{6,30},{8,16},{10,18},{12,20},{14,22},{16,8},... | collective-permute-start | bytes 196616 | tf_op jit(solution)/shard_map/ppermute | solution.py:325
  25.1 10.6 %collective-permute-start.14 = (f32[256,128]{1,0:T(8,128)S(1)}, f32[256,128]{1,0:T(8,128)S(1)}, u32[]{:S(2)}, u32[]{:S(2)}) collective-permute-start(f32[256,128]{1,0:T(8,128)S(1)} %class_rows.3.refs_3_), channel_id=1, source_target_pairs={{0,2},{2,0},{4,6},{6,4},{8,10},{10,8},{12,14},{14,12},{16,18},{18,... | collective-permute-start | bytes 393224 | tf_op jit(solution)/shard_map/ppermute | solution.py:325
  25.6 5.0 %collective-permute-start.5 = (f32[128,128]{1,0:T(8,128)S(1)}, f32[128,128]{1,0:T(8,128)S(1)}, u32[]{:S(2)}, u32[]{:S(2)}) collective-permute-start(f32[128,128]{1,0:T(8,128)S(1)} %pad_maximum_fusion.refs_3_), channel_id=1, source_target_pairs={{0,8},{2,10},{4,12},{6,14},{8,0},{10,2},{12,4},{14,6},{16,24},{18,... | collective-permute-start | bytes 196616 | tf_op jit(solution)/shard_map/ppermute | solution.py:325
  25.7 7.5 %collective-permute-start.4 = (f32[128,128]{1,0:T(8,128)S(1)}, f32[128,128]{1,0:T(8,128)S(1)}, u32[]{:S(2)}, u32[]{:S(2)}) collective-permute-start(f32[128,128]{1,0:T(8,128)S(1)} %pad_maximum_fusion.refs_3_), channel_id=1, source_target_pairs={{0,16},{2,18},{4,20},{6,22},{8,24},{10,26},{12,28},{14,30},{16,0},... | collective-permute-start | bytes 196616 | tf_op jit(solution)/shard_map/ppermute | solution.py:325
  27.0 6.2 %collective-permute-start.3 = (f32[128,128]{1,0:T(8,128)S(1)}, f32[128,128]{1,0:T(8,128)S(1)}, u32[]{:S(2)}, u32[]{:S(2)}) collective-permute-start(f32[128,128]{1,0:T(8,128)S(1)} %pad_maximum_fusion.refs_3_), channel_id=1, source_target_pairs={{0,24},{2,26},{4,28},{6,30},{8,16},{10,18},{12,20},{14,22},{16,8},... | collective-permute-start | bytes 196616 | tf_op jit(solution)/shard_map/ppermute | solution.py:325
  30.1 10.0 %collective-permute-start.13 = (f32[256,128]{1,0:T(8,128)S(1)}, f32[256,128]{1,0:T(8,128)S(1)}, u32[]{:S(2)}, u32[]{:S(2)}) collective-permute-start(f32[256,128]{1,0:T(8,128)S(1)} %class_rows.3.refs_3_), channel_id=1, source_target_pairs={{0,4},{2,6},{4,0},{6,2},{8,12},{10,14},{12,8},{14,10},{16,20},{18,... | collective-permute-start | bytes 393224 | tf_op jit(solution)/shard_map/ppermute | solution.py:325
  30.7 9.5 %collective-permute-start.12 = (f32[256,128]{1,0:T(8,128)S(1)}, f32[256,128]{1,0:T(8,128)S(1)}, u32[]{:S(2)}, u32[]{:S(2)}) collective-permute-start(f32[256,128]{1,0:T(8,128)S(1)} %class_rows.3.refs_3_), channel_id=1, source_target_pairs={{0,6},{2,4},{4,2},{6,0},{8,14},{10,12},{12,10},{14,8},{16,22},{18,... | collective-permute-start | bytes 393224 | tf_op jit(solution)/shard_map/ppermute | solution.py:325
  33.8 7.1 %collective-permute-start.8 = (f32[256,128]{1,0:T(8,128)S(1)}, f32[256,128]{1,0:T(8,128)S(1)}, u32[]{:S(2)}, u32[]{:S(2)}) collective-permute-start(f32[256,128]{1,0:T(8,128)S(1)} %class_rows.2.refs_3_), channel_id=1, source_target_pairs={{0,2},{2,0},{4,6},{6,4},{8,10},{10,8},{12,14},{14,12},{16,18},{18,... | collective-permute-start | bytes 393224 | tf_op jit(solution)/shard_map/ppermute | solution.py:325
  35.2 5.7 %collective-permute-start.7 = (f32[256,128]{1,0:T(8,128)S(1)}, f32[256,128]{1,0:T(8,128)S(1)}, u32[]{:S(2)}, u32[]{:S(2)}) collective-permute-start(f32[256,128]{1,0:T(8,128)S(1)} %class_rows.2.refs_3_), channel_id=1, source_target_pairs={{0,4},{2,6},{4,0},{6,2},{8,12},{10,14},{12,8},{14,10},{16,20},{18,... | collective-permute-start | bytes 393224 | tf_op jit(solution)/shard_map/ppermute | solution.py:325
  35.7 5.9 %collective-permute-start.6 = (f32[256,128]{1,0:T(8,128)S(1)}, f32[256,128]{1,0:T(8,128)S(1)}, u32[]{:S(2)}, u32[]{:S(2)}) collective-permute-start(f32[256,128]{1,0:T(8,128)S(1)} %class_rows.2.refs_3_), channel_id=1, source_target_pairs={{0,6},{2,4},{4,2},{6,0},{8,14},{10,12},{12,10},{14,8},{16,22},{18,... | collective-permute-start | bytes 393224 | tf_op jit(solution)/shard_map/ppermute | solution.py:325

commit v6 on v5

--- a/solution.py
+++ b/solution.py
@@ -239,7 +239,7 @@
 
 
 def class_kernel(inner, listed, dct, *refs):
-    blocks, out, ordered, total = refs[-4::-1], refs[-3], refs[-2], refs[-1]
+    blocks, out, ordered = refs[-3::-1], refs[-2], refs[-1]
     me = lax.axis_index("dp")
     rows, cols = out.shape
     per_class, slots = listed.shape
@@ -253,9 +253,11 @@
             for o in range(per_class):
                 ordered[o, span, :] = split(block[pl.ds((j * per_class + o) * each, each), :], 1)
     ids = lax.broadcasted_iota(jnp.int32, (per_owner, slots), 0)
+    sums = []
     for o in range(per_class):
         onehot = jnp.where(ids == listed[pl.ds(o, 1), :], 1.0, 0.0).astype(BF16)
-        total[pl.ds(o * per_owner, per_owner), :] = add_columns(mm(onehot, ordered[o]))
+        sums.append(add_columns(mm(onehot, ordered[o])))
+    total = jnp.concatenate(sums, axis=0)
     row_table, table = left_table(dct[2], dct[3]), right_table(dct[0], dct[1])
     for r in range(0, rows, cols):
         out[r : r + cols] = inverse_tile(total[r : r + cols], row_table, table)
@@ -271,7 +273,6 @@
         out_specs=IN_VMEM,
         scratch_shapes=[
             pltpu.VMEM((per_class, slots, 2 * cols), BF16),
-            pltpu.VMEM((rows, cols), F32),
         ],
         compiler_params=PARAMS,
         name="class_rows",
@@ -338,14 +339,17 @@
     listed = lax.dynamic_slice_in_dim(listed, replica % inner * outer, outer, 0)
     peers = from_peers(picks, 1)
     each = owners // inner // HALVES
-    lines, outs = [], []
+    lines, outs, planes = [], [], []
     for h in range(HALVES):
         span = slice(h * picks[0].shape[0] // HALVES, (h + 1) * picks[0].shape[0] // HALVES)
-        plane = jnp.concatenate([p[span] for p in peers])
-        lines.append(from_peers([plane] * outer, inner))
+        planes.append(jnp.concatenate([p[span] for p in peers]))
+    slots_of = [listed[h * each : (h + 1) * each] for h in range(HALVES)]
+    planes[0], *slots_of = lax.optimization_barrier((planes[0], *slots_of))
+    for h in range(HALVES):
+        lines.append(from_peers([planes[h]] * outer, inner))
     for h in range(HALVES):
         own = class_rows(
-            listed[h * each : (h + 1) * each], lines[h], dct, inner, rows // inner // HALVES
+            slots_of[h], lines[h], dct, inner, rows // inner // HALVES
         )
         outs.append(from_peers([own] * inner, 1))
     new_momentum = inverse(rest, dct, rows)

time: 42.5 us -> 42.5 us (level)
  transfers between devices with their start and end apart: 15 -> 15, of which waited for: 6 -> 5; matrix products, arithmetic and copies ran while one was open for 1% -> 1% of each run, Pallas kernels for 10% -> 10%
where the time goes in v6:
time: 42.5 us; the launch traced here: 42.3 us
  starting transfers between devices  20.5 us (48%)
  waiting for transfers between devices  11.2 us (26%)
  Pallas kernels  9.52 us (22%)
  between operations  0.75 us (2%)
    ppermute x15, starting transfers between devices, from_peer(): return lax.ppermute(value, 'dp', [(d, d ^ shift) for d in range(owners)])  20.5 us
    ppermute x15, waiting for transfers between devices, from_peer(): return lax.ppermute(value, 'dp', [(d, d ^ shift) for d in range(owners)])  11.2 us
    pallas_call x1, Pallas kernels, forward(): pl.pallas_call(functools.partial(forward_kernel, inner), out_shape=[block...  4.12 us
    pallas_call x1, Pallas kernels, inverse(): pl.pallas_call(inverse_kernel, out_shape=jax.ShapeDtypeStruct((rows, cols...  2.75 us
    pallas_call x2, Pallas kernels, finish(): pl.pallas_call(functools.partial(finish_kernel, half, count), out_shape=j...  1.48 us
    pallas_call x2, Pallas kernels, class_rows(): pl.pallas_call(functools.partial(class_kernel, inner), out_shape=pltpu.VM...  1.16 us
  transfers between devices with their start and end apart: 15, of which 5 were waited for; matrix products, arithmetic and copies ran while one was open for 1% of the time, Pallas kernels for 10%

profile of v6, /device:TPU:0, one launch (start us, length us, event | category | flops | bytes accessed | tf_op | source)
XLA Modules:
  0.0 42.3 jit_solution(3691747818008748727)
XLA Ops:
  0.6 0.0 copy-start
  0.7 4.1 %forward.1 = (f32[64,128]{1,0:T(8,128)S(1)}, f32[64,128]{1,0:T(8,128)S(1)}, f32[64,128]{1,0:T(8,128)S(1)}, f32[64,128]{1,0:T(8,128)S(1)}, f32[1032,128]{1,0:T(8,128)S(1)}, /*index=5*/f32[1032,128]{1,0:T(8,128)S(1)}) custom-call(s32[16,2,8,16]{3,2,1,0:T(8,128)} %bitcast.11, bf16[2,256,2048]{2,1,0:T(8,128)(2,1)} %bitcast.9, bf16[2,256,128]{2,1,0:T(8,128)(2,1)} %bitcast.15, ...), custom_call_target="tpu_custom_call" | custom-call | tf_op jit(solution)/shard_map/forward/pallas_call | solution.py:178
  4.8 3.0 %collective-permute-start = (f32[64,128]{1,0:T(8,128)S(1)}, f32[64,128]{1,0:T(8,128)S(1)}, u32[]{:S(2)}, u32[]{:S(2)}) collective-permute-start(f32[64,128]{1,0:T(8,128)S(1)} %get-tuple-element.12), channel_id=1, source_target_pairs={{0,2},{2,0},{4,6},{6,4},{8,10},{10,8},{12,14},{14,12},{16,18},{18,... | collective-permute-start | bytes 98312 | tf_op jit(solution)/shard_map/ppermute | solution.py:326
  7.8 1.5 %collective-permute-start.1 = (f32[64,128]{1,0:T(8,128)S(1)}, f32[64,128]{1,0:T(8,128)S(1)}, u32[]{:S(2)}, u32[]{:S(2)}) collective-permute-start(f32[64,128]{1,0:T(8,128)S(1)} %get-tuple-element.13), channel_id=1, source_target_pairs={{0,4},{2,6},{4,0},{6,2},{8,12},{10,14},{12,8},{14,10},{16,20},{18,... | collective-permute-start | bytes 98312 | tf_op jit(solution)/shard_map/ppermute | solution.py:326
  9.3 0.0 collective-permute-start.2
  9.4 0.1 constant_dynamic-slice_fusion.1
  9.5 0.1 copy.12.listed
  9.6 0.1 copy.11.listed
  9.7 0.0 collective-permute-done
  9.7 2.0 %collective-permute-done.1 = f32[64,128]{1,0:T(8,128)S(1)} collective-permute-done((f32[64,128]{1,0:T(8,128)S(1)}, f32[64,128]{1,0:T(8,128)S(1)}, u32[]{:S(2)}, u32[]{:S(2)}) %collective-permute-start.1) | collective-permute-done | bytes 32800 | tf_op jit(solution)/shard_map/ppermute | solution.py:326
  11.7 2.4 %collective-permute-done.2 = f32[64,128]{1,0:T(8,128)S(1)} collective-permute-done((f32[64,128]{1,0:T(8,128)S(1)}, f32[64,128]{1,0:T(8,128)S(1)}, u32[]{:S(2)}, u32[]{:S(2)}) %collective-permute-start.2) | collective-permute-done | bytes 32800 | tf_op jit(solution)/shard_map/ppermute | solution.py:326
  14.2 1.6 %collective-permute-start.11 = (f32[128,128]{1,0:T(8,128)S(1)}, f32[128,128]{1,0:T(8,128)S(1)}, u32[]{:S(2)}, u32[]{:S(2)}) collective-permute-start(f32[128,128]{1,0:T(8,128)S(1)} %pad_maximum_fusion.refs_3_), channel_id=1, source_target_pairs={{0,8},{2,10},{4,12},{6,14},{8,0},{10,2},{12,4},{14,6},{16,24},{18,... | collective-permute-start | bytes 196616 | tf_op jit(solution)/shard_map/ppermute | solution.py:326
  15.8 2.6 %collective-permute-start.10 = (f32[128,128]{1,0:T(8,128)S(1)}, f32[128,128]{1,0:T(8,128)S(1)}, u32[]{:S(2)}, u32[]{:S(2)}) collective-permute-start(f32[128,128]{1,0:T(8,128)S(1)} %pad_maximum_fusion.refs_3_), channel_id=1, source_target_pairs={{0,16},{2,18},{4,20},{6,22},{8,24},{10,26},{12,28},{14,30},{16,0},... | collective-permute-start | bytes 196616 | tf_op jit(solution)/shard_map/ppermute | solution.py:326
  18.4 0.2 collective-permute-start.9
  18.6 3.8 %collective-permute-done.10.refs_1_ = f32[128,128]{1,0:T(8,128)S(1)} collective-permute-done((f32[128,128]{1,0:T(8,128)S(1)}, f32[128,128]{1,0:T(8,128)S(1)}, u32[]{:S(2)}, u32[]{:S(2)}) %collective-permute-start.10) | collective-permute-done | bytes 65568 | tf_op jit(solution)/shard_map/ppermute | solution.py:326
  22.4 2.2 %collective-permute-done.9.refs_0_ = f32[128,128]{1,0:T(8,128)S(1)} collective-permute-done((f32[128,128]{1,0:T(8,128)S(1)}, f32[128,128]{1,0:T(8,128)S(1)}, u32[]{:S(2)}, u32[]{:S(2)}) %collective-permute-start.9) | collective-permute-done | bytes 65568 | tf_op jit(solution)/shard_map/ppermute | solution.py:326
  24.6 0.6 %class_rows.3.refs_3_ = f32[256,128]{1,0:T(8,128)S(1)} custom-call(s32[2,256]{1,0:T(2,128)S(1)} %copy.11.listed, bf16[4,128,128]{2,1,0:T(8,128)(2,1)S(1)} %copy-done, f32[128,128]{1,0:T(8,128)S(1)} %collective-permute-done.9.refs_0_, f32[128,128]{1,0:T(8,128)S(1)} %collective-permute-done.10.refs_1_, f32[128,128]{1,0:T(8,128)S(1)} %collective-permute-done.11.refs_2_, ...), custom_call_target="tpu_custom_call" | custom-call | tf_op jit(solution)/shard_map/class_rows/pallas_call | solution.py:269
  25.1 0.5 %collective-permute-start.14 = (f32[256,128]{1,0:T(8,128)S(1)}, f32[256,128]{1,0:T(8,128)S(1)}, u32[]{:S(2)}, u32[]{:S(2)}) collective-permute-start(f32[256,128]{1,0:T(8,128)S(1)} %class_rows.3.refs_3_), channel_id=1, source_target_pairs={{0,2},{2,0},{4,6},{6,4},{8,10},{10,8},{12,14},{14,12},{16,18},{18,... | collective-permute-start | bytes 393224 | tf_op jit(solution)/shard_map/ppermute | solution.py:326
  25.6 0.0 collective-permute-start.5
  25.7 1.4 %collective-permute-start.4 = (f32[128,128]{1,0:T(8,128)S(1)}, f32[128,128]{1,0:T(8,128)S(1)}, u32[]{:S(2)}, u32[]{:S(2)}) collective-permute-start(f32[128,128]{1,0:T(8,128)S(1)} %pad_maximum_fusion.1.refs_3_), channel_id=1, source_target_pairs={{0,16},{2,18},{4,20},{6,22},{8,24},{10,26},{12,28},{14,30},{16,0},... | collective-permute-start | bytes 196616 | tf_op jit(solution)/shard_map/ppermute | solution.py:326
  27.0 3.0 %collective-permute-start.3 = (f32[128,128]{1,0:T(8,128)S(1)}, f32[128,128]{1,0:T(8,128)S(1)}, u32[]{:S(2)}, u32[]{:S(2)}) collective-permute-start(f32[128,128]{1,0:T(8,128)S(1)} %pad_maximum_fusion.1.refs_3_), channel_id=1, source_target_pairs={{0,24},{2,26},{4,28},{6,30},{8,16},{10,18},{12,20},{14,22},{16,8},... | collective-permute-start | bytes 196616 | tf_op jit(solution)/shard_map/ppermute | solution.py:326
  30.0 0.5 %collective-permute-start.13 = (f32[256,128]{1,0:T(8,128)S(1)}, f32[256,128]{1,0:T(8,128)S(1)}, u32[]{:S(2)}, u32[]{:S(2)}) collective-permute-start(f32[256,128]{1,0:T(8,128)S(1)} %class_rows.3.refs_3_), channel_id=1, source_target_pairs={{0,4},{2,6},{4,0},{6,2},{8,12},{10,14},{12,8},{14,10},{16,20},{18,... | collective-permute-start | bytes 393224 | tf_op jit(solution)/shard_map/ppermute | solution.py:326
  30.6 0.0 collective-permute-done.5.refs_2_
  30.6 2.5 %collective-permute-start.12 = (f32[256,128]{1,0:T(8,128)S(1)}, f32[256,128]{1,0:T(8,128)S(1)}, u32[]{:S(2)}, u32[]{:S(2)}) collective-permute-start(f32[256,128]{1,0:T(8,128)S(1)} %class_rows.3.refs_3_), channel_id=1, source_target_pairs={{0,6},{2,4},{4,2},{6,0},{8,14},{10,12},{12,10},{14,8},{16,22},{18,... | collective-permute-start | bytes 393224 | tf_op jit(solution)/shard_map/ppermute | solution.py:326
  33.1 0.6 %class_rows.2.refs_3_ = f32[256,128]{1,0:T(8,128)S(1)} custom-call(s32[2,256]{1,0:T(2,128)S(1)} %copy.12.listed, bf16[4,128,128]{2,1,0:T(8,128)(2,1)S(1)} %copy-done, f32[128,128]{1,0:T(8,128)S(1)} %collective-permute-done.3.refs_0_, f32[128,128]{1,0:T(8,128)S(1)} %collective-permute-done.4.refs_1_, f32[128,128]{1,0:T(8,128)S(1)} %collective-permute-done.5.refs_2_, ...), custom_call_target="tpu_custom_call" | custom-call | tf_op jit(solution)/shard_map/class_rows/pallas_call | solution.py:269
  33.7 1.5 %collective-permute-start.8 = (f32[256,128]{1,0:T(8,128)S(1)}, f32[256,128]{1,0:T(8,128)S(1)}, u32[]{:S(2)}, u32[]{:S(2)}) collective-permute-start(f32[256,128]{1,0:T(8,128)S(1)} %class_rows.2.refs_3_), channel_id=1, source_target_pairs={{0,2},{2,0},{4,6},{6,4},{8,10},{10,8},{12,14},{14,12},{16,18},{18,... | collective-permute-start | bytes 393224 | tf_op jit(solution)/shard_map/ppermute | solution.py:326
  35.2 0.5 %collective-permute-start.7 = (f32[256,128]{1,0:T(8,128)S(1)}, f32[256,128]{1,0:T(8,128)S(1)}, u32[]{:S(2)}, u32[]{:S(2)}) collective-permute-start(f32[256,128]{1,0:T(8,128)S(1)} %class_rows.2.refs_3_), channel_id=1, source_target_pairs={{0,4},{2,6},{4,0},{6,2},{8,12},{10,14},{12,8},{14,10},{16,20},{18,... | collective-permute-start | bytes 393224 | tf_op jit(solution)/shard_map/ppermute | solution.py:326
  35.7 1.5 %collective-permute-start.6 = (f32[256,128]{1,0:T(8,128)S(1)}, f32[256,128]{1,0:T(8,128)S(1)}, u32[]{:S(2)}, u32[]{:S(2)}) collective-permute-start(f32[256,128]{1,0:T(8,128)S(1)} %class_rows.2.refs_3_), channel_id=1, source_target_pairs={{0,6},{2,4},{4,2},{6,0},{8,14},{10,12},{12,10},{14,8},{16,22},{18,... | collective-permute-start | bytes 393224 | tf_op jit(solution)/shard_map/ppermute | solution.py:326
  37.2 2.8 %inverse.1 = f32[2048,128]{1,0:T(8,128)} custom-call(bf16[4,128,128]{2,1,0:T(8,128)(2,1)S(1)} %copy-done, f32[1032,128]{1,0:T(8,128)S(1)} %get-tuple-element.18.refs_0_, f32[1032,128]{1,0:T(8,128)S(1)} %get-tuple-element.19.refs_1_), custom_call_target="tpu_custom_call" | custom-call | tf_op jit(solution)/shard_map/inverse/pallas_call | solution.py:230
  40.0 0.7 %finish.2.refs_4_ = bf16[4,2,256,128]{3,2,1,0:T(8,128)(2,1)} custom-call(f32[256,128]{1,0:T(8,128)S(1)} %collective-permute-done.12.refs_0_, f32[256,128]{1,0:T(8,128)S(1)} %collective-permute-done.13.refs_1_, f32[256,128]{1,0:T(8,128)S(1)} %collective-permute-done.14.refs_2_, f32[256,128]{1,0:T(8,128)S(1)} %class_rows.3.refs_3_), custom_call_target="tpu_custom_call" | custom-call | tf_op jit(solution)/shard_map/finish/pallas_call | solution.py:298
  40.8 0.8 %collective-permute-done.6.refs_0_ = f32[256,128]{1,0:T(8,128)S(1)} collective-permute-done((f32[256,128]{1,0:T(8,128)S(1)}, f32[256,128]{1,0:T(8,128)S(1)}, u32[]{:S(2)}, u32[]{:S(2)}) %collective-permute-start.6) | collective-permute-done | bytes 131104 | tf_op jit(solution)/shard_map/ppermute | solution.py:326
  41.6 0.7 %finish.3 = bf16[4,2,256,128]{3,2,1,0:T(8,128)(2,1)} custom-call(f32[256,128]{1,0:T(8,128)S(1)} %collective-permute-done.6.refs_0_, f32[256,128]{1,0:T(8,128)S(1)} %collective-permute-done.7.refs_1_, f32[256,128]{1,0:T(8,128)S(1)} %collective-permute-done.8.refs_2_, f32[256,128]{1,0:T(8,128)S(1)} %class_rows.2.refs_3_, ...), custom_call_target="tpu_custom_call", output_to_operand_aliasing={{}: (4, {})} | custom-call | tf_op jit(solution)/shard_map/finish/pallas_call | solution.py:298
  (17 shorter events, 0.1 us)
Async XLA Ops:
  0.6 8.7 %copy-start.1 = (s32[16,2,16,8]{2,3,1,0:T(8,128)S(1)}, s32[16,2,16,8]{2,3,1,0:T(8,128)}, u32[]{:S(2)}) copy-start(s32[16,2,16,8]{2,3,1,0:T(8,128)} %param.8) | copy-start | bytes 49156
  0.6 23.9 %copy-start = (bf16[4,128,128]{2,1,0:T(8,128)(2,1)S(1)}, bf16[4,128,128]{2,1,0:T(8,128)(2,1)}, u32[]{:S(2)}) copy-start(bf16[4,128,128]{2,1,0:T(8,128)(2,1)} %constant.24.clone.dct_hbm.dct) | copy-start | bytes 393220
  4.8 4.9 %collective-permute-start = (f32[64,128]{1,0:T(8,128)S(1)}, f32[64,128]{1,0:T(8,128)S(1)}, u32[]{:S(2)}, u32[]{:S(2)}) collective-permute-start(f32[64,128]{1,0:T(8,128)S(1)} %get-tuple-element.12), channel_id=1, source_target_pairs={{0,2},{2,0},{4,6},{6,4},{8,10},{10,8},{12,14},{14,12},{16,18},{18,... | collective-permute-start | bytes 98312 | tf_op jit(solution)/shard_map/ppermute | solution.py:326
  7.8 3.9 %collective-permute-start.1 = (f32[64,128]{1,0:T(8,128)S(1)}, f32[64,128]{1,0:T(8,128)S(1)}, u32[]{:S(2)}, u32[]{:S(2)}) collective-permute-start(f32[64,128]{1,0:T(8,128)S(1)} %get-tuple-element.13), channel_id=1, source_target_pairs={{0,4},{2,6},{4,0},{6,2},{8,12},{10,14},{12,8},{14,10},{16,20},{18,... | collective-permute-start | bytes 98312 | tf_op jit(solution)/shard_map/ppermute | solution.py:326
  9.3 4.8 %collective-permute-start.2 = (f32[64,128]{1,0:T(8,128)S(1)}, f32[64,128]{1,0:T(8,128)S(1)}, u32[]{:S(2)}, u32[]{:S(2)}) collective-permute-start(f32[64,128]{1,0:T(8,128)S(1)} %get-tuple-element.14), channel_id=1, source_target_pairs={{0,6},{2,4},{4,2},{6,0},{8,14},{10,12},{12,10},{14,8},{16,22},{18,... | collective-permute-start | bytes 98312 | tf_op jit(solution)/shard_map/ppermute | solution.py:326
  14.2 4.5 %collective-permute-start.11 = (f32[128,128]{1,0:T(8,128)S(1)}, f32[128,128]{1,0:T(8,128)S(1)}, u32[]{:S(2)}, u32[]{:S(2)}) collective-permute-start(f32[128,128]{1,0:T(8,128)S(1)} %pad_maximum_fusion.refs_3_), channel_id=1, source_target_pairs={{0,8},{2,10},{4,12},{6,14},{8,0},{10,2},{12,4},{14,6},{16,24},{18,... | collective-permute-start | bytes 196616 | tf_op jit(solution)/shard_map/ppermute | solution.py:326
  15.8 6.6 %collective-permute-start.10 = (f32[128,128]{1,0:T(8,128)S(1)}, f32[128,128]{1,0:T(8,128)S(1)}, u32[]{:S(2)}, u32[]{:S(2)}) collective-permute-start(f32[128,128]{1,0:T(8,128)S(1)} %pad_maximum_fusion.refs_3_), channel_id=1, source_target_pairs={{0,16},{2,18},{4,20},{6,22},{8,24},{10,26},{12,28},{14,30},{16,0},... | collective-permute-start | bytes 196616 | tf_op jit(solution)/shard_map/ppermute | solution.py:326
  18.4 6.2 %collective-permute-start.9 = (f32[128,128]{1,0:T(8,128)S(1)}, f32[128,128]{1,0:T(8,128)S(1)}, u32[]{:S(2)}, u32[]{:S(2)}) collective-permute-start(f32[128,128]{1,0:T(8,128)S(1)} %pad_maximum_fusion.refs_3_), channel_id=1, source_target_pairs={{0,24},{2,26},{4,28},{6,30},{8,16},{10,18},{12,20},{14,22},{16,8},... | collective-permute-start | bytes 196616 | tf_op jit(solution)/shard_map/ppermute | solution.py:326
  25.1 10.6 %collective-permute-start.14 = (f32[256,128]{1,0:T(8,128)S(1)}, f32[256,128]{1,0:T(8,128)S(1)}, u32[]{:S(2)}, u32[]{:S(2)}) collective-permute-start(f32[256,128]{1,0:T(8,128)S(1)} %class_rows.3.refs_3_), channel_id=1, source_target_pairs={{0,2},{2,0},{4,6},{6,4},{8,10},{10,8},{12,14},{14,12},{16,18},{18,... | collective-permute-start | bytes 393224 | tf_op jit(solution)/shard_map/ppermute | solution.py:326
  25.6 4.9 %collective-permute-start.5 = (f32[128,128]{1,0:T(8,128)S(1)}, f32[128,128]{1,0:T(8,128)S(1)}, u32[]{:S(2)}, u32[]{:S(2)}) collective-permute-start(f32[128,128]{1,0:T(8,128)S(1)} %pad_maximum_fusion.1.refs_3_), channel_id=1, source_target_pairs={{0,8},{2,10},{4,12},{6,14},{8,0},{10,2},{12,4},{14,6},{16,24},{18,... | collective-permute-start | bytes 196616 | tf_op jit(solution)/shard_map/ppermute | solution.py:326
  25.7 7.4 %collective-permute-start.4 = (f32[128,128]{1,0:T(8,128)S(1)}, f32[128,128]{1,0:T(8,128)S(1)}, u32[]{:S(2)}, u32[]{:S(2)}) collective-permute-start(f32[128,128]{1,0:T(8,128)S(1)} %pad_maximum_fusion.1.refs_3_), channel_id=1, source_target_pairs={{0,16},{2,18},{4,20},{6,22},{8,24},{10,26},{12,28},{14,30},{16,0},... | collective-permute-start | bytes 196616 | tf_op jit(solution)/shard_map/ppermute | solution.py:326
  27.0 6.1 %collective-permute-start.3 = (f32[128,128]{1,0:T(8,128)S(1)}, f32[128,128]{1,0:T(8,128)S(1)}, u32[]{:S(2)}, u32[]{:S(2)}) collective-permute-start(f32[128,128]{1,0:T(8,128)S(1)} %pad_maximum_fusion.1.refs_3_), channel_id=1, source_target_pairs={{0,24},{2,26},{4,28},{6,30},{8,16},{10,18},{12,20},{14,22},{16,8},... | collective-permute-start | bytes 196616 | tf_op jit(solution)/shard_map/ppermute | solution.py:326
  30.0 10.0 %collective-permute-start.13 = (f32[256,128]{1,0:T(8,128)S(1)}, f32[256,128]{1,0:T(8,128)S(1)}, u32[]{:S(2)}, u32[]{:S(2)}) collective-permute-start(f32[256,128]{1,0:T(8,128)S(1)} %class_rows.3.refs_3_), channel_id=1, source_target_pairs={{0,4},{2,6},{4,0},{6,2},{8,12},{10,14},{12,8},{14,10},{16,20},{18,... | collective-permute-start | bytes 393224 | tf_op jit(solution)/shard_map/ppermute | solution.py:326
  30.6 9.5 %collective-permute-start.12 = (f32[256,128]{1,0:T(8,128)S(1)}, f32[256,128]{1,0:T(8,128)S(1)}, u32[]{:S(2)}, u32[]{:S(2)}) collective-permute-start(f32[256,128]{1,0:T(8,128)S(1)} %class_rows.3.refs_3_), channel_id=1, source_target_pairs={{0,6},{2,4},{4,2},{6,0},{8,14},{10,12},{12,10},{14,8},{16,22},{18,... | collective-permute-start | bytes 393224 | tf_op jit(solution)/shard_map/ppermute | solution.py:326
  33.7 7.1 %collective-permute-start.8 = (f32[256,128]{1,0:T(8,128)S(1)}, f32[256,128]{1,0:T(8,128)S(1)}, u32[]{:S(2)}, u32[]{:S(2)}) collective-permute-start(f32[256,128]{1,0:T(8,128)S(1)} %class_rows.2.refs_3_), channel_id=1, source_target_pairs={{0,2},{2,0},{4,6},{6,4},{8,10},{10,8},{12,14},{14,12},{16,18},{18,... | collective-permute-start | bytes 393224 | tf_op jit(solution)/shard_map/ppermute | solution.py:326
  35.2 5.6 %collective-permute-start.7 = (f32[256,128]{1,0:T(8,128)S(1)}, f32[256,128]{1,0:T(8,128)S(1)}, u32[]{:S(2)}, u32[]{:S(2)}) collective-permute-start(f32[256,128]{1,0:T(8,128)S(1)} %class_rows.2.refs_3_), channel_id=1, source_target_pairs={{0,4},{2,6},{4,0},{6,2},{8,12},{10,14},{12,8},{14,10},{16,20},{18,... | collective-permute-start | bytes 393224 | tf_op jit(solution)/shard_map/ppermute | solution.py:326
  35.7 5.9 %collective-permute-start.6 = (f32[256,128]{1,0:T(8,128)S(1)}, f32[256,128]{1,0:T(8,128)S(1)}, u32[]{:S(2)}, u32[]{:S(2)}) collective-permute-start(f32[256,128]{1,0:T(8,128)S(1)} %class_rows.2.refs_3_), channel_id=1, source_target_pairs={{0,6},{2,4},{4,2},{6,0},{8,14},{10,12},{12,10},{14,8},{16,22},{18,... | collective-permute-start | bytes 393224 | tf_op jit(solution)/shard_map/ppermute | solution.py:326
